TPU v7x, 32 devices: a whole 2x2x4 slice. The times are simulated.
32 devices in a mesh: seq: 8 (over z, x), tp: 4 (over y, core).
Axes of the slice: x: 2, y: 2, z: 4, core: 2. Of those that a mesh axis runs over, the one named last changes fastest.
Arguments:
- query: bfloat16 [4096, 2048], P('seq', 'tp'), may hold values from -6 to 6
- keys: bfloat16 [4096, 2048], P('seq', 'tp'), may hold values from -6 to 6
- values: bfloat16 [4096, 2048], P('seq', 'tp'), may hold values from -7 to 7
- beta: float32 [16], P('tp'), may hold values from -2 to 2
- out_weight: bfloat16 [2048, 2048], P('tp'), may hold values from -0.125 to 0.125
- cotangent: bfloat16 [4096, 2048], P(('seq', 'tp')), may hold values from -6 to 6
Outputs:
- output: bfloat16 [4096, 2048], P(('seq', 'tp'))
- grad_query: bfloat16 [4096, 2048], P('seq', 'tp')
- grad_keys: bfloat16 [4096, 2048], P('seq', 'tp')
- grad_values: bfloat16 [4096, 2048], P('seq', 'tp')
All inputs are finite; a program needn't handle non-finite values.
Results may differ from a plain program's by a relative error of at most 0.0055.
The roundings to bfloat16 on the way count: a program that leaves them out, or rounds other values in their place, can miss the bound.
Values may be sent and summed in bfloat16 or wider, within the bound.
No kernel may reach another device: no remote copies, remote signals or barrier semaphores. Data moves between devices by JAX's collectives and lax.ppermute only.
A program may use at most 128 MiB of HBM per device.

v0:
```python
import jax
import jax.numpy as jnp
from jax import lax
from jax.sharding import PartitionSpec as P

HD = 128


precise = lax.Precision.HIGH


def entering(shard, axis, join, neutral, backward):
    count = lax.axis_size(axis)
    place = lax.axis_index(axis)
    ahead = count - 1 - place if backward else place
    gathered = jax.tree.map(
        lambda a, kind: lax.all_gather(a.astype(kind), axis), shard, (jnp.bfloat16, jnp.bfloat16)
    )
    state = jax.tree.map(lambda a, e: jnp.zeros_like(a) + jnp.asarray(e, a.dtype), shard, neutral)

    def one(hop, state):
        source = count - 1 - hop if backward else hop
        return join(
            state,
            jax.tree.map(
                lambda a, own: lax.dynamic_index_in_dim(a, source, 0, False).astype(own.dtype),
                gathered,
                shard,
            ),
        )

    return lax.fori_loop(0, ahead, one, state)


def plus_one(inputs):
    return jnp.where(inputs > 0, inputs + 1.0, jnp.exp(jnp.minimum(inputs, 0.0)))


def slope_of(inputs):
    return jnp.where(inputs > 0, jnp.ones_like(inputs), jnp.exp(jnp.minimum(inputs, 0.0)))


def add_pair(earlier, later):
    return (earlier[0] + later[0], earlier[1] + later[1])


def local(query, keys, values, beta, out_weight, cotangent):
    length = query.shape[0]
    width = query.shape[1]
    local_heads = width // HD
    scale_factor = HD ** (-0.5)

    def shaped(tensor):
        return tensor.reshape(length, local_heads, HD)

    query_h, keys_h, values_h = (shaped(query), shaped(keys), shaped(values))
    gate_mix = jax.nn.sigmoid(beta)[None, :, None]
    query_f = query_h.astype(jnp.float32)
    keys_f = keys_h.astype(jnp.float32)
    query_feat = plus_one(query_f)
    key_feat = plus_one(keys_f)
    own_memory = jnp.einsum(
        "lhc,lhd->hcd", key_feat, values_h, precision=precise, preferred_element_type=jnp.float32
    )
    own_sum = jnp.sum(key_feat, 0)
    memory, memory_sum = entering(
        (own_memory, own_sum),
        "seq",
        add_pair,
        (jnp.zeros_like(own_memory), jnp.zeros_like(own_sum)),
        False,
    )
    causal = jnp.arange(length)[:, None] >= jnp.arange(length)[None, :]
    scores = (
        jnp.einsum("lhc,mhc->hlm", query_h, keys_h, preferred_element_type=jnp.float32)
        * scale_factor
    )
    scores = jnp.where(causal[None], scores, -jnp.inf)
    top_score = jnp.max(scores, -1, keepdims=True)
    expo = jnp.exp(scores - top_score)
    probs = expo / jnp.sum(expo, -1, keepdims=True)
    probs_b = probs.astype(jnp.bfloat16)
    local_out = jnp.einsum("hlm,mhc->lhc", probs_b, values_h, preferred_element_type=jnp.float32)
    numer = jnp.einsum(
        "lhc,hcd->lhd", query_feat, memory, precision=precise, preferred_element_type=jnp.float32
    )
    denom = (
        jnp.einsum(
            "lhc,hc->lh",
            query_feat,
            memory_sum,
            precision=precise,
            preferred_element_type=jnp.float32,
        )
        + 1.0
    )
    mem_out = numer / denom[..., None]
    mixed = (
        (gate_mix * mem_out + (1.0 - gate_mix) * local_out)
        .astype(jnp.bfloat16)
        .reshape(length, width)
    )
    output = lax.psum_scatter(
        jnp.dot(mixed, out_weight, preferred_element_type=jnp.float32),
        "tp",
        scatter_dimension=0,
        tiled=True,
    ).astype(jnp.bfloat16)
    grad_mixed = lax.dot_general(
        lax.all_gather(cotangent, "tp", axis=0, tiled=True),
        out_weight,
        (((1,), (1,)), ((), ())),
        preferred_element_type=jnp.float32,
    ).astype(jnp.bfloat16)
    grad_f = shaped(grad_mixed).astype(jnp.float32)
    grad_mem = gate_mix * grad_f
    grad_numer = grad_mem / denom[..., None]
    grad_denom = -jnp.sum(grad_mem * mem_out, -1) / denom
    memory_grad = jnp.einsum(
        "lhc,lhd->hcd",
        query_feat,
        grad_numer,
        precision=precise,
        preferred_element_type=jnp.float32,
    )
    sum_grad = jnp.einsum(
        "lh,lhc->hc", grad_denom, query_feat, precision=precise, preferred_element_type=jnp.float32
    )
    later_memory, later_sum = entering(
        (memory_grad, sum_grad),
        "seq",
        add_pair,
        (jnp.zeros_like(memory_grad), jnp.zeros_like(sum_grad)),
        True,
    )
    grad_local = ((1.0 - gate_mix) * grad_f).astype(jnp.bfloat16)
    grad_probs = jnp.einsum(
        "lhc,mhc->hlm", grad_local, values_h, preferred_element_type=jnp.float32
    )
    delta = jnp.sum(probs * grad_probs, -1, keepdims=True)
    grad_scores = (probs * (grad_probs - delta) * scale_factor).astype(jnp.bfloat16)
    query_local = jnp.einsum(
        "hlm,mhc->lhc", grad_scores, keys_h, preferred_element_type=jnp.float32
    )
    keys_local = jnp.einsum(
        "hlm,lhc->mhc", grad_scores, query_h, preferred_element_type=jnp.float32
    )
    values_local = jnp.einsum(
        "hlm,lhc->mhc", probs_b, grad_local, preferred_element_type=jnp.float32
    )
    grad_qfeat = (
        jnp.einsum(
            "lhd,hcd->lhc",
            grad_numer,
            memory,
            precision=precise,
            preferred_element_type=jnp.float32,
        )
        + grad_denom[..., None] * memory_sum[None]
    )
    grad_kfeat = (
        jnp.einsum(
            "lhd,hcd->lhc",
            values_h,
            later_memory,
            precision=precise,
            preferred_element_type=jnp.float32,
        )
        + later_sum[None]
    )
    values_mem = jnp.einsum(
        "lhc,hcd->lhd",
        key_feat,
        later_memory,
        precision=precise,
        preferred_element_type=jnp.float32,
    )
    grad_query = (
        (query_local + grad_qfeat * slope_of(query_f)).astype(jnp.bfloat16).reshape(length, width)
    )
    grad_keys = (
        (keys_local + grad_kfeat * slope_of(keys_f)).astype(jnp.bfloat16).reshape(length, width)
    )
    grad_values = (values_local + values_mem).astype(jnp.bfloat16).reshape(length, width)
    return (output, grad_query, grad_keys, grad_values)


def solution(mesh):
    in_specs = (
        P("seq", "tp"),
        P("seq", "tp"),
        P("seq", "tp"),
        P("tp"),
        P("tp", None),
        P(("seq", "tp"), None),
    )
    out_specs = (P(("seq", "tp"), None), P("seq", "tp"), P("seq", "tp"), P("seq", "tp"))
    return jax.shard_map(local, mesh=mesh, in_specs=in_specs, out_specs=out_specs, check_vma=False)
```

profile of v0, /device:TPU:0, one launch (start us, length us, event | category | flops | bytes accessed | tf_op | source)
XLA Modules:
  0.0 177.1 jit_solution(11170226067630797144)
XLA Ops:
  7.2 1.4 copy.32
  8.7 2.3 %convolution_convert_fusion.2 = bf16[4,128,128]{2,1,0:T(8,128)(2,1)} fusion(bf16[512,4,128]{0,2,1:T(8,128)(2,1)S(1)} %bitcast.123, bf16[512,512]{1,0:T(8,128)(2,1)} %param.12), kind=kOutput, calls=%fused_computation.55 | convolution fusion | flops 202702848 | bytes 1179648 | tf_op jit(solution)/shard_map/lhc,lhd->hcd/dot_general | solution.py:62
  11.8 2.0 %copy.34 = bf16[512,512]{0,1:T(8,128)(2,1)} copy(bf16[512,512]{1,0:T(8,128)(2,1)} %param.10) | data formatting | bytes 1048576 | tf_op args[0]
  14.1 22.3 %all_gather.27 = bf16[8,4,128]{2,1,0:T(4,128)(2,1)S(1)} all-gather(bf16[1,4,128]{2,1,0:T(4,128)(2,1)S(1)} %bitcast.147), channel_id=1, replica_groups=mesh['seq'=8,'tp'=4] {'seq'}, dimensions={0}, use_global_device_ids=true | all-gather | bytes 9216 | tf_op jit(solution)/shard_map/all_gather | solution.py:17
  36.4 17.7 %all-gather.10.cloned.1.call-done = bf16[32,128,128]{2,1,0:T(8,128)(2,1)} async-done(((bf16[4,128,128]{2,1,0:T(8,128)(2,1)}), bf16[32,128,128]{2,1,0:T(8,128)(2,1)}) %all-gather.10.cloned.1.call-update) | async-done | bytes 1048592 | tf_op jit(solution)/shard_map/all_gather | solution.py:17
  54.2 1.7 fusion.57
  55.9 21.1 %all-gather.8.cloned.1.call-done = bf16[512,2048]{1,0:T(8,128)(2,1)} async-done(((bf16[128,2048]{1,0:T(8,128)(2,1)}), bf16[512,2048]{1,0:T(8,128)(2,1)}) %all-gather.8.cloned.1.call-update) | async-done | bytes 2097168 | tf_op jit(solution)/shard_map/all_gather | solution.py:110
  77.0 2.9 %convolution_convert_fusion = bf16[512,512]{0,1:T(8,128)(2,1)S(1)} fusion(bf16[512,2048]{1,0:T(8,128)(2,1)} %all-gather.8.cloned.1.call-done, bf16[512,2048]{1,0:T(8,128)(2,1)S(1)} %copy-done), kind=kOutput, calls=%fused_computation.48 | convolution fusion | flops 1074003968 | bytes 4718592 | tf_op jit(solution)/shard_map/dot_general | solution.py:109
  80.7 1.6 convolution_convert_fusion.1
  83.3 4.6 %fusion.111 = (f32[4,512]{1,0:T(4,128)S(1)}, f32[4,512,512]{1,2,0:T(8,128)}) fusion(pred[512,512]{0,1:T(8,128)(4,1)} %iota_compare_fusion, bf16[512,4,128]{0,2,1:T(8,128)(2,1)S(1)} %bitcast.131, bf16[512,4,128]{0,2,1:T(8,128)(2,1)S(1)} %bitcast.124), kind=kOutput, calls=%fused_computation.125 | convolution fusion | flops 272630272 | bytes 5513216 | tf_op jit(solution)/shard_map/sub | solution.py:80
  87.9 2.1 %fusion.38 = (f32[512,4]{0,1:T(4,128)S(1)}, f32[512,4,128]{0,2,1:T(8,128)S(1)}) fusion(f32[4]{0:T(128)S(1)} %get-tuple-element.156, bf16[512,512]{0,1:T(8,128)(2,1)} %copy-done.4, f32[512,4]{0,1:T(4,128)S(1)} %fusion.91, f32[4,128,128]{2,1,0:T(8,128)S(1)} %get-tuple-element.119, bf16[512,4,128]{0,2,1:T(8,128)(2,1)S(1)} %bitcast.132), kind=kOutput, calls=%fused_computation.56 | convolution fusion | flops 203945984 | bytes 2375696 | tf_op jit(solution)/shard_map/lhc,hcd->lhd/dot_general | solution.py:84
  91.0 3.2 %fusion.112 = f32[512,2048]{1,0:T(8,128)} fusion(bf16[512,512]{0,1:T(8,128)(2,1)S(1)} %bitcast.142, bf16[512,2048]{1,0:T(8,128)(2,1)S(1)} %copy-done), kind=kOutput, calls=%fused_computation.126 | convolution fusion | flops 1073741824 | bytes 6815744 | tf_op jit(solution)/shard_map/dot_general | solution.py:104
  94.3 3.9 %fusion.64 = f32[4,512,512]{1,2,0:T(8,128)} fusion(bf16[512,4,128]{0,2,1:T(8,128)(2,1)} %bitcast.139, f32[4]{0:T(128)S(1)} %get-tuple-element.155, bf16[512,512]{1,0:T(8,128)(2,1)} %param.12), kind=kOutput, calls=%fused_computation.75 | convolution fusion | flops 269221888 | bytes 5242896 | tf_op jit(solution)/shard_map/lhc,mhc->hlm/dot_general | solution.py:137
  98.2 8.9 %fusion.17 = f32[512,4,128]{0,2,1:T(8,128)} fusion(bf16[512,4,128]{0,2,1:T(8,128)(2,1)S(1)} %bitcast.125, f32[4,512,512]{1,2,0:T(8,128)} %fusion.64, f32[4,512,512]{1,2,0:T(8,128)} %get-tuple-element.158, f32[4,512]{1,0:T(4,128)S(1)} %get-tuple-element.157), kind=kOutput, calls=%fused_computation.29 | convolution fusion | flops 275778048 | bytes 9969664 | tf_op jit(solution)/shard_map/hlm,mhc->lhc/dot_general | solution.py:142
  107.1 3.2 %fusion.34 = bf16[512,4,128]{0,2,1:T(8,128)(2,1)} fusion(f32[512,4,128]{0,2,1:T(8,128)} %fusion.17, f32[4,128,128]{2,1,0:T(8,128)S(1)} %get-tuple-element.119, bf16[512,4,128]{0,2,1:T(8,128)(2,1)S(1)} %bitcast.133, bf16[512,4,128]{0,2,1:T(8,128)(2,1)} %bitcast.140, f32[4,128]{1,0:T(4,128)S(1)} %get-tuple-element.120, f32[512,4]{0,1:T(4,128)S(1)} %negate_divide_fusion, ...), kind=kOutput, calls=%fused_computation.50 | convolution fusion | flops 204472320 | bytes 2902032 | tf_op jit(solution)/shard_map/lhd,hcd->lhc/dot_general | solution.py:152
  110.3 2.0 %copy.51 = bf16[512,512]{1,0:T(8,128)(2,1)} copy(bf16[512,512]{0,1:T(8,128)(2,1)} %bitcast.136) | data formatting | bytes 1048576
  113.0 20.5 %all-gather.3 = bf16[8,4,128]{2,1,0:T(4,128)(2,1)S(1)} all-gather(bf16[1,4,128]{2,1,0:T(4,128)(2,1)S(1)} %convert_bitcast_fusion), channel_id=4, replica_groups=mesh['seq'=8,'tp'=4] {'seq'}, dimensions={0}, use_global_device_ids=true | all-gather | bytes 9216 | tf_op jit(solution)/shard_map/all_gather | solution.py:17
  133.5 8.7 %fusion.20 = f32[512,4,128]{0,2,1:T(8,128)} fusion(bf16[512,4,128]{0,2,1:T(8,128)(2,1)S(1)} %bitcast.135, f32[4,512,512]{1,2,0:T(8,128)} %fusion.64, f32[4,512,512]{1,2,0:T(8,128)} %get-tuple-element.158, f32[4,512]{1,0:T(4,128)S(1)} %get-tuple-element.157), kind=kOutput, calls=%fused_computation.30 | convolution fusion | flops 275778048 | bytes 9969664 | tf_op jit(solution)/shard_map/hlm,lhc->mhc/dot_general | solution.py:145
  142.2 4.6 %fusion.49 = f32[4,128,512]{2,1,0:T(8,128)} fusion(bf16[512,4,128]{0,2,1:T(8,128)(2,1)} %bitcast.141, f32[4]{0:T(128)S(1)} %get-tuple-element.155, f32[4,512,512]{1,2,0:T(8,128)} %get-tuple-element.158, f32[4,512]{1,0:T(4,128)S(1)} %get-tuple-element.157), kind=kOutput, calls=%fused_computation.67 | convolution fusion | flops 271319040 | bytes 5775376 | tf_op jit(solution)/shard_map/hlm,lhc->mhc/dot_general | solution.py:148
  146.8 7.1 %while.27 = (s32[]{:T(128)}, f32[4,128,128]{2,1,0:T(8,128)S(1)}, f32[4,128]{1,0:T(4,128)S(1)}, s32[]{:T(128)}, bf16[8,4,128,128]{3,2,1,0:T(8,128)(2,1)}, /*index...) while((s32[]{:T(128)}, f32[4,128,128]{2,1,0:T(8,128)S(1)}, ...), condition=%wide.region_9.10_spmd, body=%wide.region_8.9_spmd.sunk | while | flops 132102 | bytes 660643 | solution.py:32
  153.9 2.1 %fusion.35 = bf16[512,4,128]{0,2,1:T(8,128)(2,1)S(1)} fusion(f32[512,4,128]{0,2,1:T(8,128)} %fusion.20, f32[4,128,128]{2,1,0:T(8,128)S(1)} %get-tuple-element.121, bf16[512,4,128]{0,2,1:T(8,128)(2,1)S(1)} %bitcast.126, f32[4,128]{1,0:T(4,128)S(1)} %get-tuple-element.122, bf16[512,512]{1,0:T(8,128)(2,1)} %param.12), kind=kOutput, calls=%fused_computation.51 | convolution fusion | flops 203423744 | bytes 2885632 | tf_op jit(solution)/shard_map/lhd,hcd->lhc/dot_general | solution.py:162
  157.0 2.0 %fusion.33 = bf16[4,128,512]{2,1,0:T(8,128)(2,1)S(1)} fusion(f32[4,128,512]{2,1,0:T(8,128)} %fusion.49, f32[4,128,128]{2,1,0:T(8,128)S(1)} %get-tuple-element.121, bf16[512,4,128]{0,2,1:T(8,128)(2,1)S(1)} %bitcast.127), kind=kOutput, calls=%fused_computation.49 | convolution fusion | flops 203161600 | bytes 2359296 | tf_op jit(solution)/shard_map/lhc,hcd->lhd/dot_general | solution.py:171
  160.0 8.4 %reduce-scatter.2.cloned.1.call-done = f32[128,2048]{1,0:T(8,128)} async-done(((f32[512,2048]{1,0:T(8,128)}), f32[128,2048]{1,0:T(8,128)}) %reduce-scatter.2.cloned.1.call-update) | async-done | bytes 1048592 | tf_op jit(solution)/shard_map/reduce_scatter | solution.py:103
  168.5 2.1 %convert_element_type.105 = bf16[128,2048]{1,0:T(8,128)(2,1)} convert(f32[128,2048]{1,0:T(8,128)} %reduce-scatter.2.cloned.1.call-done) | non-fusion elementwise | flops 262144 | bytes 1572864 | tf_op jit(solution)/shard_map/convert_element_type | solution.py:108
  (52 shorter events, 13.7 us)
Async XLA Ops:
  7.2 69.8 %copy-start = (bf16[512,2048]{1,0:T(8,128)(2,1)S(1)}, bf16[512,2048]{1,0:T(8,128)(2,1)}, u32[]{:S(2)}) copy-start(bf16[512,2048]{1,0:T(8,128)(2,1)} %param.14) | copy-start | bytes 6291460
  7.2 6.6 %copy-start.1 = (bf16[512,512]{1,0:T(8,128)(2,1)S(1)}, bf16[512,512]{1,0:T(8,128)(2,1)}, u32[]{:S(2)}) copy-start(bf16[512,512]{1,0:T(8,128)(2,1)} %param.11) | copy-start | bytes 1572868
  7.2 29.2 %copy-start.5 = (f32[4]{0:T(128)S(1)}, f32[4]{0:T(128)}, u32[]{:S(2)}) copy-start(f32[4]{0:T(128)} %param.13) | copy-start | bytes 52
  7.2 46.9 %all-gather.10.cloned.1.call-start = ((), (), s32[]{:S(2)}) async-start(), calls=%async_computation.3 | async-start | bytes 1179648 | tf_op jit(solution)/shard_map/all_gather | solution.py:17
  11.0 66.0 %all-gather.8.cloned.1.call-start = ((), (), s32[]{:S(2)}) async-start(), calls=%async_computation.2 | async-start | bytes 2621440 | tf_op jit(solution)/shard_map/all_gather | solution.py:110
  11.7 135.1 %all-gather.12.cloned.1.call-start = ((), (), s32[]{:S(2)}) async-start(), calls=%async_computation.4 | async-start | bytes 1179648 | tf_op jit(solution)/shard_map/all_gather | solution.py:17
  54.2 26.5 %copy-start.2 = (bf16[512,512]{0,1:T(8,128)(2,1)S(1)}, bf16[512,512]{0,1:T(8,128)(2,1)}, u32[]{:S(2)}) copy-start(bf16[512,512]{0,1:T(8,128)(2,1)} %copy.34) | copy-start | bytes 1572868
  79.9 0.8 copy-start.4
  82.3 86.2 %reduce-scatter.2.cloned.1.call-start = ((), (), s32[]{:S(2)}) async-start(), calls=%async_computation.1 | async-start | bytes 5242880 | tf_op jit(solution)/shard_map/reduce_scatter | solution.py:103
  87.9 2.1 %copy-start.3 = (bf16[512,512]{1,0:T(8,128)(2,1)S(1)}, bf16[512,512]{1,0:T(8,128)(2,1)}, u32[]{:S(2)}) copy-start(bf16[512,512]{1,0:T(8,128)(2,1)} %param.12) | copy-start | bytes 1572868
  87.9 2.6 %copy-start.6 = (f32[4,512,512]{1,2,0:T(8,128)S(1)}, f32[4,512,512]{1,2,0:T(8,128)}, u32[]{:S(2)}) copy-start(f32[4,512,512]{1,2,0:T(8,128)} %get-tuple-element.158) | copy-start | bytes 12582916
Sparse Core Ops, SparseCore 0:
  11.1 42.9 all-gather.9
  55.7 21.2 all-gather.7
  82.4 40.2 all-gather.11
  125.1 43.3 reduce-scatter.1
where the time goes:
time: 178 us; the launch traced here: 177 us
  matrix products  52.9 us (30%)
  waiting for transfers between devices  48 us (27%)
  blocking collectives  42.8 us (24%)
  between operations  13.9 us (8%)
  other arithmetic  10.1 us (6%)
  local copies, waits for them, and re-layouts  8.85 us (5%)
    all_gather x2, blocking collectives, entering(): lax.all_gather(a.astype(kind), axis)  42.8 us
    all_gather x1, waiting for transfers between devices, local(): lax.all_gather(cotangent, 'tp', axis=0, tiled=True)  21.1 us
    all_gather x2, waiting for transfers between devices, entering(): lax.all_gather(a.astype(kind), axis)  17.7 us
    dot_general x1, matrix products, local(): jnp.einsum('hlm,mhc->lhc', grad_scores, keys_h, preferred_element_type=jn...  8.85 us
    unnamed x19, local copies, waits for them, and re-layouts  8.81 us
    dot_general x1, matrix products, local(): jnp.einsum('hlm,lhc->mhc', grad_scores, query_h, preferred_element_type=j...  8.69 us
    reduce_scatter x1, waiting for transfers between devices, local(): lax.psum_scatter(jnp.dot(mixed, out_weight, preferred_element_type=jnp.fl...  8.41 us
    add x14, other arithmetic, add_pair(): return (earlier[0] + later[0], earlier[1] + later[1])  6.87 us
  transfers between devices with their start and end apart: 4, of which 3 were waited for; matrix products, arithmetic and copies ran while one was open for 34% of the time, Pallas kernels for 0%

commit v1 on v0

v1 whole, which is shorter than its diff:
```python
import functools

import jax
import jax.numpy as jnp
from jax import lax
from jax.experimental import pallas as pl
from jax.experimental.pallas import tpu as pltpu
from jax.sharding import PartitionSpec as P

HD = 128
PAD = 16
SCALE = HD ** (-0.5)

f32 = jnp.float32
bf16 = jnp.bfloat16

VM = pl.BlockSpec(memory_space=pltpu.VMEM)
SM = pl.BlockSpec(memory_space=pltpu.SMEM)


def dot(a, b, ca, cb):
    return lax.dot_general(a, b, (((ca,), (cb,)), ((), ())), preferred_element_type=f32)


def split(x):
    hi = x.astype(bf16)
    return hi, (x - hi.astype(f32)).astype(bf16)


def feat(x):
    return jnp.where(x > 0, x + 1.0, jnp.exp(jnp.minimum(x, 0.0)))


def slope(x):
    return jnp.where(x > 0, 1.0, jnp.exp(jnp.minimum(x, 0.0)))


def gate(beta_ref, h):
    return jax.nn.sigmoid(jnp.full((1, HD), beta_ref[h], f32))


def cols(h):
    return slice(h * HD, (h + 1) * HD)


def call(body, outs, specs, out_specs=None, scratch=(), flops=1 << 28, trans=0, name=None, vmem=40):
    if out_specs is None:
        out_specs = [VM] * len(outs)
    return pl.pallas_call(
        body,
        out_shape=[jax.ShapeDtypeStruct(s, d) for s, d in outs],
        in_specs=specs,
        out_specs=out_specs,
        scratch_shapes=list(scratch),
        compiler_params=pltpu.CompilerParams(vmem_limit_bytes=vmem << 20),
        cost_estimate=pl.CostEstimate(flops=flops, transcendentals=trans, bytes_accessed=1 << 20),
        name=name,
    )


def pad_rows(rows):
    return jnp.concatenate(rows + [jnp.zeros((PAD - len(rows), HD), f32)], 0).astype(bf16)


def own_memory_body(heads, k_ref, v_ref, o_ref):
    rows = []
    for h in range(heads):
        kf = feat(k_ref[:, cols(h)].astype(f32))
        hi, lo = split(kf)
        v = v_ref[:, cols(h)]
        o_ref[cols(h), :] = (dot(hi, v, 0, 0) + dot(lo, v, 0, 0)).astype(bf16)
        rows.append(jnp.sum(kf, 0, keepdims=True))
    o_ref[heads * HD :, :] = pad_rows(rows)


def read_memory(qf, mem_ref, heads, h):
    qh, ql = split(qf)
    mh, ml = split(mem_ref[cols(h), :])
    msum = mem_ref[heads * HD + h : heads * HD + h + 1, :]
    numer = dot(qh, mh, 1, 0) + dot(ql, mh, 1, 0) + dot(qh, ml, 1, 0)
    denom = jnp.sum(qf * msum, 1, keepdims=True) + 1.0
    r = 1.0 / denom
    return numer * r, r, mh, ml, msum


def probs_parts(q_ref, k_ref, h, j, block):
    q = q_ref[j * block : (j + 1) * block, cols(h)]
    parts = []
    for i in range(j + 1):
        k = k_ref[i * block : (i + 1) * block, cols(h)]
        s = dot(k, q, 1, 1) * SCALE
        if i == j:
            shape = (block, block)
            keep = lax.broadcasted_iota(jnp.int32, shape, 0) <= lax.broadcasted_iota(jnp.int32, shape, 1)
            s = jnp.where(keep, s, -jnp.inf)
        parts.append(s)
    top = functools.reduce(jnp.maximum, [jnp.max(s, 0, keepdims=True) for s in parts])
    parts = [jnp.exp(s - top) for s in parts]
    r = 1.0 / sum(jnp.sum(e, 0, keepdims=True) for e in parts)
    return q, [e * r for e in parts]


def local_forward_body(heads, block, q_ref, k_ref, v_ref, o_ref):
    for h in range(heads):
        vt = v_ref[:, cols(h)].T
        for j in range(q_ref.shape[0] // block):
            _, parts = probs_parts(q_ref, k_ref, h, j, block)
            acc = sum(
                dot(vt[:, i * block : (i + 1) * block], p.astype(bf16), 1, 0) for i, p in enumerate(parts)
            )
            o_ref[j * block : (j + 1) * block, cols(h)] = acc.T


def grad_mixed_body(count, place_ref, *refs):
    pieces, w_ref, o_ref, all_ref = refs[:count], refs[count], refs[count + 1], refs[count + 2]
    rows = pieces[0].shape[0]
    for i, piece in enumerate(pieces):
        spot = pl.multiple_of(place_ref[i] * rows, rows)
        all_ref[pl.ds(spot, rows), :] = piece[...]
    o_ref[...] = dot(all_ref[...], w_ref[...], 1, 1).astype(bf16)


def memory_grad_body(heads, q_ref, mem_ref, g_ref, beta_ref, o_ref):
    rows = []
    for h in range(heads):
        qf = feat(q_ref[:, cols(h)].astype(f32))
        mem_out, r, _, _, _ = read_memory(qf, mem_ref, heads, h)
        gmem = gate(beta_ref, h) * g_ref[:, cols(h)].astype(f32)
        nh, nl = split(gmem * r)
        gden = -jnp.sum(gmem * mem_out, 1, keepdims=True) * r
        qh, ql = split(qf)
        o_ref[cols(h), :] = (dot(qh, nh, 0, 0) + dot(ql, nh, 0, 0) + dot(qh, nl, 0, 0)).astype(bf16)
        rows.append(jnp.sum(gden * qf, 0, keepdims=True))
    o_ref[heads * HD :, :] = pad_rows(rows)


def output_body(heads, count, place_ref, q_ref, mem_ref, lo_ref, beta_ref, w_ref, send_ref, keep_ref, mix_ref):
    for h in range(heads):
        qf = feat(q_ref[:, cols(h)].astype(f32))
        mem_out = read_memory(qf, mem_ref, heads, h)[0]
        g = gate(beta_ref, h)
        mix_ref[:, cols(h)] = (g * mem_out + (1.0 - g) * lo_ref[:, cols(h)]).astype(bf16)
    rows = q_ref.shape[0] // count
    half = count // 2

    def gathered(first):
        out = []
        for i in range(first, first + half):
            spot = pl.multiple_of(place_ref[i] * rows, rows)
            out.append(mix_ref[pl.ds(spot, rows), :])
        return jnp.concatenate(out, 0)

    send_ref[...] = dot(gathered(0), w_ref[...], 1, 0).astype(bf16)
    keep_ref[...] = dot(gathered(half), w_ref[...], 1, 0)


def local_backward_body(heads, block, q_ref, k_ref, v_ref, g_ref, mem_ref, beta_ref, gq_ref, gk_ref, gv_ref):
    blocks = q_ref.shape[0] // block
    for h in range(heads):
        g = gate(beta_ref, h)
        kt = k_ref[:, cols(h)].T
        gk = [None] * blocks
        gv = [None] * blocks

        def add(acc, i, x):
            acc[i] = x if acc[i] is None else acc[i] + x

        gq = []
        for j in range(blocks):
            q, parts = probs_parts(q_ref, k_ref, h, j, block)
            gl = ((1.0 - g) * g_ref[j * block : (j + 1) * block, cols(h)].astype(f32)).astype(bf16)
            gps = [dot(v_ref[i * block : (i + 1) * block, cols(h)], gl, 1, 1) for i in range(j + 1)]
            delta = sum(jnp.sum(p * gp, 0, keepdims=True) for p, gp in zip(parts, gps))
            acc = None
            for i, (p, gp) in enumerate(zip(parts, gps)):
                gs = (p * (gp - delta) * SCALE).astype(bf16)
                add(gk, i, dot(gs, q, 1, 0))
                add(gv, i, dot(p.astype(bf16), gl, 1, 0))
                t = dot(kt[:, i * block : (i + 1) * block], gs, 1, 0)
                acc = t if acc is None else acc + t
            gq.append(acc.T)
        for i in range(blocks):
            gk_ref[i * block : (i + 1) * block, cols(h)] = gk[i]
            gv_ref[i * block : (i + 1) * block, cols(h)] = gv[i]
        qx = q_ref[:, cols(h)].astype(f32)
        qf = feat(qx)
        mem_out, r, mh, ml, msum = read_memory(qf, mem_ref, heads, h)
        gmem = g * g_ref[:, cols(h)].astype(f32)
        nh, nl = split(gmem * r)
        gden = -jnp.sum(gmem * mem_out, 1, keepdims=True) * r
        gqf = dot(nh, mh, 1, 1) + dot(nl, mh, 1, 1) + dot(nh, ml, 1, 1) + gden * msum
        gq_ref[:, cols(h)] = (jnp.concatenate(gq, 0) + gqf * slope(qx)).astype(bf16)


def final_body(heads, k_ref, v_ref, mem_ref, kl_ref, vl_ref, gk_ref, gv_ref):
    for h in range(heads):
        kx = k_ref[:, cols(h)].astype(f32)
        kh, klo = split(feat(kx))
        mh, ml = split(mem_ref[cols(h), :])
        msum = mem_ref[heads * HD + h : heads * HD + h + 1, :]
        v = v_ref[:, cols(h)]
        gkf = dot(v, mh, 1, 1) + dot(v, ml, 1, 1) + msum
        gk_ref[:, cols(h)] = (kl_ref[:, cols(h)] + gkf * slope(kx)).astype(bf16)
        vm = dot(kh, mh, 1, 0) + dot(klo, mh, 1, 0) + dot(kh, ml, 1, 0)
        gv_ref[:, cols(h)] = (vl_ref[:, cols(h)] + vm).astype(bf16)


def swap(x, axis, bit):
    count = lax.axis_size(axis)
    return lax.ppermute(x, axis, [(i, i ^ bit) for i in range(count)])


def scan(own, axis, backward):
    count = lax.axis_size(axis)
    place = lax.axis_index(axis)
    total = own
    state = jnp.zeros(own.shape, f32)
    bit = 1
    while bit < count:
        other = swap(total.astype(bf16), axis, bit).astype(f32)
        upper = (place & bit) != 0
        take = jnp.logical_not(upper) if backward else upper
        state = state + jnp.where(take, other, 0.0)
        total = total.astype(f32) + other
        bit *= 2
    return state


def reverse_bits(value, count):
    out = 0
    bit = 1
    while bit < count:
        out = out * 2 + (1 if value & bit else 0)
        bit *= 2
    return out


def local(query, keys, values, beta, out_weight, cotangent):
    length, width = query.shape
    heads = width // HD
    model = out_weight.shape[1]
    tp = lax.axis_size("tp")
    place = lax.axis_index("tp")
    block = min(256, length)
    packed = (heads * HD + PAD, HD)

    bit = tp // 2
    pieces = [cotangent]
    while bit:
        pieces = pieces + [swap(p, "tp", bit) for p in pieces]
        bit //= 2
    gather_places = jnp.stack([place ^ reverse_bits(i, tp) for i in range(tp)]).astype(jnp.int32)
    scatter_places = jnp.stack([place ^ reverse_bits(tp - 1 - i, tp) for i in range(tp)]).astype(jnp.int32)

    own = call(
        functools.partial(own_memory_body, heads), [(packed, bf16)], [VM, VM], name="own_memory"
    )(keys, values)[0]
    memory = scan(own, "seq", False)
    local_out = call(
        functools.partial(local_forward_body, heads, block),
        [((length, width), f32)],
        [VM, VM, VM],
        name="local_forward",
    )(query, keys, values)[0]
    grad = call(
        functools.partial(grad_mixed_body, tp),
        [((length, width), bf16)],
        [SM] + [VM] * (tp + 1),
        scratch=[pltpu.VMEM((length, model), bf16)],
        name="grad_mixed",
    )(gather_places, *pieces, out_weight)[0]
    memory_grad = call(
        functools.partial(memory_grad_body, heads),
        [(packed, bf16)],
        [VM, VM, VM, SM],
        name="memory_grad",
    )(query, memory, grad, beta)[0]
    later = scan(memory_grad, "seq", True)
    part = length // tp
    send, keep = call(
        functools.partial(output_body, heads, tp),
        [((length // 2, model), bf16), ((length // 2, model), f32)],
        [SM, VM, VM, VM, SM, VM],
        scratch=[pltpu.VMEM((length, width), bf16)],
        name="output",
    )(scatter_places, query, memory, local_out, beta, out_weight)
    bit = 1
    while bit < tp:
        total = keep + swap(send, "tp", bit).astype(f32)
        bit *= 2
        if bit < tp:
            half = total.shape[0] // 2
            send, keep = total[:half].astype(bf16), total[half:]
    output = total.astype(bf16)
    grad_query, keys_local, values_local = call(
        functools.partial(local_backward_body, heads, block),
        [((length, width), bf16), ((length, width), f32), ((length, width), f32)],
        [VM, VM, VM, VM, VM, SM],
        name="local_backward",
    )(query, keys, values, grad, memory, beta)
    grad_keys, grad_values = call(
        functools.partial(final_body, heads),
        [((length, width), bf16), ((length, width), bf16)],
        [VM, VM, VM, VM, VM],
        name="final",
    )(keys, values, later, keys_local, values_local)
    return (output, grad_query, grad_keys, grad_values)


def solution(mesh):
    in_specs = (
        P("seq", "tp"),
        P("seq", "tp"),
        P("seq", "tp"),
        P("tp"),
        P("tp", None),
        P(("seq", "tp"), None),
    )
    out_specs = (P(("seq", "tp"), None), P("seq", "tp"), P("seq", "tp"), P("seq", "tp"))
    return jax.shard_map(local, mesh=mesh, in_specs=in_specs, out_specs=out_specs, check_vma=False)
```

time: 178 us -> 62.1 us (0.35)
  matrix products: 52.9 us -> 0 us
  blocking collectives: 42.8 us -> 0 us
  waiting for transfers between devices: 48 us -> 15.4 us
  Pallas kernels: 0 us -> 17.9 us
  starting transfers between devices: 0.34 us -> 16.4 us
  between operations: 13.9 us -> 0.79 us
  other arithmetic: 10.1 us -> 6.08 us
  local copies, waits for them, and re-layouts: 8.85 us -> 5.19 us
    dot_general x15 -> x0, matrix products: 48.3 us -> none  [the longest x1 8.85 us: local(): jnp.einsum('hlm,mhc->lhc', grad_scores, keys_h, preferred_element_type=jn...]
    all_gather x2 -> x0, blocking collectives: 42.8 us -> none  [entering(): lax.all_gather(a.astype(kind), axis)]
    all_gather x3 -> x0, waiting for transfers between devices: 38.9 us -> none  [the longest x1 21.1 us: local(): lax.all_gather(cotangent, 'tp', axis=0, tiled=True)]
    pallas_call x0 -> x7, Pallas kernels: none -> 17.9 us  [the longest x1 6.28 us: local(): call(functools.partial(local_backward_body, heads, block), [((length, wid...]
    ppermute x0 -> x11, starting transfers between devices: none -> 16.4 us  [swap(): return lax.ppermute(x, axis, [(i, i ^ bit) for i in range(count)])]
    ppermute x0 -> x11, waiting for transfers between devices: none -> 15.4 us  [swap(): return lax.ppermute(x, axis, [(i, i ^ bit) for i in range(count)])]
    reduce_scatter x1 -> x0, waiting for transfers between devices: 8.41 us -> none  [local(): lax.psum_scatter(jnp.dot(mixed, out_weight, preferred_element_type=jnp.fl...]
    sub x1 -> x0, matrix products: 4.55 us -> none  [local(): expo = jnp.exp(scores - top_score)]
  transfers between devices with their start and end apart: 4 -> 11, of which waited for: 3 -> 7; matrix products, arithmetic and copies ran while one was open for 34% -> 7% of each run, Pallas kernels for 0% -> 28%
where the time goes in v1:
time: 62.1 us; the launch traced here: 61.7 us
  Pallas kernels  17.9 us (29%)
  starting transfers between devices  16.4 us (26%)
  waiting for transfers between devices  15.4 us (25%)
  other arithmetic  6.08 us (10%)
  local copies, waits for them, and re-layouts  5.19 us (8%)
  between operations  0.79 us (1%)
    ppermute x11, starting transfers between devices, swap(): return lax.ppermute(x, axis, [(i, i ^ bit) for i in range(count)])  16.4 us
    ppermute x11, waiting for transfers between devices, swap(): return lax.ppermute(x, axis, [(i, i ^ bit) for i in range(count)])  15.4 us
    pallas_call x1, Pallas kernels, local(): call(functools.partial(local_backward_body, heads, block), [((length, wid...  6.28 us
    unnamed x32, local copies, waits for them, and re-layouts  4.27 us
    pallas_call x1, Pallas kernels, local(): call(functools.partial(output_body, heads, tp), [((length // 2, model), b...  2.66 us
    pallas_call x1, Pallas kernels, local(): call(functools.partial(grad_mixed_body, tp), [((length, width), bf16)], [...  2.42 us
    pallas_call x1, Pallas kernels, local(): call(functools.partial(local_forward_body, heads, block), [((length, widt...  2.21 us
    add x2, other arithmetic, scan(): state = state + jnp.where(take, other, 0.0)  2.11 us
  transfers between devices with their start and end apart: 11, of which 7 were waited for; matrix products, arithmetic and copies ran while one was open for 7% of the time, Pallas kernels for 28%

profile of v1, /device:TPU:0, one launch (start us, length us, event | category | flops | bytes accessed | tf_op | source)
XLA Modules:
  0.0 61.7 jit_solution(10928585600420094519)
XLA Ops:
  0.7 1.1 %copy-done.2 = bf16[512,512]{1,0:T(8,128)(2,1)S(1)} copy-done((bf16[512,512]{1,0:T(8,128)(2,1)S(1)}, bf16[512,512]{1,0:T(8,128)(2,1)}, u32[]{:S(2)}) %copy-start.2) | copy-done | bytes 524312
  3.5 3.0 %collective-permute-start = (bf16[528,128]{1,0:T(8,128)(2,1)S(1)}, bf16[528,128]{1,0:T(8,128)(2,1)S(1)}, u32[]{:S(2)}, u32[]{:S(2)}) collective-permute-start(bf16[528,128]{1,0:T(8,128)(2,1)S(1)} %own_memory.1), channel_id=1, source_target_pairs={{0,4},{4,0},{8,12},{12,8},{16,20},{20,16},{24,28},{28,24},{1,5},{5... | collective-permute-start | bytes 405512 | tf_op jit(solution)/shard_map/ppermute | solution.py:210
  6.5 3.6 %collective-permute-done = bf16[528,128]{1,0:T(8,128)(2,1)S(1)} collective-permute-done((bf16[528,128]{1,0:T(8,128)(2,1)S(1)}, bf16[528,128]{1,0:T(8,128)(2,1)S(1)}, u32[]{:S(2)}, u32[]{:S(2)}) %collective-permute-start) | collective-permute-done | bytes 135200 | tf_op jit(solution)/shard_map/ppermute | solution.py:210
  10.8 1.8 %collective-permute-start.1 = (bf16[528,128]{1,0:T(8,128)(2,1)}, bf16[528,128]{1,0:T(8,128)(2,1)S(1)}, u32[]{:S(2)}, u32[]{:S(2)}) collective-permute-start(bf16[528,128]{1,0:T(8,128)(2,1)} %fusion.7), channel_id=1, source_target_pairs={{0,8},{4,12},{8,0},{12,4},{16,24},{20,28},{24,16},{28,20},{1,9},{5... | collective-permute-start | bytes 405512 | tf_op jit(solution)/shard_map/ppermute | solution.py:210
  12.6 1.5 %collective-permute-start.5 = (bf16[128,2048]{1,0:T(8,128)(2,1)}, bf16[128,2048]{1,0:T(8,128)(2,1)}, u32[]{:S(2)}, u32[]{:S(2)}) collective-permute-start(bf16[128,2048]{1,0:T(8,128)(2,1)} %refs_0_.1), channel_id=1, source_target_pairs={{0,2},{1,3},{2,0},{3,1},{4,6},{5,7},{6,4},{7,5},{8,10},{9,11},{10,... | collective-permute-start | bytes 1572872 | tf_op jit(solution)/shard_map/ppermute | solution.py:210
  14.1 1.9 %collective-permute-done.1 = bf16[528,128]{1,0:T(8,128)(2,1)S(1)} collective-permute-done((bf16[528,128]{1,0:T(8,128)(2,1)}, bf16[528,128]{1,0:T(8,128)(2,1)S(1)}, u32[]{:S(2)}, u32[]{:S(2)}) %collective-permute-start.1) | collective-permute-done | bytes 135200 | tf_op jit(solution)/shard_map/ppermute | solution.py:210
  16.1 2.9 %collective-permute-start.2 = (bf16[528,128]{1,0:T(8,128)(2,1)S(1)}, bf16[528,128]{1,0:T(8,128)(2,1)S(1)}, u32[]{:S(2)}, u32[]{:S(2)}) collective-permute-start(bf16[528,128]{1,0:T(8,128)(2,1)S(1)} %fusion.3), channel_id=1, source_target_pairs={{0,16},{4,20},{8,24},{12,28},{16,0},{20,4},{24,8},{28,12},{1,17},{... | collective-permute-start | bytes 405512 | tf_op jit(solution)/shard_map/ppermute | solution.py:210
  19.0 1.0 %copy-done.5 = bf16[512,512]{1,0:T(8,128)(2,1)S(1)} copy-done((bf16[512,512]{1,0:T(8,128)(2,1)S(1)}, bf16[512,512]{1,0:T(8,128)(2,1)}, u32[]{:S(2)}) %copy-start.5) | copy-done | bytes 524312
  20.0 2.2 %local_forward.1.lo_ref = f32[512,512]{1,0:T(8,128)S(1)} custom-call(bf16[512,512]{1,0:T(8,128)(2,1)S(1)} %copy-done.1, bf16[512,512]{1,0:T(8,128)(2,1)S(1)} %copy-done.3, bf16[512,512]{1,0:T(8,128)(2,1)S(1)} %copy-done.5), custom_call_target="tpu_custom_call" | custom-call | flops 268435456 | bytes 1048576 | tf_op jit(solution)/shard_map/local_forward/pallas_call | solution.py:259
  22.3 1.2 %collective-permute-done.2 = bf16[528,128]{1,0:T(8,128)(2,1)S(1)} collective-permute-done((bf16[528,128]{1,0:T(8,128)(2,1)S(1)}, bf16[528,128]{1,0:T(8,128)(2,1)S(1)}, u32[]{:S(2)}, u32[]{:S(2)}) %collective-permute-start.2) | collective-permute-done | bytes 135200 | tf_op jit(solution)/shard_map/ppermute | solution.py:210
  24.6 2.7 %output.1 = (bf16[256,2048]{1,0:T(8,128)(2,1)S(1)}, f32[256,2048]{1,0:T(8,128)S(1)}) custom-call(s32[4]{0:T(128)S(1)} %pad_add_fusion.place_ref, bf16[512,512]{1,0:T(8,128)(2,1)S(1)} %copy-done.1, f32[528,128]{1,0:T(8,128)S(1)} %fusion.2.mem_ref, f32[512,512]{1,0:T(8,128)S(1)} %local_forward.1.lo_ref, f32[4]{0:T(128)S(1)} %copy-done.10, ...), custom_call_target="tpu_custom_call" | custom-call | flops 268435456 | bytes 1048576 | tf_op jit(solution)/shard_map/output/pallas_call | solution.py:280
  28.0 2.7 %collective-permute-done.6.refs_2_ = bf16[128,2048]{1,0:T(8,128)(2,1)S(1)} collective-permute-done((bf16[128,2048]{1,0:T(8,128)(2,1)S(1)}, bf16[128,2048]{1,0:T(8,128)(2,1)S(1)}, u32[]{:S(2)}, u32[]{:S(2)}) %collective-permute-start.6) | collective-permute-done | bytes 524320 | tf_op jit(solution)/shard_map/ppermute | solution.py:210
  31.5 2.4 %grad_mixed.1.g_ref = bf16[512,512]{1,0:T(8,128)(2,1)S(1)} custom-call(s32[4]{0:T(128)S(1)} %pad_add_fusion.1.place_ref, bf16[128,2048]{1,0:T(8,128)(2,1)S(1)} %copy-done.9, bf16[128,2048]{1,0:T(8,128)(2,1)} %collective-permute-done.5.refs_1_, bf16[128,2048]{1,0:T(8,128)(2,1)S(1)} %collective-permute-done.6.refs_2_, ...), custom_call_target="tpu_custom_call" | custom-call | flops 268435456 | bytes 1048576 | tf_op jit(solution)/shard_map/grad_mixed/pallas_call | solution.py:265
  33.9 1.8 %memory_grad.1 = bf16[528,128]{1,0:T(8,128)(2,1)S(1)} custom-call(bf16[512,512]{1,0:T(8,128)(2,1)S(1)} %copy-done.1, f32[528,128]{1,0:T(8,128)S(1)} %fusion.2.mem_ref, bf16[512,512]{1,0:T(8,128)(2,1)S(1)} %grad_mixed.1.g_ref, f32[4]{0:T(128)S(1)} %copy-done.10), custom_call_target="tpu_custom_call" | custom-call | flops 268435456 | bytes 1048576 | tf_op jit(solution)/shard_map/memory_grad/pallas_call | solution.py:272
  35.7 1.8 %collective-permute-start.8 = (bf16[528,128]{1,0:T(8,128)(2,1)S(1)}, bf16[528,128]{1,0:T(8,128)(2,1)S(1)}, u32[]{:S(2)}, u32[]{:S(2)}) collective-permute-start(bf16[528,128]{1,0:T(8,128)(2,1)S(1)} %memory_grad.1), channel_id=1, source_target_pairs={{0,4},{4,0},{8,12},{12,8},{16,20},{20,16},{24,28},{28,24},{1,5},{5... | collective-permute-start | bytes 405512 | tf_op jit(solution)/shard_map/ppermute | solution.py:210
  37.5 3.9 %collective-permute-done.8 = bf16[528,128]{1,0:T(8,128)(2,1)S(1)} collective-permute-done((bf16[528,128]{1,0:T(8,128)(2,1)S(1)}, bf16[528,128]{1,0:T(8,128)(2,1)S(1)}, u32[]{:S(2)}, u32[]{:S(2)}) %collective-permute-start.8) | collective-permute-done | bytes 135200 | tf_op jit(solution)/shard_map/ppermute | solution.py:210
  43.7 1.5 %collective-permute-start.4 = (bf16[128,2048]{1,0:T(8,128)(2,1)}, bf16[128,2048]{1,0:T(8,128)(2,1)}, u32[]{:S(2)}, u32[]{:S(2)}) collective-permute-start(bf16[128,2048]{1,0:T(8,128)(2,1)} %slice.15), channel_id=1, source_target_pairs={{0,2},{1,3},{2,0},{3,1},{4,6},{5,7},{6,4},{7,5},{8,10},{9,11},{10,... | collective-permute-start | bytes 1572872 | tf_op jit(solution)/shard_map/ppermute | solution.py:210
  45.3 1.3 %collective-permute-done.9 = bf16[528,128]{1,0:T(8,128)(2,1)S(1)} collective-permute-done((bf16[528,128]{1,0:T(8,128)(2,1)S(1)}, bf16[528,128]{1,0:T(8,128)(2,1)S(1)}, u32[]{:S(2)}, u32[]{:S(2)}) %collective-permute-start.9) | collective-permute-done | bytes 135200 | tf_op jit(solution)/shard_map/ppermute | solution.py:210
  47.3 2.3 %collective-permute-start.10 = (bf16[528,128]{1,0:T(8,128)(2,1)}, bf16[528,128]{1,0:T(8,128)(2,1)}, u32[]{:S(2)}, u32[]{:S(2)}) collective-permute-start(bf16[528,128]{1,0:T(8,128)(2,1)} %fusion.6), channel_id=1, source_target_pairs={{0,16},{4,20},{8,24},{12,28},{16,0},{20,4},{24,8},{28,12},{1,17},{... | collective-permute-start | bytes 405512 | tf_op jit(solution)/shard_map/ppermute | solution.py:210
  49.6 1.0 %copy-done.8 = bf16[512,512]{1,0:T(8,128)(2,1)S(1)} copy-done((bf16[512,512]{1,0:T(8,128)(2,1)S(1)}, bf16[512,512]{1,0:T(8,128)(2,1)}, u32[]{:S(2)}) %copy-start.8) | copy-done | bytes 524312
  50.6 6.3 %local_backward.1 = (bf16[512,512]{1,0:T(8,128)(2,1)}, f32[512,512]{1,0:T(8,128)S(1)}, f32[512,512]{1,0:T(8,128)S(1)}) custom-call(bf16[512,512]{1,0:T(8,128)(2,1)S(1)} %copy-done.1, bf16[512,512]{1,0:T(8,128)(2,1)S(1)} %copy-done.3, bf16[512,512]{1,0:T(8,128)(2,1)S(1)} %copy-done.6, bf16[512,512]{1,0:T(8,128)(2,1)S(1)} %copy-done.8, ...), custom_call_target="tpu_custom_call" | custom-call | flops 268435456 | bytes 1048576 | tf_op jit(solution)/shard_map/local_backward/pallas_call | solution.py:295
  56.9 1.1 %fusion.5.mem_ref = f32[528,128]{1,0:T(8,128)S(1)} fusion(bf16[528,128]{1,0:T(8,128)(2,1)S(1)} %collective-permute-done.8, bf16[528,128]{1,0:T(8,128)(2,1)S(1)} %copy-done.15, bf16[528,128]{1,0:T(8,128)(2,1)} %collective-permute-done.10, pred[]{:T(512)S(6)} %not.11, pred[]{:T(512)S(6)} %not.10, pred[]{:T(512)S(6)} %not.9), kind=kLoop, calls=%fused_computation.16 | loop fusion | flops 540672 | bytes 675843 | tf_op jit(solution)/shard_map/add | solution.py:223
  58.0 1.7 %final.1 = (bf16[512,512]{1,0:T(8,128)(2,1)}, bf16[512,512]{1,0:T(8,128)(2,1)}) custom-call(bf16[512,512]{1,0:T(8,128)(2,1)S(1)} %copy-done.3, bf16[512,512]{1,0:T(8,128)(2,1)S(1)} %copy-done.6, f32[528,128]{1,0:T(8,128)S(1)} %fusion.5.mem_ref, f32[512,512]{1,0:T(8,128)S(1)} %get-tuple-element.14.kl_ref, f32[512,512]{1,0:T(8,128)S(1)} %get-tuple-element.15.vl_ref), custom_call_target="tpu_custom_call" | custom-call | flops 268435456 | bytes 1048576 | tf_op jit(solution)/shard_map/final/pallas_call | solution.py:301
  59.8 1.9 %fusion = bf16[128,2048]{1,0:T(8,128)(2,1)} fusion(f32[256,2048]{1,0:T(8,128)S(1)} %copy-done.12, bf16[128,2048]{1,0:T(8,128)(2,1)} %collective-permute-done.4), kind=kLoop, calls=%fused_computation.3 | loop fusion | flops 786432 | bytes 2097152 | tf_op jit(solution)/shard_map/convert_element_type | solution.py:294
  (48 shorter events, 8.1 us)
Async XLA Ops:
  0.6 18.4 %copy-start.1 = (bf16[512,512]{1,0:T(8,128)(2,1)S(1)}, bf16[512,512]{1,0:T(8,128)(2,1)}, u32[]{:S(2)}) copy-start(bf16[512,512]{1,0:T(8,128)(2,1)} %q_ref.7) | copy-start | bytes 1572868
  0.6 1.1 %copy-start.2 = (bf16[512,512]{1,0:T(8,128)(2,1)S(1)}, bf16[512,512]{1,0:T(8,128)(2,1)}, u32[]{:S(2)}) copy-start(bf16[512,512]{1,0:T(8,128)(2,1)} %k_ref.7) | copy-start | bytes 1572868
  2.8 16.2 %copy-start.3 = (bf16[512,512]{1,0:T(8,128)(2,1)S(1)}, bf16[512,512]{1,0:T(8,128)(2,1)}, u32[]{:S(2)}) copy-start(bf16[512,512]{1,0:T(8,128)(2,1)} %k_ref.7) | copy-start | bytes 1572868
  2.8 21.7 %copy-start.10 = (f32[4]{0:T(128)S(1)}, f32[4]{0:T(128)}, u32[]{:S(2)}) copy-start(f32[4]{0:T(128)} %beta_ref.5) | copy-start | bytes 52
  3.5 21.1 %copy-start = (bf16[512,2048]{1,0:T(8,128)(2,1)S(1)}, bf16[512,2048]{1,0:T(8,128)(2,1)}, u32[]{:S(2)}) copy-start(bf16[512,2048]{1,0:T(8,128)(2,1)} %refs_4_.1) | copy-start | bytes 6291460
  3.5 6.6 %collective-permute-start = (bf16[528,128]{1,0:T(8,128)(2,1)S(1)}, bf16[528,128]{1,0:T(8,128)(2,1)S(1)}, u32[]{:S(2)}, u32[]{:S(2)}) collective-permute-start(bf16[528,128]{1,0:T(8,128)(2,1)S(1)} %own_memory.1), channel_id=1, source_target_pairs={{0,4},{4,0},{8,12},{12,8},{16,20},{20,16},{24,28},{28,24},{1,5},{5... | collective-permute-start | bytes 405512 | tf_op jit(solution)/shard_map/ppermute | solution.py:210
  10.8 5.2 %collective-permute-start.1 = (bf16[528,128]{1,0:T(8,128)(2,1)}, bf16[528,128]{1,0:T(8,128)(2,1)S(1)}, u32[]{:S(2)}, u32[]{:S(2)}) collective-permute-start(bf16[528,128]{1,0:T(8,128)(2,1)} %fusion.7), channel_id=1, source_target_pairs={{0,8},{4,12},{8,0},{12,4},{16,24},{20,28},{24,16},{28,20},{1,9},{5... | collective-permute-start | bytes 405512 | tf_op jit(solution)/shard_map/ppermute | solution.py:210
  12.6 15.2 %collective-permute-start.5 = (bf16[128,2048]{1,0:T(8,128)(2,1)}, bf16[128,2048]{1,0:T(8,128)(2,1)}, u32[]{:S(2)}, u32[]{:S(2)}) collective-permute-start(bf16[128,2048]{1,0:T(8,128)(2,1)} %refs_0_.1), channel_id=1, source_target_pairs={{0,2},{1,3},{2,0},{3,1},{4,6},{5,7},{6,4},{7,5},{8,10},{9,11},{10,... | collective-permute-start | bytes 1572872 | tf_op jit(solution)/shard_map/ppermute | solution.py:210
  16.0 6.3 %copy-start.13 = (bf16[528,128]{1,0:T(8,128)(2,1)}, bf16[528,128]{1,0:T(8,128)(2,1)S(1)}, u32[]{:S(2)}) copy-start(bf16[528,128]{1,0:T(8,128)(2,1)S(1)} %collective-permute-done.1) | copy-start | bytes 405508
  16.1 7.5 %collective-permute-start.2 = (bf16[528,128]{1,0:T(8,128)(2,1)S(1)}, bf16[528,128]{1,0:T(8,128)(2,1)S(1)}, u32[]{:S(2)}, u32[]{:S(2)}) collective-permute-start(bf16[528,128]{1,0:T(8,128)(2,1)S(1)} %fusion.3), channel_id=1, source_target_pairs={{0,16},{4,20},{8,24},{12,28},{16,0},{20,4},{24,8},{28,12},{1,17},{... | collective-permute-start | bytes 405512 | tf_op jit(solution)/shard_map/ppermute | solution.py:210
  24.5 2.8 %copy-start.9 = (bf16[128,2048]{1,0:T(8,128)(2,1)S(1)}, bf16[128,2048]{1,0:T(8,128)(2,1)}, u32[]{:S(2)}) copy-start(bf16[128,2048]{1,0:T(8,128)(2,1)} %refs_0_.1) | copy-start | bytes 1572868
  27.2 15.2 %collective-permute-start.3 = (bf16[256,2048]{1,0:T(8,128)(2,1)S(1)}, bf16[256,2048]{1,0:T(8,128)(2,1)S(1)}, u32[]{:S(2)}, u32[]{:S(2)}) collective-permute-start(bf16[256,2048]{1,0:T(8,128)(2,1)S(1)} %get-tuple-element.12), channel_id=1, source_target_pairs={{0,1},{1,0},{2,3},{3,2},{4,5},{5,4},{6,7},{7,6},{8,9},{9,8},{10,11... | collective-permute-start | bytes 3145736 | tf_op jit(solution)/shard_map/ppermute | solution.py:210
  27.3 3.4 %collective-permute-start.6 = (bf16[128,2048]{1,0:T(8,128)(2,1)S(1)}, bf16[128,2048]{1,0:T(8,128)(2,1)S(1)}, u32[]{:S(2)}, u32[]{:S(2)}) collective-permute-start(bf16[128,2048]{1,0:T(8,128)(2,1)S(1)} %copy-done.9), channel_id=1, source_target_pairs={{0,1},{1,0},{2,3},{3,2},{4,5},{5,4},{6,7},{7,6},{8,9},{9,8},{10,11... | collective-permute-start | bytes 1572872 | tf_op jit(solution)/shard_map/ppermute | solution.py:210
  27.8 3.6 %collective-permute-start.7 = (bf16[128,2048]{1,0:T(8,128)(2,1)}, bf16[128,2048]{1,0:T(8,128)(2,1)S(1)}, u32[]{:S(2)}, u32[]{:S(2)}) collective-permute-start(bf16[128,2048]{1,0:T(8,128)(2,1)} %collective-permute-done.5.refs_1_), channel_id=1, source_target_pairs={{0,1},{1,0},{2,3},{3,2},{4,5},{5,4},{6,7},{7,6},{8,9},{9,8},{10,11... | collective-permute-start | bytes 1572872 | tf_op jit(solution)/shard_map/ppermute | solution.py:210
  33.9 8.9 %copy-start.7 = (bf16[512,512]{1,0:T(8,128)(2,1)}, bf16[512,512]{1,0:T(8,128)(2,1)S(1)}, u32[]{:S(2)}) copy-start(bf16[512,512]{1,0:T(8,128)(2,1)S(1)} %grad_mixed.1.g_ref) | copy-start | bytes 1572868
  35.7 5.7 %collective-permute-start.8 = (bf16[528,128]{1,0:T(8,128)(2,1)S(1)}, bf16[528,128]{1,0:T(8,128)(2,1)S(1)}, u32[]{:S(2)}, u32[]{:S(2)}) collective-permute-start(bf16[528,128]{1,0:T(8,128)(2,1)S(1)} %memory_grad.1), channel_id=1, source_target_pairs={{0,4},{4,0},{8,12},{12,8},{16,20},{20,16},{24,28},{28,24},{1,5},{5... | collective-permute-start | bytes 405512 | tf_op jit(solution)/shard_map/ppermute | solution.py:210
  41.5 5.1 %collective-permute-start.9 = (bf16[528,128]{1,0:T(8,128)(2,1)S(1)}, bf16[528,128]{1,0:T(8,128)(2,1)S(1)}, u32[]{:S(2)}, u32[]{:S(2)}) collective-permute-start(bf16[528,128]{1,0:T(8,128)(2,1)S(1)} %fusion.8), channel_id=1, source_target_pairs={{0,8},{4,12},{8,0},{12,4},{16,24},{20,28},{24,16},{28,20},{1,9},{5... | collective-permute-start | bytes 405512 | tf_op jit(solution)/shard_map/ppermute | solution.py:210
  42.4 7.1 %copy-start.6 = (bf16[512,512]{1,0:T(8,128)(2,1)S(1)}, bf16[512,512]{1,0:T(8,128)(2,1)}, u32[]{:S(2)}) copy-start(bf16[512,512]{1,0:T(8,128)(2,1)} %v_ref.7) | copy-start | bytes 1572868
  42.8 4.5 %copy-start.11 = (f32[256,2048]{1,0:T(8,128)}, f32[256,2048]{1,0:T(8,128)S(1)}, u32[]{:S(2)}) copy-start(f32[256,2048]{1,0:T(8,128)S(1)} %convert_add_fusion) | copy-start | bytes 6291460
  43.7 16.1 %collective-permute-start.4 = (bf16[128,2048]{1,0:T(8,128)(2,1)}, bf16[128,2048]{1,0:T(8,128)(2,1)}, u32[]{:S(2)}, u32[]{:S(2)}) collective-permute-start(bf16[128,2048]{1,0:T(8,128)(2,1)} %slice.15), channel_id=1, source_target_pairs={{0,2},{1,3},{2,0},{3,1},{4,6},{5,7},{6,4},{7,5},{8,10},{9,11},{10,... | collective-permute-start | bytes 1572872 | tf_op jit(solution)/shard_map/ppermute | solution.py:210
  46.6 3.0 %copy-start.14 = (bf16[528,128]{1,0:T(8,128)(2,1)}, bf16[528,128]{1,0:T(8,128)(2,1)S(1)}, u32[]{:S(2)}) copy-start(bf16[528,128]{1,0:T(8,128)(2,1)S(1)} %collective-permute-done.9) | copy-start | bytes 405508
  47.3 9.6 %collective-permute-start.10 = (bf16[528,128]{1,0:T(8,128)(2,1)}, bf16[528,128]{1,0:T(8,128)(2,1)}, u32[]{:S(2)}, u32[]{:S(2)}) collective-permute-start(bf16[528,128]{1,0:T(8,128)(2,1)} %fusion.6), channel_id=1, source_target_pairs={{0,16},{4,20},{8,24},{12,28},{16,0},{20,4},{24,8},{28,12},{1,17},{... | collective-permute-start | bytes 405512 | tf_op jit(solution)/shard_map/ppermute | solution.py:210
  50.6 6.3 %copy-start.15 = (bf16[528,128]{1,0:T(8,128)(2,1)S(1)}, bf16[528,128]{1,0:T(8,128)(2,1)}, u32[]{:S(2)}) copy-start(bf16[528,128]{1,0:T(8,128)(2,1)} %copy-done.14) | copy-start | bytes 405508
  56.9 2.9 %copy-start.12 = (f32[256,2048]{1,0:T(8,128)S(1)}, f32[256,2048]{1,0:T(8,128)}, u32[]{:S(2)}) copy-start(f32[256,2048]{1,0:T(8,128)} %copy-done.11) | copy-start | bytes 6291460
  (3 other events, 3.1 us)

commit v2 on v1

v2 whole, which is shorter than its diff:
```python
import functools

import jax
import jax.numpy as jnp
from jax import lax
from jax.experimental import pallas as pl
from jax.experimental.pallas import tpu as pltpu
from jax.sharding import PartitionSpec as P


HD = 128
PAD = 16
SCALE = HD ** (-0.5)

f32 = jnp.float32
bf16 = jnp.bfloat16

VM = pl.BlockSpec(memory_space=pltpu.VMEM)


def dot(a, b, ca, cb):
    return lax.dot_general(a, b, (((ca,), (cb,)), ((), ())), preferred_element_type=f32)


def split(x):
    hi = x.astype(bf16)
    return hi, (x - hi.astype(f32)).astype(bf16)


def feat(x):
    return jnp.where(x > 0, x + 1.0, jnp.exp(jnp.minimum(x, 0.0)))


def slope(x):
    return jnp.where(x > 0, 1.0, jnp.exp(jnp.minimum(x, 0.0)))


def cols(h):
    return slice(h * HD, (h + 1) * HD)


def call(body, outs, specs, out_specs=None, scratch=(), flops=1 << 28, vmem=24, alias=None):
    if out_specs is None:
        out_specs = [VM] * len(outs)
    return pl.pallas_call(
        body,
        out_shape=[jax.ShapeDtypeStruct(s, d) for s, d in outs],
        in_specs=specs,
        out_specs=out_specs,
        scratch_shapes=list(scratch),
        input_output_aliases=alias or {},
        compiler_params=pltpu.CompilerParams(vmem_limit_bytes=vmem << 20),
        cost_estimate=pl.CostEstimate(flops=flops, transcendentals=0, bytes_accessed=1 << 20),
    )


def pad_rows(rows):
    return jnp.concatenate(rows + [jnp.zeros((PAD - len(rows), HD), f32)], 0).astype(bf16)


def own_memory_body(heads, k_hbm, v_hbm, q_hbm, beta_hbm, o_ref, k_ref, v_ref, q_ref, gate_ref, beta_ref, sems, beta_sem):
    beta_copy = pltpu.make_async_copy(beta_hbm, beta_ref, beta_sem)
    pairs = ((k_hbm, k_ref), (v_hbm, v_ref), (q_hbm, q_ref))
    copies = [
        [pltpu.make_async_copy(a.at[:, cols(h)], b.at[:, cols(h)], sems.at[i, h]) for i, (a, b) in enumerate(pairs)]
        for h in range(heads)
    ]
    for h in range(heads):
        copies[h][0].start()
        copies[h][1].start()
    beta_copy.start()
    for h in range(heads):
        copies[h][2].start()
    rows = []
    for h in range(heads):
        copies[h][0].wait()
        copies[h][1].wait()
        kf = feat(k_ref[:, cols(h)].astype(f32))
        hi, lo = split(kf)
        v = v_ref[:, cols(h)]
        o_ref[cols(h), :] = (dot(hi, v, 0, 0) + dot(lo, v, 0, 0)).astype(bf16)
        rows.append(jnp.sum(kf, 0, keepdims=True))
    o_ref[heads * HD :, :] = pad_rows(rows)
    beta_copy.wait()
    for h in range(heads):
        gate_ref[h : h + 1, :] = jax.nn.sigmoid(jnp.full((1, HD), beta_ref[h], f32))
    for h in range(heads):
        copies[h][2].wait()


def add_body(*refs):
    total = refs[0][...].astype(f32)
    for ref in refs[1:-1]:
        total = total + ref[...].astype(f32)
    refs[-1][...] = total.astype(bf16)


def scan_state(refs, backward, rows):
    place = lax.axis_index("seq")
    state = None
    for i, ref in enumerate(refs):
        upper = (place // (1 << i)) % 2
        take = (1 - upper if backward else upper).astype(f32)
        x = ref[rows, :].astype(f32) * take
        state = x if state is None else state + x
    return state


def read_memory(qf, mem_ref, heads, h):
    qh, ql = split(qf)
    mh, ml = split(mem_ref[cols(h), :])
    msum = mem_ref[heads * HD + h : heads * HD + h + 1, :]
    numer = dot(qh, mh, 1, 0) + dot(ql, mh, 1, 0) + dot(qh, ml, 1, 0)
    denom = jnp.sum(qf * msum, 1, keepdims=True) + 1.0
    r = 1.0 / denom
    return numer * r, r, mh, ml, msum


def probs_parts(q_ref, k_ref, h, j, block):
    q = q_ref[j * block : (j + 1) * block, cols(h)]
    parts = []
    for i in range(j + 1):
        k = k_ref[i * block : (i + 1) * block, cols(h)]
        s = dot(k, q, 1, 1) * SCALE
        if i == j:
            shape = (block, block)
            keep = lax.broadcasted_iota(jnp.int32, shape, 0) <= lax.broadcasted_iota(jnp.int32, shape, 1)
            s = jnp.where(keep, s, -jnp.inf)
        parts.append(s)
    top = functools.reduce(jnp.maximum, [jnp.max(s, 0, keepdims=True) for s in parts])
    parts = [jnp.exp(s - top) for s in parts]
    r = 1.0 / sum(jnp.sum(e, 0, keepdims=True) for e in parts)
    return q, [e * r for e in parts]


def local_forward_body(heads, block, q_ref, k_ref, v_ref, o_ref):
    for h in range(heads):
        vt = v_ref[:, cols(h)].T
        for j in range(q_ref.shape[0] // block):
            _, parts = probs_parts(q_ref, k_ref, h, j, block)
            acc = sum(
                dot(vt[:, i * block : (i + 1) * block], p.astype(bf16), 1, 0) for i, p in enumerate(parts)
            )
            o_ref[j * block : (j + 1) * block, cols(h)] = acc.T


def grad_mixed_body(*refs):
    pieces, w_ref, o_ref = refs[:-2], refs[-2], refs[-1]
    x = jnp.concatenate([p[...] for p in pieces], 0)
    o_ref[...] = dot(x, w_ref[...], 1, 1).astype(bf16)


def memory_grad_body(heads, count, order, *refs):
    grads, q_ref, gate_ref = refs[: len(order)], refs[len(order)], refs[len(order) + 1]
    mem_ref = refs[len(order) + 2]
    o_ref, g_ref = refs[-2:]
    place = lax.axis_index("tp")
    for grad, masks in zip(grads, order):
        rows = grad.shape[0] // len(masks)
        for i, m in enumerate(masks):
            spot = pl.multiple_of(flipped(place, m, count) * rows, rows)
            g_ref[pl.ds(spot, rows), :] = grad[i * rows : (i + 1) * rows, :]
    rows = []
    for h in range(heads):
        qf = feat(q_ref[:, cols(h)].astype(f32))
        mem_out, r, _, _, _ = read_memory(qf, mem_ref, heads, h)
        gmem = gate_ref[h : h + 1, :] * g_ref[:, cols(h)].astype(f32)
        nh, nl = split(gmem * r)
        gden = -jnp.sum(gmem * mem_out, 1, keepdims=True) * r
        qh, ql = split(qf)
        o_ref[cols(h), :] = (dot(qh, nh, 0, 0) + dot(ql, nh, 0, 0) + dot(qh, nl, 0, 0)).astype(bf16)
        rows.append(jnp.sum(gden * qf, 0, keepdims=True))
    o_ref[heads * HD :, :] = pad_rows(rows)


def flipped(place, mask, count):
    out = 0
    bit = 1
    while bit < count:
        own = (place // bit) % 2
        out = out + bit * ((1 - own) if mask & bit else own)
        bit *= 2
    return out


def mixed_rows(heads, count, masks, q_ref, mem_ref, lo_ref, gate_ref, mix_ref):
    place = lax.axis_index("tp")
    rows = q_ref.shape[0] // count
    for i, m in enumerate(masks):
        spot = pl.multiple_of(flipped(place, m, count) * rows, rows)
        for h in range(heads):
            qf = feat(q_ref[pl.ds(spot, rows), cols(h)].astype(f32))
            mem_out = read_memory(qf, mem_ref, heads, h)[0]
            g = gate_ref[h : h + 1, :]
            x = g * mem_out + (1.0 - g) * lo_ref[pl.ds(spot, rows), cols(h)]
            mix_ref[i * rows : (i + 1) * rows, cols(h)] = x.astype(bf16)


def output_send_body(heads, count, masks, steps, q_ref, lo_ref, gate_ref, w_ref, *refs):
    recvs, (mem_ref, send_ref, mix_ref) = refs[:steps], refs[steps:]
    mem_ref[...] = scan_state(recvs, False, slice(None))
    mixed_rows(heads, count, masks, q_ref, mem_ref, lo_ref, gate_ref, mix_ref)
    send_ref[...] = dot(mix_ref[...], w_ref[...], 1, 0).astype(bf16)


def output_keep_body(heads, count, masks, q_ref, mem_ref, lo_ref, gate_ref, w_ref, recv_ref, send_ref, keep_ref, mix_ref):
    mixed_rows(heads, count, masks, q_ref, mem_ref, lo_ref, gate_ref, mix_ref)
    total = dot(mix_ref[...], w_ref[...], 1, 0) + recv_ref[...].astype(f32)
    half = send_ref.shape[0]
    send_ref[...] = total[:half].astype(bf16)
    keep_ref[...] = total[half:]


def output_done_body(keep_ref, recv_ref, o_ref):
    o_ref[...] = (keep_ref[...] + recv_ref[...].astype(f32)).astype(bf16)


def local_backward_body(
    heads, group, block, q_ref, k_ref, v_ref, g_ref, mem_ref, gate_ref, *refs
):
    gq_hbm, gk_ref, gv_ref, gq_ref, sems = refs[-5:]
    blocks = q_ref.shape[0] // block
    copies = []
    for n, h in enumerate(group):
        g = gate_ref[h : h + 1, :]
        kt = k_ref[:, cols(h)].T
        gk = [None] * blocks
        gv = [None] * blocks

        def add(acc, i, x):
            acc[i] = x if acc[i] is None else acc[i] + x

        gq = []
        for j in range(blocks):
            q, parts = probs_parts(q_ref, k_ref, h, j, block)
            gl = ((1.0 - g) * g_ref[j * block : (j + 1) * block, cols(h)].astype(f32)).astype(bf16)
            gps = [dot(v_ref[i * block : (i + 1) * block, cols(h)], gl, 1, 1) for i in range(j + 1)]
            delta = sum(jnp.sum(p * gp, 0, keepdims=True) for p, gp in zip(parts, gps))
            acc = None
            for i, (p, gp) in enumerate(zip(parts, gps)):
                gs = (p * (gp - delta) * SCALE).astype(bf16)
                add(gk, i, dot(gs, q, 1, 0))
                add(gv, i, dot(p.astype(bf16), gl, 1, 0))
                t = dot(kt[:, i * block : (i + 1) * block], gs, 1, 0)
                acc = t if acc is None else acc + t
            gq.append(acc.T)
        for i in range(blocks):
            gk_ref[i * block : (i + 1) * block, cols(n)] = gk[i]
            gv_ref[i * block : (i + 1) * block, cols(n)] = gv[i]
        qx = q_ref[:, cols(h)].astype(f32)
        qf = feat(qx)
        mem_out, r, mh, ml, msum = read_memory(qf, mem_ref, heads, h)
        gmem = g * g_ref[:, cols(h)].astype(f32)
        nh, nl = split(gmem * r)
        gden = -jnp.sum(gmem * mem_out, 1, keepdims=True) * r
        gqf = dot(nh, mh, 1, 1) + dot(nl, mh, 1, 1) + dot(nh, ml, 1, 1) + gden * msum
        gq_ref[:, cols(n)] = (jnp.concatenate(gq, 0) + gqf * slope(qx)).astype(bf16)
        copy = pltpu.make_async_copy(gq_ref.at[:, cols(n)], gq_hbm.at[:, cols(h)], sems.at[n])
        copy.start()
        copies.append(copy)
    for copy in copies:
        copy.wait()


def final_body(heads, groups, steps, *refs):
    k_ref, v_ref = refs[:2]
    recvs = refs[2 : 2 + steps]
    locals_ = refs[2 + steps : 2 + steps + 2 * len(groups)]
    gk_hbm, gv_hbm, gk_ref, gv_ref, sems = refs[-5:]
    sums = scan_state(recvs, True, slice(heads * HD, heads * HD + PAD))
    copies = []
    for n, group in enumerate(groups):
        kl_ref, vl_ref = locals_[2 * n : 2 * n + 2]
        for i, h in enumerate(group):
            kx = k_ref[:, cols(h)].astype(f32)
            kh, klo = split(feat(kx))
            mh, ml = split(scan_state(recvs, True, cols(h)))
            v = v_ref[:, cols(h)]
            gkf = dot(v, mh, 1, 1) + dot(v, ml, 1, 1) + sums[h : h + 1, :]
            gk_ref[:, cols(h)] = (kl_ref[:, cols(i)] + gkf * slope(kx)).astype(bf16)
            copies.append(pltpu.make_async_copy(gk_ref.at[:, cols(h)], gk_hbm.at[:, cols(h)], sems.at[0, h]))
            copies[-1].start()
            vm = dot(kh, mh, 1, 0) + dot(klo, mh, 1, 0) + dot(kh, ml, 1, 0)
            gv_ref[:, cols(h)] = (vl_ref[:, cols(i)] + vm).astype(bf16)
            copies.append(pltpu.make_async_copy(gv_ref.at[:, cols(h)], gv_hbm.at[:, cols(h)], sems.at[1, h]))
            copies[-1].start()
    for copy in copies:
        copy.wait()


def swap(x, axis, bit):
    count = lax.axis_size(axis)
    return lax.ppermute(x, axis, [(i, i ^ bit) for i in range(count)])


def scan(own, axis):
    count = lax.axis_size(axis)
    recvs = []
    send = own
    bit = 1
    while bit < count:
        step = len(recvs)
        if step:
            specs = [VM] * (step + 1)
            send = call(add_body, [(own.shape, bf16)], specs, flops=1 << 20)(own, *recvs)[0]
        recvs.append(swap(send, axis, bit))
        bit *= 2
    return recvs


def reverse_bits(value, count):
    out = 0
    bit = 1
    while bit < count:
        out = out * 2 + (1 if value & bit else 0)
        bit *= 2
    return out


def local(query, keys, values, beta, out_weight, cotangent):
    length, width = query.shape
    heads = width // HD
    model = out_weight.shape[1]
    tp = lax.axis_size("tp")
    block = min(256, length)
    packed = (heads * HD + PAD, HD)
    hbm = pl.BlockSpec(memory_space=pltpu.HBM)
    full = (length, width)

    own, keys, values, query, gates = call(
        functools.partial(own_memory_body, heads),
        [(packed, bf16), (full, bf16), (full, bf16), (full, bf16), ((8, HD), f32)],
        [hbm] * 4,
        scratch=[pltpu.SMEM((heads,), f32), pltpu.SemaphoreType.DMA((3, heads)), pltpu.SemaphoreType.DMA],
    )(*[pltpu.with_memory_space_constraint(x, pltpu.HBM) for x in (keys, values, query, beta)])
    fwd = scan(own, "seq")
    steps = len(fwd)

    held = {0: cotangent}
    first, second = [0], []
    if tp > 1:
        held[1] = swap(cotangent, "tp", 1)
        first = [0, 1]
    bit = 2
    far = [0]
    while bit < tp:
        for m in list(far):
            held[m | bit] = swap(held[m], "tp", bit)
            far.append(m | bit)
        bit *= 2
    for m in far[1:]:
        held[m | 1] = swap(held[m], "tp", 1)
        second += [m, m | 1]
    order = [first] + ([second] if second else [])

    local_out = call(
        functools.partial(local_forward_body, heads, block), [(full, f32)], [VM, VM, VM]
    )(query, keys, values)[0]

    grads = []
    for masks in order:
        rows = cotangent.shape[0] * len(masks)
        grads.append(
            call(
                grad_mixed_body, [((rows, width), bf16)], [VM] * (len(masks) + 1)
            )(*[held[m] for m in masks], out_weight)[0]
        )

    places = [reverse_bits(tp - 1 - i, tp) for i in range(tp)]
    half = tp // 2
    memory, send = call(
        functools.partial(output_send_body, heads, tp, places[:half], steps),
        [(packed, f32), ((length // 2, model), bf16)],
        [VM] * (4 + steps),
        scratch=[pltpu.VMEM((length // 2, width), bf16)],
    )(query, local_out, gates, out_weight, *fwd)
    recv = swap(send, "tp", 1)

    memory_grad, grad = call(
        functools.partial(memory_grad_body, heads, tp, order), [(packed, bf16), (full, bf16)], [VM] * (len(order) + 3)
    )(*grads, query, gates, memory)
    bwd = scan(memory_grad, "seq")

    quarter = length // 4
    send, keep = call(
        functools.partial(output_keep_body, heads, tp, places[half:]),
        [((quarter, model), bf16), ((quarter, model), f32)],
        [VM] * 6,
        scratch=[pltpu.VMEM((length // 2, width), bf16)],
    )(query, memory, local_out, gates, out_weight, recv)
    bit = 2
    while 2 * bit < tp:
        total = keep + swap(send, "tp", bit).astype(f32)
        part = total.shape[0] // 2
        send, keep = total[:part].astype(bf16), total[part:]
        bit *= 2
    recv = swap(send, "tp", bit)
    output = call(output_done_body, [((length // tp, model), bf16)], [VM, VM], flops=1 << 20)(keep, recv)[0]

    cut = max(1, heads // 2)
    groups = [list(range(i, min(heads, i + cut))) for i in range(0, heads, cut)]
    grad_query = None
    locals_ = []
    for group in groups:
        part = (length, len(group) * HD)
        args = [query, keys, values, grad, memory, gates]
        specs = [VM] * 6
        alias = None
        if grad_query is not None:
            args.append(grad_query)
            specs.append(hbm)
            alias = {6: 0}
        grad_query, kl, vl = call(
            functools.partial(local_backward_body, heads, group, block),
            [(full, bf16), (part, f32), (part, f32)],
            specs,
            out_specs=[hbm, VM, VM],
            scratch=[pltpu.VMEM(part, bf16), pltpu.SemaphoreType.DMA((len(group),))],
            alias=alias,
        )(*args)
        locals_ += [kl, vl]
    grad_keys, grad_values = call(
        functools.partial(final_body, heads, groups, steps),
        [(full, bf16), (full, bf16)],
        [VM] * (2 + steps + len(locals_)),
        out_specs=[hbm, hbm],
        scratch=[pltpu.VMEM(full, bf16), pltpu.VMEM(full, bf16), pltpu.SemaphoreType.DMA((2, heads))],
    )(keys, values, *bwd, *locals_)
    return (output, grad_query, grad_keys, grad_values)


def solution(mesh):
    in_specs = (
        P("seq", "tp"),
        P("seq", "tp"),
        P("seq", "tp"),
        P("tp"),
        P("tp", None),
        P(("seq", "tp"), None),
    )
    out_specs = (P(("seq", "tp"), None), P("seq", "tp"), P("seq", "tp"), P("seq", "tp"))

    return jax.shard_map(local, mesh=mesh, in_specs=in_specs, out_specs=out_specs, check_vma=False)
```

time: 62.1 us -> 66.4 us (1.069)
  waiting for transfers between devices: 15.4 us -> 30 us
  other arithmetic: 6.08 us -> 0 us
  local copies, waits for them, and re-layouts: 5.19 us -> 0.01 us
  Pallas kernels: 17.9 us -> 19.3 us
    ppermute x11, waiting for transfers between devices: 15.4 us -> 30 us  [swap(): return lax.ppermute(x, axis, [(i, i ^ bit) for i in range(count)])]
    unnamed x32 -> x4, local copies, waits for them, and re-layouts: 4.27 us -> 0.01 us
    convert_element_type x5 -> x0, other arithmetic: 3.46 us -> none  [the longest x1 1.94 us: local(): output = total.astype(bf16)]
    add x3 -> x0, other arithmetic: 2.47 us -> none  [the longest x2 2.11 us: scan(): state = state + jnp.where(take, other, 0.0)]
    pallas_call x7 -> x15, Pallas kernels: 17.9 us -> 19.3 us  [the longest x2 6.56 us: local(): call(functools.partial(local_backward_body, heads, group, block), [(full,...]
    slice x1 -> x0, local copies, waits for them, and re-layouts: 0.92 us -> none  [local(): send, keep = (total[:half].astype(bf16), total[half:])]
  transfers between devices with their start and end apart: 11 -> 11, of which waited for: 7 -> 6; matrix products, arithmetic and copies ran while one was open for 7% -> 0% of each run, Pallas kernels for 28% -> 22%
where the time goes in v2:
time: 66.4 us; the launch traced here: 66.2 us
  waiting for transfers between devices  30 us (45%)
  Pallas kernels  19.3 us (29%)
  starting transfers between devices  16.1 us (24%)
  between operations  0.78 us (1%)
    ppermute x11, waiting for transfers between devices, swap(): return lax.ppermute(x, axis, [(i, i ^ bit) for i in range(count)])  30 us
    ppermute x11, starting transfers between devices, swap(): return lax.ppermute(x, axis, [(i, i ^ bit) for i in range(count)])  16.1 us
    pallas_call x2, Pallas kernels, local(): call(functools.partial(local_backward_body, heads, group, block), [(full,...  6.56 us
    pallas_call x1, Pallas kernels, local(): call(functools.partial(own_memory_body, heads), [(packed, bf16), (full, b...  2.47 us
    pallas_call x1, Pallas kernels, local(): call(functools.partial(local_forward_body, heads, block), [(full, f32)],...  2.22 us
    pallas_call x1, Pallas kernels, local(): call(functools.partial(final_body, heads, groups, steps), [(full, bf16),...  1.84 us
    pallas_call x2, Pallas kernels, local(): call(grad_mixed_body, [((rows, width), bf16)], [VM] * (len(masks) + 1))  1.48 us
    pallas_call x1, Pallas kernels, local(): call(functools.partial(memory_grad_body, heads, tp, order), [(packed, bf1...  1.33 us
  transfers between devices with their start and end apart: 11, of which 6 were waited for; matrix products, arithmetic and copies ran while one was open for 0% of the time, Pallas kernels for 22%

profile of v2, /device:TPU:0, one launch (start us, length us, event | category | flops | bytes accessed | tf_op | source)
XLA Modules:
  0.0 66.2 jit_solution(6036900498064459907)
XLA Ops:
  0.6 2.5 %shard_map.93 = (bf16[528,128]{1,0:T(8,128)(2,1)S(1)}, bf16[512,512]{1,0:T(8,128)(2,1)S(1)}, bf16[512,512]{1,0:T(8,128)(2,1)S(1)}, bf16[512,512]{1,0:T(8,128)(2,1)S(1)}, f32[8,128]{1,0:T(8,128)S(1)}) custom-call(bf16[512,512]{1,0:T(8,128)(2,1)} %k_hbm.1, bf16[512,512]{1,0:T(8,128)(2,1)} %v_hbm.1, bf16[512,512]{1,0:T(8,128)(2,1)} %q_hbm.1, f32[4]{0:T(128)} %beta_hbm.1), custom_call_target="tpu_custom_call" | custom-call | flops 268435456 | bytes 1048576 | tf_op jit(solution)/shard_map/pallas_call | solution.py:330
  3.1 3.0 %collective-permute-start = (bf16[528,128]{1,0:T(8,128)(2,1)S(1)}, bf16[528,128]{1,0:T(8,128)(2,1)S(1)}, u32[]{:S(2)}, u32[]{:S(2)}) collective-permute-start(bf16[528,128]{1,0:T(8,128)(2,1)S(1)} %get-tuple-element.27.refs_0_), channel_id=1, source_target_pairs={{0,4},{4,0},{8,12},{12,8},{16,20},{20,16},{24,28},{28,24},{1,5},{5... | collective-permute-start | bytes 405512 | tf_op jit(solution)/shard_map/ppermute | solution.py:293
  6.1 3.6 %collective-permute-done.refs_1_.refs_0_ = bf16[528,128]{1,0:T(8,128)(2,1)S(1)} collective-permute-done((bf16[528,128]{1,0:T(8,128)(2,1)S(1)}, bf16[528,128]{1,0:T(8,128)(2,1)S(1)}, u32[]{:S(2)}, u32[]{:S(2)}) %collective-permute-start) | collective-permute-done | bytes 135200 | tf_op jit(solution)/shard_map/ppermute | solution.py:293
  9.8 1.9 %collective-permute-start.1 = (bf16[528,128]{1,0:T(8,128)(2,1)S(1)}, bf16[528,128]{1,0:T(8,128)(2,1)S(1)}, u32[]{:S(2)}, u32[]{:S(2)}) collective-permute-start(bf16[528,128]{1,0:T(8,128)(2,1)S(1)} %shard_map.95), channel_id=1, source_target_pairs={{0,8},{4,12},{8,0},{12,4},{16,24},{20,28},{24,16},{28,20},{1,9},{5... | collective-permute-start | bytes 405512 | tf_op jit(solution)/shard_map/ppermute | solution.py:293
  11.7 3.2 %collective-permute-done.1.refs_2_.refs_1_ = bf16[528,128]{1,0:T(8,128)(2,1)S(1)} collective-permute-done((bf16[528,128]{1,0:T(8,128)(2,1)S(1)}, bf16[528,128]{1,0:T(8,128)(2,1)S(1)}, u32[]{:S(2)}, u32[]{:S(2)}) %collective-permute-start.1) | collective-permute-done | bytes 135200 | tf_op jit(solution)/shard_map/ppermute | solution.py:293
  14.9 2.9 %collective-permute-start.2 = (bf16[528,128]{1,0:T(8,128)(2,1)S(1)}, bf16[528,128]{1,0:T(8,128)(2,1)S(1)}, u32[]{:S(2)}, u32[]{:S(2)}) collective-permute-start(bf16[528,128]{1,0:T(8,128)(2,1)S(1)} %shard_map.96), channel_id=1, source_target_pairs={{0,16},{4,20},{8,24},{12,28},{16,0},{20,4},{24,8},{28,12},{1,17},{... | collective-permute-start | bytes 405512 | tf_op jit(solution)/shard_map/ppermute | solution.py:293
  17.8 2.2 %shard_map.94.lo_ref = f32[512,512]{1,0:T(8,128)S(1)} custom-call(bf16[512,512]{1,0:T(8,128)(2,1)S(1)} %get-tuple-element.23.q_ref.refs_2_, bf16[512,512]{1,0:T(8,128)(2,1)S(1)} %get-tuple-element.24.k_ref.refs_0_, bf16[512,512]{1,0:T(8,128)(2,1)S(1)} %get-tuple-element.25.v_ref.refs_1_), custom_call_target="tpu_custom_call" | custom-call | flops 268435456 | bytes 1048576 | tf_op jit(solution)/shard_map/pallas_call | solution.py:356
  20.0 2.3 %collective-permute-done.2.refs_2_ = bf16[528,128]{1,0:T(8,128)(2,1)S(1)} collective-permute-done((bf16[528,128]{1,0:T(8,128)(2,1)S(1)}, bf16[528,128]{1,0:T(8,128)(2,1)S(1)}, u32[]{:S(2)}, u32[]{:S(2)}) %collective-permute-start.2) | collective-permute-done | bytes 135200 | tf_op jit(solution)/shard_map/ppermute | solution.py:293
  22.4 1.2 %shard_map.97 = (f32[528,128]{1,0:T(8,128)S(1)}, bf16[256,2048]{1,0:T(8,128)(2,1)S(1)}) custom-call(bf16[512,512]{1,0:T(8,128)(2,1)S(1)} %get-tuple-element.23.q_ref.refs_2_, f32[512,512]{1,0:T(8,128)S(1)} %shard_map.94.lo_ref, f32[8,128]{1,0:T(8,128)S(1)} %get-tuple-element.26.gate_ref.refs_3_, bf16[512,2048]{1,0:T(8,128)(2,1)S(1)} %copy-done, ...), custom_call_target="tpu_custom_call" | custom-call | flops 268435456 | bytes 1048576 | tf_op jit(solution)/shard_map/pallas_call | solution.py:371
  23.6 1.8 %collective-permute-start.6 = (bf16[128,2048]{1,0:T(8,128)(2,1)S(1)}, bf16[128,2048]{1,0:T(8,128)(2,1)S(1)}, u32[]{:S(2)}, u32[]{:S(2)}) collective-permute-start(bf16[128,2048]{1,0:T(8,128)(2,1)S(1)} %copy-done.1), channel_id=1, source_target_pairs={{0,2},{1,3},{2,0},{3,1},{4,6},{5,7},{6,4},{7,5},{8,10},{9,11},{10,... | collective-permute-start | bytes 1572872 | tf_op jit(solution)/shard_map/ppermute | solution.py:293
  25.6 12.4 %collective-permute-done.6.refs_0_ = bf16[128,2048]{1,0:T(8,128)(2,1)S(1)} collective-permute-done((bf16[128,2048]{1,0:T(8,128)(2,1)S(1)}, bf16[128,2048]{1,0:T(8,128)(2,1)S(1)}, u32[]{:S(2)}, u32[]{:S(2)}) %collective-permute-start.6) | collective-permute-done | bytes 524320 | tf_op jit(solution)/shard_map/ppermute | solution.py:293
  38.0 1.1 %shard_map.98 = (bf16[128,2048]{1,0:T(8,128)(2,1)S(1)}, f32[128,2048]{1,0:T(8,128)S(1)}) custom-call(bf16[512,512]{1,0:T(8,128)(2,1)S(1)} %get-tuple-element.23.q_ref.refs_2_, f32[528,128]{1,0:T(8,128)S(1)} %get-tuple-element.28.mem_ref.refs_4_, f32[512,512]{1,0:T(8,128)S(1)} %shard_map.94.lo_ref, f32[8,128]{1,0:T(8,128)S(1)} %get-tuple-element.26.gate_ref.refs_3_, ...), custom_call_target="tpu_custom_call" | custom-call | flops 268435456 | bytes 1048576 | tf_op jit(solution)/shard_map/pallas_call | solution.py:385
  39.1 1.8 %collective-permute-start.4 = (bf16[128,2048]{1,0:T(8,128)(2,1)S(1)}, bf16[128,2048]{1,0:T(8,128)(2,1)S(1)}, u32[]{:S(2)}, u32[]{:S(2)}) collective-permute-start(bf16[128,2048]{1,0:T(8,128)(2,1)S(1)} %get-tuple-element.31), channel_id=1, source_target_pairs={{0,2},{1,3},{2,0},{3,1},{4,6},{5,7},{6,4},{7,5},{8,10},{9,11},{10,... | collective-permute-start | bytes 1572872 | tf_op jit(solution)/shard_map/ppermute | solution.py:293
  40.9 0.7 %shard_map.100.refs_0_ = bf16[256,512]{1,0:T(8,128)(2,1)S(1)} custom-call(bf16[128,2048]{1,0:T(8,128)(2,1)S(1)} %copy-done.1, bf16[128,2048]{1,0:T(8,128)(2,1)S(1)} %collective-permute-done.5.refs_1_, bf16[512,2048]{1,0:T(8,128)(2,1)S(1)} %copy-done), custom_call_target="tpu_custom_call" | custom-call | flops 268435456 | bytes 1048576 | tf_op jit(solution)/shard_map/pallas_call | solution.py:364
  41.6 0.7 %shard_map.101.refs_1_ = bf16[256,512]{1,0:T(8,128)(2,1)S(1)} custom-call(bf16[128,2048]{1,0:T(8,128)(2,1)S(1)} %collective-permute-done.6.refs_0_, bf16[128,2048]{1,0:T(8,128)(2,1)S(1)} %collective-permute-done.7.refs_1_, bf16[512,2048]{1,0:T(8,128)(2,1)S(1)} %copy-done), custom_call_target="tpu_custom_call" | custom-call | flops 268435456 | bytes 1048576 | tf_op jit(solution)/shard_map/pallas_call | solution.py:364
  42.4 1.3 %shard_map.102 = (bf16[528,128]{1,0:T(8,128)(2,1)S(1)}, bf16[512,512]{1,0:T(8,128)(2,1)S(1)}) custom-call(bf16[256,512]{1,0:T(8,128)(2,1)S(1)} %shard_map.100.refs_0_, bf16[256,512]{1,0:T(8,128)(2,1)S(1)} %shard_map.101.refs_1_, bf16[512,512]{1,0:T(8,128)(2,1)S(1)} %get-tuple-element.23.q_ref.refs_2_, f32[8,128]{1,0:T(8,128)S(1)} %get-tuple-element.26.gate_ref.refs_3_, ...), custom_call_target="tpu_custom_call" | custom-call | flops 268435456 | bytes 1048576 | tf_op jit(solution)/shard_map/pallas_call | solution.py:379
  43.7 1.5 %collective-permute-start.8 = (bf16[528,128]{1,0:T(8,128)(2,1)S(1)}, bf16[528,128]{1,0:T(8,128)(2,1)S(1)}, u32[]{:S(2)}, u32[]{:S(2)}) collective-permute-start(bf16[528,128]{1,0:T(8,128)(2,1)S(1)} %get-tuple-element.35.refs_0_), channel_id=1, source_target_pairs={{0,4},{4,0},{8,12},{12,8},{16,20},{20,16},{24,28},{28,24},{1,5},{5... | collective-permute-start | bytes 405512 | tf_op jit(solution)/shard_map/ppermute | solution.py:293
  45.3 4.2 %collective-permute-done.8.refs_1_.refs_2_ = bf16[528,128]{1,0:T(8,128)(2,1)S(1)} collective-permute-done((bf16[528,128]{1,0:T(8,128)(2,1)S(1)}, bf16[528,128]{1,0:T(8,128)(2,1)S(1)}, u32[]{:S(2)}, u32[]{:S(2)}) %collective-permute-start.8) | collective-permute-done | bytes 135200 | tf_op jit(solution)/shard_map/ppermute | solution.py:293
  50.3 4.3 %collective-permute-done.9.refs_2_.refs_3_ = bf16[528,128]{1,0:T(8,128)(2,1)S(1)} collective-permute-done((bf16[528,128]{1,0:T(8,128)(2,1)S(1)}, bf16[528,128]{1,0:T(8,128)(2,1)S(1)}, u32[]{:S(2)}, u32[]{:S(2)}) %collective-permute-start.9) | collective-permute-done | bytes 135200 | tf_op jit(solution)/shard_map/ppermute | solution.py:293
  54.7 2.2 %collective-permute-start.10 = (bf16[528,128]{1,0:T(8,128)(2,1)S(1)}, bf16[528,128]{1,0:T(8,128)(2,1)S(1)}, u32[]{:S(2)}, u32[]{:S(2)}) collective-permute-start(bf16[528,128]{1,0:T(8,128)(2,1)S(1)} %shard_map.106), channel_id=1, source_target_pairs={{0,16},{4,20},{8,24},{12,28},{16,0},{20,4},{24,8},{28,12},{1,17},{... | collective-permute-start | bytes 405512 | tf_op jit(solution)/shard_map/ppermute | solution.py:293
  56.9 3.3 %shard_map.103 = (bf16[512,512]{1,0:T(8,128)(2,1)}, f32[512,256]{1,0:T(8,128)S(1)}, f32[512,256]{1,0:T(8,128)S(1)}) custom-call(bf16[512,512]{1,0:T(8,128)(2,1)S(1)} %get-tuple-element.23.q_ref.refs_2_, bf16[512,512]{1,0:T(8,128)(2,1)S(1)} %get-tuple-element.24.k_ref.refs_0_, bf16[512,512]{1,0:T(8,128)(2,1)S(1)} %get-tuple-element.25.v_ref.refs_1_, ...), custom_call_target="tpu_custom_call" | custom-call | flops 268435456 | bytes 1048576 | tf_op jit(solution)/shard_map/pallas_call | solution.py:413
  60.2 3.3 %shard_map.104 = (bf16[512,512]{1,0:T(8,128)(2,1)}, f32[512,256]{1,0:T(8,128)S(1)}, f32[512,256]{1,0:T(8,128)S(1)}) custom-call(bf16[512,512]{1,0:T(8,128)(2,1)S(1)} %get-tuple-element.23.q_ref.refs_2_, bf16[512,512]{1,0:T(8,128)(2,1)S(1)} %get-tuple-element.24.k_ref.refs_0_, ...), custom_call_target="tpu_custom_call", output_to_operand_aliasing={{0}: (6, {})} | custom-call | flops 268435456 | bytes 1048576 | tf_op jit(solution)/shard_map/pallas_call | solution.py:413
  63.5 1.8 %shard_map.107 = (bf16[512,512]{1,0:T(8,128)(2,1)}, bf16[512,512]{1,0:T(8,128)(2,1)}) custom-call(bf16[512,512]{1,0:T(8,128)(2,1)S(1)} %get-tuple-element.24.k_ref.refs_0_, bf16[512,512]{1,0:T(8,128)(2,1)S(1)} %get-tuple-element.25.v_ref.refs_1_, bf16[528,128]{1,0:T(8,128)(2,1)S(1)} %collective-permute-done.8.refs_1_.refs_2_, ...), custom_call_target="tpu_custom_call" | custom-call | flops 268435456 | bytes 1048576 | tf_op jit(solution)/shard_map/pallas_call | solution.py:422
  65.3 0.9 %shard_map.99 = bf16[128,2048]{1,0:T(8,128)(2,1)} custom-call(f32[128,2048]{1,0:T(8,128)S(1)} %get-tuple-element.30.keep_ref, bf16[128,2048]{1,0:T(8,128)(2,1)S(1)} %collective-permute-done.4.recv_ref), custom_call_target="tpu_custom_call" | custom-call | flops 1048576 | bytes 1048576 | tf_op jit(solution)/shard_map/pallas_call | solution.py:398
  (17 shorter events, 1.2 us)
Async XLA Ops:
  3.1 19.3 %copy-start = (bf16[512,2048]{1,0:T(8,128)(2,1)S(1)}, bf16[512,2048]{1,0:T(8,128)(2,1)}, u32[]{:S(2)}) copy-start(bf16[512,2048]{1,0:T(8,128)(2,1)} %refs_2_.3) | copy-start | bytes 6291460
  3.1 6.6 %collective-permute-start = (bf16[528,128]{1,0:T(8,128)(2,1)S(1)}, bf16[528,128]{1,0:T(8,128)(2,1)S(1)}, u32[]{:S(2)}, u32[]{:S(2)}) collective-permute-start(bf16[528,128]{1,0:T(8,128)(2,1)S(1)} %get-tuple-element.27.refs_0_), channel_id=1, source_target_pairs={{0,4},{4,0},{8,12},{12,8},{16,20},{20,16},{24,28},{28,24},{1,5},{5... | collective-permute-start | bytes 405512 | tf_op jit(solution)/shard_map/ppermute | solution.py:293
  9.8 5.1 %collective-permute-start.1 = (bf16[528,128]{1,0:T(8,128)(2,1)S(1)}, bf16[528,128]{1,0:T(8,128)(2,1)S(1)}, u32[]{:S(2)}, u32[]{:S(2)}) collective-permute-start(bf16[528,128]{1,0:T(8,128)(2,1)S(1)} %shard_map.95), channel_id=1, source_target_pairs={{0,8},{4,12},{8,0},{12,4},{16,24},{20,28},{24,16},{28,20},{1,9},{5... | collective-permute-start | bytes 405512 | tf_op jit(solution)/shard_map/ppermute | solution.py:293
  14.9 7.5 %collective-permute-start.2 = (bf16[528,128]{1,0:T(8,128)(2,1)S(1)}, bf16[528,128]{1,0:T(8,128)(2,1)S(1)}, u32[]{:S(2)}, u32[]{:S(2)}) collective-permute-start(bf16[528,128]{1,0:T(8,128)(2,1)S(1)} %shard_map.96), channel_id=1, source_target_pairs={{0,16},{4,20},{8,24},{12,28},{16,0},{20,4},{24,8},{28,12},{1,17},{... | collective-permute-start | bytes 405512 | tf_op jit(solution)/shard_map/ppermute | solution.py:293
  20.0 3.6 %copy-start.1 = (bf16[128,2048]{1,0:T(8,128)(2,1)S(1)}, bf16[128,2048]{1,0:T(8,128)(2,1)}, u32[]{:S(2)}) copy-start(bf16[128,2048]{1,0:T(8,128)(2,1)} %refs_0_.1) | copy-start | bytes 1572868
  23.6 14.4 %collective-permute-start.3 = (bf16[256,2048]{1,0:T(8,128)(2,1)S(1)}, bf16[256,2048]{1,0:T(8,128)(2,1)S(1)}, u32[]{:S(2)}, u32[]{:S(2)}) collective-permute-start(bf16[256,2048]{1,0:T(8,128)(2,1)S(1)} %get-tuple-element.29), channel_id=1, source_target_pairs={{0,1},{1,0},{2,3},{3,2},{4,5},{5,4},{6,7},{7,6},{8,9},{9,8},{10,11... | collective-permute-start | bytes 3145736 | tf_op jit(solution)/shard_map/ppermute | solution.py:293
  23.6 14.3 %collective-permute-start.6 = (bf16[128,2048]{1,0:T(8,128)(2,1)S(1)}, bf16[128,2048]{1,0:T(8,128)(2,1)S(1)}, u32[]{:S(2)}, u32[]{:S(2)}) collective-permute-start(bf16[128,2048]{1,0:T(8,128)(2,1)S(1)} %copy-done.1), channel_id=1, source_target_pairs={{0,2},{1,3},{2,0},{3,1},{4,6},{5,7},{6,4},{7,5},{8,10},{9,11},{10,... | collective-permute-start | bytes 1572872 | tf_op jit(solution)/shard_map/ppermute | solution.py:293
  25.5 15.4 %collective-permute-start.5 = (bf16[128,2048]{1,0:T(8,128)(2,1)S(1)}, bf16[128,2048]{1,0:T(8,128)(2,1)S(1)}, u32[]{:S(2)}, u32[]{:S(2)}) collective-permute-start(bf16[128,2048]{1,0:T(8,128)(2,1)S(1)} %copy-done.1), channel_id=1, source_target_pairs={{0,1},{1,0},{2,3},{3,2},{4,5},{5,4},{6,7},{7,6},{8,9},{9,8},{10,11... | collective-permute-start | bytes 1572872 | tf_op jit(solution)/shard_map/ppermute | solution.py:293
  38.0 3.7 %collective-permute-start.7 = (bf16[128,2048]{1,0:T(8,128)(2,1)S(1)}, bf16[128,2048]{1,0:T(8,128)(2,1)S(1)}, u32[]{:S(2)}, u32[]{:S(2)}) collective-permute-start(bf16[128,2048]{1,0:T(8,128)(2,1)S(1)} %collective-permute-done.6.refs_0_), channel_id=1, source_target_pairs={{0,1},{1,0},{2,3},{3,2},{4,5},{5,4},{6,7},{7,6},{8,9},{9,8},{10,11... | collective-permute-start | bytes 1572872 | tf_op jit(solution)/shard_map/ppermute | solution.py:293
  39.1 26.2 %collective-permute-start.4 = (bf16[128,2048]{1,0:T(8,128)(2,1)S(1)}, bf16[128,2048]{1,0:T(8,128)(2,1)S(1)}, u32[]{:S(2)}, u32[]{:S(2)}) collective-permute-start(bf16[128,2048]{1,0:T(8,128)(2,1)S(1)} %get-tuple-element.31), channel_id=1, source_target_pairs={{0,2},{1,3},{2,0},{3,1},{4,6},{5,7},{6,4},{7,5},{8,10},{9,11},{10,... | collective-permute-start | bytes 1572872 | tf_op jit(solution)/shard_map/ppermute | solution.py:293
  43.7 5.8 %collective-permute-start.8 = (bf16[528,128]{1,0:T(8,128)(2,1)S(1)}, bf16[528,128]{1,0:T(8,128)(2,1)S(1)}, u32[]{:S(2)}, u32[]{:S(2)}) collective-permute-start(bf16[528,128]{1,0:T(8,128)(2,1)S(1)} %get-tuple-element.35.refs_0_), channel_id=1, source_target_pairs={{0,4},{4,0},{8,12},{12,8},{16,20},{20,16},{24,28},{28,24},{1,5},{5... | collective-permute-start | bytes 405512 | tf_op jit(solution)/shard_map/ppermute | solution.py:293
  49.5 5.1 %collective-permute-start.9 = (bf16[528,128]{1,0:T(8,128)(2,1)S(1)}, bf16[528,128]{1,0:T(8,128)(2,1)S(1)}, u32[]{:S(2)}, u32[]{:S(2)}) collective-permute-start(bf16[528,128]{1,0:T(8,128)(2,1)S(1)} %shard_map.105), channel_id=1, source_target_pairs={{0,8},{4,12},{8,0},{12,4},{16,24},{20,28},{24,16},{28,20},{1,9},{5... | collective-permute-start | bytes 405512 | tf_op jit(solution)/shard_map/ppermute | solution.py:293
  54.7 8.8 %collective-permute-start.10 = (bf16[528,128]{1,0:T(8,128)(2,1)S(1)}, bf16[528,128]{1,0:T(8,128)(2,1)S(1)}, u32[]{:S(2)}, u32[]{:S(2)}) collective-permute-start(bf16[528,128]{1,0:T(8,128)(2,1)S(1)} %shard_map.106), channel_id=1, source_target_pairs={{0,16},{4,20},{8,24},{12,28},{16,0},{20,4},{24,8},{28,12},{1,17},{... | collective-permute-start | bytes 405512 | tf_op jit(solution)/shard_map/ppermute | solution.py:293

commit v3 on v2

v3 whole, which is shorter than its diff:
```python
import functools

import jax
import jax.numpy as jnp
from jax import lax
from jax.experimental import pallas as pl
from jax.experimental.pallas import tpu as pltpu
from jax.sharding import PartitionSpec as P


HD = 128
PAD = 16
SCALE = HD ** (-0.5)

f32 = jnp.float32
bf16 = jnp.bfloat16

VM = pl.BlockSpec(memory_space=pltpu.VMEM)


def dot(a, b, ca, cb):
    return lax.dot_general(a, b, (((ca,), (cb,)), ((), ())), preferred_element_type=f32)


def split(x):
    hi = x.astype(bf16)
    return hi, (x - hi.astype(f32)).astype(bf16)


def side(a, b):
    return jnp.concatenate([a, b], 1)


def halves(y):
    return y[:, : y.shape[1] // 2] + y[:, y.shape[1] // 2 :]


def twofold(x, m, transposed=False):
    mh, ml = split(m)
    both = jnp.concatenate([mh, ml], 0) if transposed else side(mh, ml)
    if transposed:
        return halves(dot(side(*split(x)), side(both, both), 1, 1))
    return halves(dot(side(*split(x)), jnp.concatenate([both, both], 0), 1, 0))


def feat(x):
    return jnp.where(x > 0, x + 1.0, jnp.exp(jnp.minimum(x, 0.0)))


def slope(x):
    return jnp.where(x > 0, 1.0, jnp.exp(jnp.minimum(x, 0.0)))


def cols(h):
    return slice(h * HD, (h + 1) * HD)


def call(body, outs, specs, out_specs=None, scratch=(), flops=1 << 28, vmem=24, alias=None):
    if out_specs is None:
        out_specs = [VM] * len(outs)
    return pl.pallas_call(
        body,
        out_shape=[jax.ShapeDtypeStruct(s, d) for s, d in outs],
        in_specs=specs,
        out_specs=out_specs,
        scratch_shapes=list(scratch),
        input_output_aliases=alias or {},
        compiler_params=pltpu.CompilerParams(vmem_limit_bytes=vmem << 20),
        cost_estimate=pl.CostEstimate(flops=flops, transcendentals=0, bytes_accessed=1 << 20),
    )


def pad_rows(rows):
    return jnp.concatenate(rows + [jnp.zeros((PAD - len(rows), HD), f32)], 0).astype(bf16)


def rows_of(h):
    return slice(PAD + h * HD, PAD + (h + 1) * HD)


def memory_of(mem_ref, h):
    return mem_ref[rows_of(h), :], mem_ref[h : h + 1, :]


def own_memory_body(heads, k_hbm, v_hbm, o_ref, k_ref, v_ref, sems):
    part = k_ref.shape[0] // heads
    blocks = [slice(i * part, (i + 1) * part) for i in range(heads)]
    copies = [
        [pltpu.make_async_copy(a.at[rows], b.at[rows], sems.at[i, n]) for i, (a, b) in enumerate(((k_hbm, k_ref), (v_hbm, v_ref)))]
        for n, rows in enumerate(blocks)
    ]
    for pair in copies:
        for copy in pair:
            copy.start()
    both = [None] * heads
    sums = [None] * heads
    for rows, pair in zip(blocks, copies):
        for copy in pair:
            copy.wait()
        for h in range(heads):
            kf = feat(k_ref[rows, cols(h)].astype(f32))
            x = dot(side(*split(kf)), v_ref[rows, cols(h)], 0, 0)
            y = jnp.sum(kf, 0, keepdims=True)
            both[h] = x if both[h] is None else both[h] + x
            sums[h] = y if sums[h] is None else sums[h] + y
    for h in range(heads):
        o_ref[rows_of(h), :] = (both[h][:HD] + both[h][HD:]).astype(bf16)
    o_ref[:PAD, :] = pad_rows(sums)


def load_query_body(heads, q_hbm, beta_hbm, q_ref, qt_ref, gate_ref, beta_ref, sems):
    rows = q_ref.shape[0] // heads
    beta_copy = pltpu.make_async_copy(beta_hbm, beta_ref, sems.at[heads])
    beta_copy.start()
    parts = [pl.ds(i * rows, rows) for i in range(heads)]
    copies = [pltpu.make_async_copy(q_hbm.at[p], q_ref.at[p], sems.at[i]) for i, p in enumerate(parts)]
    for copy in copies:
        copy.start()
    beta_copy.wait()
    for h in range(heads):
        gate_ref[h : h + 1, :] = jax.nn.sigmoid(jnp.full((1, HD), beta_ref[h], f32))
    for copy in copies:
        copy.wait()
    for h in range(heads):
        both = side(*split(feat(q_ref[:, cols(h)].astype(f32))))
        qt_ref[2 * h * HD : 2 * (h + 1) * HD, :] = both.T


def add_body(count, *refs):
    total = refs[0][...].astype(f32)
    for ref in refs[1:count]:
        total = total + ref[...].astype(f32)
    start = 0
    for out in refs[count:]:
        out[...] = total[start : start + out.shape[0]].astype(bf16)
        start += out.shape[0]


def scan_state(backward, refs, rows):
    place = lax.axis_index("seq")
    cut = refs[-2].shape[0] if refs[-1] is not None else None
    state = None
    for i, ref in enumerate(refs[:-1]):
        upper = (place // (1 << i)) % 2
        take = (1 - upper if backward else upper).astype(f32)
        part = rows
        if i == len(refs) - 2 and cut is not None and rows.start >= cut:
            ref, part = refs[-1], slice(rows.start - cut, rows.stop - cut)
        x = ref[part, :].astype(f32) * take
        state = x if state is None else state + x
    return state


def read_memory(qf, matrix, msum):
    numer = twofold(qf, matrix)
    r = 1.0 / (jnp.sum(qf * msum, 1, keepdims=True) + 1.0)
    return numer * r, r


def probs_parts(q_ref, k_ref, h, j, block):
    q = q_ref[j * block : (j + 1) * block, cols(h)]
    parts = []
    for i in range(j + 1):
        k = k_ref[i * block : (i + 1) * block, cols(h)]
        s = dot(k, q, 1, 1) * SCALE
        if i == j:
            shape = (block, block)
            keep = lax.broadcasted_iota(jnp.int32, shape, 0) <= lax.broadcasted_iota(jnp.int32, shape, 1)
            s = jnp.where(keep, s, -jnp.inf)
        parts.append(s)
    top = functools.reduce(jnp.maximum, [jnp.max(s, 0, keepdims=True) for s in parts])
    parts = [jnp.exp(s - top) for s in parts]
    r = 1.0 / sum(jnp.sum(e, 0, keepdims=True) for e in parts)
    return q, [e * r for e in parts]


def local_forward_body(heads, block, q_ref, k_ref, v_ref, o_ref):
    for h in range(heads):
        vt = v_ref[:, cols(h)].T
        for j in range(q_ref.shape[0] // block):
            _, parts = probs_parts(q_ref, k_ref, h, j, block)
            acc = sum(
                dot(vt[:, i * block : (i + 1) * block], p.astype(bf16), 1, 0) for i, p in enumerate(parts)
            )
            o_ref[j * block : (j + 1) * block, cols(h)] = acc.T


def grad_mixed_body(*refs):
    pieces, w_ref, o_ref = refs[:-2], refs[-2], refs[-1]
    x = jnp.concatenate([p[...] for p in pieces], 0)
    o_ref[...] = dot(x, w_ref[...], 1, 1).astype(bf16)


def gather_grad(count, order, grads, g_ref):
    place = lax.axis_index("tp")
    for grad, masks in zip(grads, order):
        rows = grad.shape[0] // len(masks)
        for i, m in enumerate(masks):
            spot = pl.multiple_of(flipped(place, m, count) * rows, rows)
            g_ref[pl.ds(spot, rows), :] = grad[i * rows : (i + 1) * rows, :]


def segment_memory_grad(h, q_ref, qt_ref, g_ref, gate_ref, matrix, msum):
    qf = feat(q_ref[:, cols(h)].astype(f32))
    mem_out, r = read_memory(qf, matrix, msum)
    gmem = gate_ref[h : h + 1, :] * g_ref[:, cols(h)].astype(f32)
    gden = -jnp.sum(gmem * mem_out, 1, keepdims=True) * r
    both = halves(dot(qt_ref[2 * h * HD : 2 * (h + 1) * HD, :], side(*split(gmem * r)), 1, 0))
    return (both[:HD] + both[HD:]).astype(bf16), jnp.sum(gden * qf, 0, keepdims=True)


def memory_grad_first_body(group, count, order, steps, *refs):
    grads, (q_ref, qt_ref, gate_ref) = refs[: len(order)], refs[len(order) : len(order) + 3]
    recvs = refs[len(order) + 3 : len(order) + 3 + steps] + (None,)
    o_ref, g_ref = refs[-2:]
    gather_grad(count, order, grads, g_ref)
    sums = scan_state(False, recvs, slice(0, PAD))
    rows = []
    for h in group:
        matrix = scan_state(False, recvs, rows_of(h))
        o_ref[rows_of(h), :], row = segment_memory_grad(h, q_ref, qt_ref, g_ref, gate_ref, matrix, sums[h : h + 1, :])
        rows.append(row)
    o_ref[:PAD, :] = jnp.concatenate(rows + [jnp.zeros((PAD - len(rows), HD), f32)], 0).astype(bf16)


def memory_grad_second_body(first, group, first_ref, q_ref, qt_ref, gate_ref, g_ref, mem_ref, o_ref):
    cut = first_ref.shape[0]
    o_ref[:cut, :] = first_ref[...]
    rows = []
    for h in group:
        o_ref[rows_of(h), :], row = segment_memory_grad(h, q_ref, qt_ref, g_ref, gate_ref, *memory_of(mem_ref, h))
        rows.append(row)
    head = first_ref[:PAD, :].astype(f32)
    tail = [jnp.zeros((PAD - first - len(rows), HD), f32)]
    o_ref[:PAD, :] = jnp.concatenate([head[:first]] + rows + tail, 0).astype(bf16)


def flipped(place, mask, count):
    out = 0
    bit = 1
    while bit < count:
        own = (place // bit) % 2
        out = out + bit * ((1 - own) if mask & bit else own)
        bit *= 2
    return out


def mixed_rows(heads, count, masks, q_ref, mem_ref, lo_ref, gate_ref, mix_ref):
    place = lax.axis_index("tp")
    rows = q_ref.shape[0] // count
    for i, m in enumerate(masks):
        spot = pl.multiple_of(flipped(place, m, count) * rows, rows)
        for h in range(heads):
            qf = feat(q_ref[pl.ds(spot, rows), cols(h)].astype(f32))
            mem_out = read_memory(qf, *memory_of(mem_ref, h))[0]
            g = gate_ref[h : h + 1, :]
            x = g * mem_out + (1.0 - g) * lo_ref[pl.ds(spot, rows), cols(h)]
            mix_ref[i * rows : (i + 1) * rows, cols(h)] = x.astype(bf16)


def output_send_body(heads, count, masks, steps, q_ref, lo_ref, gate_ref, w_ref, *refs):
    recvs, (mem_ref, send_ref, mix_ref) = refs[:steps], refs[steps:]
    cut = recvs[-2].shape[0]
    for rows in (slice(0, cut), slice(cut, mem_ref.shape[0])):
        mem_ref[rows, :] = scan_state(False, recvs, rows)
    mixed_rows(heads, count, masks, q_ref, mem_ref, lo_ref, gate_ref, mix_ref)
    send_ref[...] = dot(mix_ref[...], w_ref[...], 1, 0).astype(bf16)


def output_keep_body(heads, count, masks, q_ref, mem_ref, lo_ref, gate_ref, w_ref, recv_ref, send_ref, keep_ref, mix_ref):
    mixed_rows(heads, count, masks, q_ref, mem_ref, lo_ref, gate_ref, mix_ref)
    total = dot(mix_ref[...], w_ref[...], 1, 0) + recv_ref[...].astype(f32)
    half = send_ref.shape[0]
    send_ref[...] = total[:half].astype(bf16)
    keep_ref[...] = total[half:]


def output_done_body(keep_ref, recv_ref, o_ref):
    o_ref[...] = (keep_ref[...] + recv_ref[...].astype(f32)).astype(bf16)


def local_backward_body(group, block, q_ref, k_ref, v_ref, g_ref, mem_ref, gate_ref, *refs):
    gq_ref, gk_ref, gv_ref = refs
    blocks = q_ref.shape[0] // block
    for n, h in enumerate(group):
        g = gate_ref[h : h + 1, :]
        kt = k_ref[:, cols(h)].T
        gk = [None] * blocks
        gv = [None] * blocks

        def add(acc, i, x):
            acc[i] = x if acc[i] is None else acc[i] + x

        gq = []
        for j in range(blocks):
            q, parts = probs_parts(q_ref, k_ref, h, j, block)
            gl = ((1.0 - g) * g_ref[j * block : (j + 1) * block, cols(h)].astype(f32)).astype(bf16)
            gps = [dot(v_ref[i * block : (i + 1) * block, cols(h)], gl, 1, 1) for i in range(j + 1)]
            delta = sum(jnp.sum(p * gp, 0, keepdims=True) for p, gp in zip(parts, gps))
            acc = None
            for i, (p, gp) in enumerate(zip(parts, gps)):
                gs = (p * (gp - delta) * SCALE).astype(bf16)
                add(gk, i, dot(gs, q, 1, 0))
                add(gv, i, dot(p.astype(bf16), gl, 1, 0))
                t = dot(kt[:, i * block : (i + 1) * block], gs, 1, 0)
                acc = t if acc is None else acc + t
            gq.append(acc.T)
        for i in range(blocks):
            gk_ref[i * block : (i + 1) * block, cols(n)] = gk[i]
            gv_ref[i * block : (i + 1) * block, cols(n)] = gv[i]
        qx = q_ref[:, cols(h)].astype(f32)
        qf = feat(qx)
        matrix, msum = memory_of(mem_ref, h)
        mem_out, r = read_memory(qf, matrix, msum)
        gmem = g * g_ref[:, cols(h)].astype(f32)
        gden = -jnp.sum(gmem * mem_out, 1, keepdims=True) * r
        gqf = twofold(gmem * r, matrix, True) + gden * msum
        gq_ref[:, cols(n)] = (jnp.concatenate(gq, 0) + gqf * slope(qx)).astype(bf16)


def final_body(group, moves, steps, *refs):
    k_ref, v_ref, kl_ref, vl_ref = refs[:4]
    recvs = refs[4 : 4 + steps]
    if group[0] == 0:
        recvs = recvs + (None,)
    gqs = refs[4 + steps : 4 + steps + len(moves)]
    gq_hbm, gk_hbm, gv_hbm, gk_ref, gv_ref, sems, gq_sems = refs[-7:]
    copies = []
    for n, (ref, spots) in enumerate(zip(gqs, moves)):
        copies.append(pltpu.make_async_copy(ref, gq_hbm.at[:, spots], gq_sems.at[n]))
        copies[-1].start()
    for i, h in enumerate(group):
        kx = k_ref[:, cols(h)].astype(f32)
        matrix = scan_state(True, recvs, rows_of(h))
        msum = scan_state(True, recvs, slice(0, PAD))[h : h + 1, :]
        gkf = halves(dot(v_ref[:, cols(h)], jnp.concatenate(split(matrix), 0), 1, 1)) + msum
        gk_ref[:, cols(i)] = (kl_ref[:, cols(i)] + gkf * slope(kx)).astype(bf16)
        copies.append(pltpu.make_async_copy(gk_ref.at[:, cols(i)], gk_hbm.at[:, cols(h)], sems.at[0, i]))
        copies[-1].start()
        gv_ref[:, cols(i)] = (vl_ref[:, cols(i)] + twofold(feat(kx), matrix)).astype(bf16)
        copies.append(pltpu.make_async_copy(gv_ref.at[:, cols(i)], gv_hbm.at[:, cols(h)], sems.at[1, i]))
        copies[-1].start()
    for copy in copies:
        copy.wait()


def swap(x, axis, bit):
    count = lax.axis_size(axis)
    return lax.ppermute(x, axis, [(i, i ^ bit) for i in range(count)])


def scan(own, axis, cut):
    count = lax.axis_size(axis)
    recvs = []
    bit = 1
    while bit < count:
        have = [own] + recvs
        shapes = [own.shape]
        ends = bit * 2 == count
        if ends:
            shapes = [(cut, HD), (own.shape[0] - cut, HD)]
        sends = [own]
        if len(have) > 1 or ends:
            body = functools.partial(add_body, len(have))
            outs = [(shape, bf16) for shape in shapes]
            sends = call(body, outs, [VM] * len(have), flops=1 << 20)(*have)
        for send in sends:
            recvs.append(swap(send, axis, bit))
        bit *= 2
    return recvs


def reverse_bits(value, count):
    out = 0
    bit = 1
    while bit < count:
        out = out * 2 + (1 if value & bit else 0)
        bit *= 2
    return out


def local(query, keys, values, beta, out_weight, cotangent):
    length, width = query.shape
    heads = width // HD
    model = out_weight.shape[1]
    tp = lax.axis_size("tp")
    block = min(256, length)
    packed = (heads * HD + PAD, HD)
    hbm = pl.BlockSpec(memory_space=pltpu.HBM)
    full = (length, width)
    first = -(-heads // 2)
    groups = [list(range(first)), list(range(first, heads))]
    cut = PAD + first * HD

    def in_hbm(*xs):
        return [pltpu.with_memory_space_constraint(x, pltpu.HBM) for x in xs]

    own, keys, values = call(
        functools.partial(own_memory_body, heads),
        [(packed, bf16), (full, bf16), (full, bf16)],
        [hbm] * 2,
        scratch=[pltpu.SemaphoreType.DMA((2, heads))],
    )(*in_hbm(keys, values))
    query, query_t, gates = call(
        functools.partial(load_query_body, heads),
        [(full, bf16), ((2 * width, length), bf16), ((-(-heads // 8) * 8, HD), f32)],
        [hbm] * 2,
        scratch=[pltpu.SMEM((heads,), f32), pltpu.SemaphoreType.DMA((heads + 1,))],
        flops=1 << 16,
    )(*in_hbm(query, beta))
    fwd = scan(own, "seq", cut)

    held = {0: cotangent}
    near, later = [0], []
    if tp > 1:
        held[1] = swap(cotangent, "tp", 1)
        near = [0, 1]
    bit = 2
    far = [0]
    while bit < tp:
        for m in list(far):
            held[m | bit] = swap(held[m], "tp", bit)
            far.append(m | bit)
        bit *= 2
    for m in far[1:]:
        held[m | 1] = swap(held[m], "tp", 1)
        later += [m, m | 1]
    order = [near] + ([later] if later else [])

    local_out = call(
        functools.partial(local_forward_body, heads, block), [(full, f32)], [VM, VM, VM]
    )(query, keys, values)[0]

    grads = []
    for masks in order:
        rows = cotangent.shape[0] * len(masks)
        grads.append(
            call(
                grad_mixed_body, [((rows, width), bf16)], [VM] * (len(masks) + 1)
            )(*[held[m] for m in masks], out_weight)[0]
        )

    places = [reverse_bits(tp - 1 - i, tp) for i in range(tp)]
    half = tp // 2
    steps = len(fwd)
    part, grad = call(
        functools.partial(memory_grad_first_body, groups[0], tp, order, steps - 1),
        [((cut, HD), bf16), (full, bf16)],
        [VM] * (len(order) + 2 + steps),
    )(*grads, query, query_t, gates, *fwd[:-1])
    memory, send = call(
        functools.partial(output_send_body, heads, tp, places[:half], steps),
        [(packed, f32), ((length // 2, model), bf16)],
        [VM] * (4 + steps),
        scratch=[pltpu.VMEM((length // 2, width), bf16)],
    )(query, local_out, gates, out_weight, *fwd)
    recv = swap(send, "tp", 1)
    memory_grad = call(
        functools.partial(memory_grad_second_body, first, groups[1]), [(packed, bf16)], [VM] * 6
    )(part, query, query_t, gates, grad, memory)[0]
    bwd = scan(memory_grad, "seq", cut)

    quarter = length // 4
    send, keep = call(
        functools.partial(output_keep_body, heads, tp, places[half:]),
        [((quarter, model), bf16), ((quarter, model), f32)],
        [VM] * 6,
        scratch=[pltpu.VMEM((length // 2, width), bf16)],
    )(query, memory, local_out, gates, out_weight, recv)
    bit = 2
    while 2 * bit < tp:
        total = keep + swap(send, "tp", bit).astype(f32)
        part = total.shape[0] // 2
        send, keep = total[:part].astype(bf16), total[part:]
        bit *= 2
    recv = swap(send, "tp", bit)
    output = call(
        output_done_body, [((length // tp, model), bf16)], [VM, VM], flops=1 << 20
    )(keep, recv)[0]

    pieces = []
    for group in groups:
        part = (length, len(group) * HD)
        pieces.append(
            call(
                functools.partial(local_backward_body, group, block),
                [(part, bf16), (part, f32), (part, f32)],
                [VM] * 6,
            )(query, keys, values, grad, memory, gates)
        )
    grads_out = None
    for n, group in enumerate(groups):
        recvs = bwd[:-1] if n == 0 else bwd
        args = [keys, values, *pieces[n][1:], *recvs]
        specs = [VM] * len(args)
        moves, alias = [], None
        if n == 0:
            args += [piece[0] for piece in pieces]
            specs += [VM] * len(pieces)
            moves = [slice(g[0] * HD, (g[-1] + 1) * HD) for g in groups]
        else:
            alias = {len(args) + i: i for i in range(3)}
            args += grads_out
            specs += [hbm] * 3
        part = (length, len(group) * HD)
        grads_out = call(
            functools.partial(final_body, group, moves, len(recvs)),
            [(full, bf16)] * 3,
            specs,
            out_specs=[hbm] * 3,
            scratch=[
                pltpu.VMEM(part, bf16),
                pltpu.VMEM(part, bf16),
                pltpu.SemaphoreType.DMA((2, len(group))),
                pltpu.SemaphoreType.DMA((len(groups),)),
            ],
            alias=alias,
        )(*args)
    grad_query, grad_keys, grad_values = grads_out
    return (output, grad_query, grad_keys, grad_values)


def solution(mesh):
    in_specs = (
        P("seq", "tp"),
        P("seq", "tp"),
        P("seq", "tp"),
        P("tp"),
        P("tp", None),
        P(("seq", "tp"), None),
    )
    out_specs = (P(("seq", "tp"), None), P("seq", "tp"), P("seq", "tp"), P("seq", "tp"))

    return jax.shard_map(local, mesh=mesh, in_specs=in_specs, out_specs=out_specs, check_vma=False)
```

time: 66.4 us -> 66 us (level)
  waiting for transfers between devices: 30 us -> 28.3 us
  starting transfers between devices: 16.1 us -> 17.5 us
    ppermute x11 -> x13, waiting for transfers between devices: 30 us -> 28.3 us  [swap(): return lax.ppermute(x, axis, [(i, i ^ bit) for i in range(count)])]
    ppermute x11 -> x13, starting transfers between devices: 16.1 us -> 17.5 us  [swap(): return lax.ppermute(x, axis, [(i, i ^ bit) for i in range(count)])]
    pallas_call x8 -> x11, Pallas kernels: 9.92 us -> 10.6 us  [the longest x2 4.96 us: local(): call(functools.partial(local_backward_body, group, block), [(part, bf16),...]
  transfers between devices with their start and end apart: 11 -> 13, of which waited for: 6 -> 6; matrix products, arithmetic and copies ran while one was open for 0% -> 0% of each run, Pallas kernels for 22% -> 23%
where the time goes in v3:
time: 66 us; the launch traced here: 65.9 us
  waiting for transfers between devices  28.3 us (43%)
  Pallas kernels  19.3 us (29%)
  starting transfers between devices  17.5 us (27%)
  between operations  0.81 us (1%)
    ppermute x13, waiting for transfers between devices, swap(): return lax.ppermute(x, axis, [(i, i ^ bit) for i in range(count)])  28.3 us
    ppermute x13, starting transfers between devices, swap(): return lax.ppermute(x, axis, [(i, i ^ bit) for i in range(count)])  17.5 us
    pallas_call x2, Pallas kernels, local(): call(functools.partial(local_backward_body, group, block), [(part, bf16),...  4.96 us
    pallas_call x2, Pallas kernels, local(): call(functools.partial(final_body, group, moves, len(recvs)), [(full, bf1...  2.54 us
    pallas_call x1, Pallas kernels, local(): call(functools.partial(local_forward_body, heads, block), [(full, f32)],...  2.22 us
    pallas_call x1, Pallas kernels, local(): call(functools.partial(own_memory_body, heads), [(packed, bf16), (full, b...  1.88 us
    pallas_call x1, Pallas kernels, local(): call(functools.partial(load_query_body, heads), [(full, bf16), ((2 * widt...  1.56 us
    pallas_call x2, Pallas kernels, local(): call(grad_mixed_body, [((rows, width), bf16)], [VM] * (len(masks) + 1))  1.47 us
  transfers between devices with their start and end apart: 13, of which 6 were waited for; matrix products, arithmetic and copies ran while one was open for 0% of the time, Pallas kernels for 23%

profile of v3, /device:TPU:0, one launch (start us, length us, event | category | flops | bytes accessed | tf_op | source)
XLA Modules:
  0.0 65.9 jit_solution(4607531176200193425)
XLA Ops:
  0.6 1.9 %shard_map.94 = (bf16[528,128]{1,0:T(8,128)(2,1)S(1)}, bf16[512,512]{1,0:T(8,128)(2,1)S(1)}, bf16[512,512]{1,0:T(8,128)(2,1)S(1)}) custom-call(bf16[512,512]{1,0:T(8,128)(2,1)} %k_hbm.1, bf16[512,512]{1,0:T(8,128)(2,1)} %v_hbm.1), custom_call_target="tpu_custom_call" | custom-call | flops 268435456 | bytes 1048576 | tf_op jit(solution)/shard_map/pallas_call | solution.py:398
  2.5 3.0 %collective-permute-start = (bf16[528,128]{1,0:T(8,128)(2,1)S(1)}, bf16[528,128]{1,0:T(8,128)(2,1)S(1)}, u32[]{:S(2)}, u32[]{:S(2)}) collective-permute-start(bf16[528,128]{1,0:T(8,128)(2,1)S(1)} %get-tuple-element.36.refs_0_), channel_id=1, source_target_pairs={{0,4},{4,0},{8,12},{12,8},{16,20},{20,16},{24,28},{28,24},{1,5},{5... | collective-permute-start | bytes 405512 | tf_op jit(solution)/shard_map/ppermute | solution.py:349
  5.6 3.6 %collective-permute-done.refs_1_.refs_0_.refs_5_ = bf16[528,128]{1,0:T(8,128)(2,1)S(1)} collective-permute-done((bf16[528,128]{1,0:T(8,128)(2,1)S(1)}, bf16[528,128]{1,0:T(8,128)(2,1)S(1)}, u32[]{:S(2)}, u32[]{:S(2)}) %collective-permute-start) | collective-permute-done | bytes 135200 | tf_op jit(solution)/shard_map/ppermute | solution.py:349
  9.2 1.9 %collective-permute-start.1 = (bf16[528,128]{1,0:T(8,128)(2,1)S(1)}, bf16[528,128]{1,0:T(8,128)(2,1)S(1)}, u32[]{:S(2)}, u32[]{:S(2)}) collective-permute-start(bf16[528,128]{1,0:T(8,128)(2,1)S(1)} %shard_map.96), channel_id=1, source_target_pairs={{0,8},{4,12},{8,0},{12,4},{16,24},{20,28},{24,16},{28,20},{1,9},{5... | collective-permute-start | bytes 405512 | tf_op jit(solution)/shard_map/ppermute | solution.py:349
  11.1 3.2 %collective-permute-done.1.refs_2_.refs_1_.refs_6_ = bf16[528,128]{1,0:T(8,128)(2,1)S(1)} collective-permute-done((bf16[528,128]{1,0:T(8,128)(2,1)S(1)}, bf16[528,128]{1,0:T(8,128)(2,1)S(1)}, u32[]{:S(2)}, u32[]{:S(2)}) %collective-permute-start.1) | collective-permute-done | bytes 135200 | tf_op jit(solution)/shard_map/ppermute | solution.py:349
  14.3 2.9 %collective-permute-start.2 = (bf16[272,128]{1,0:T(8,128)(2,1)S(1)}, bf16[272,128]{1,0:T(8,128)(2,1)S(1)}, u32[]{:S(2)}, u32[]{:S(2)}) collective-permute-start(bf16[272,128]{1,0:T(8,128)(2,1)S(1)} %get-tuple-element.37), channel_id=1, source_target_pairs={{0,16},{4,20},{8,24},{12,28},{16,0},{20,4},{24,8},{28,12},{1,17},{... | collective-permute-start | bytes 208904 | tf_op jit(solution)/shard_map/ppermute | solution.py:349
  17.3 1.6 %shard_map.93 = (bf16[512,512]{1,0:T(8,128)(2,1)S(1)}, bf16[1024,512]{1,0:T(8,128)(2,1)S(1)}, f32[8,128]{1,0:T(8,128)S(1)}) custom-call(bf16[512,512]{1,0:T(8,128)(2,1)} %q_hbm.1, f32[4]{0:T(128)} %beta_hbm.1), custom_call_target="tpu_custom_call" | custom-call | flops 65536 | bytes 1048576 | tf_op jit(solution)/shard_map/pallas_call | solution.py:404
  18.9 2.2 %shard_map.95.lo_ref = f32[512,512]{1,0:T(8,128)S(1)} custom-call(bf16[512,512]{1,0:T(8,128)(2,1)S(1)} %get-tuple-element.32.q_ref.refs_2_, bf16[512,512]{1,0:T(8,128)(2,1)S(1)} %get-tuple-element.33.k_ref.refs_0_, bf16[512,512]{1,0:T(8,128)(2,1)S(1)} %get-tuple-element.34.v_ref.refs_1_), custom_call_target="tpu_custom_call" | custom-call | flops 268435456 | bytes 1048576 | tf_op jit(solution)/shard_map/pallas_call | solution.py:430
  21.1 1.3 %collective-permute-done.3.refs_3_ = bf16[256,128]{1,0:T(8,128)(2,1)S(1)} collective-permute-done((bf16[256,128]{1,0:T(8,128)(2,1)S(1)}, bf16[256,128]{1,0:T(8,128)(2,1)S(1)}, u32[]{:S(2)}, u32[]{:S(2)}) %collective-permute-start.3) | collective-permute-done | bytes 65568 | tf_op jit(solution)/shard_map/ppermute | solution.py:349
  22.4 1.2 %shard_map.98 = (f32[528,128]{1,0:T(8,128)S(1)}, bf16[256,2048]{1,0:T(8,128)(2,1)S(1)}) custom-call(bf16[512,512]{1,0:T(8,128)(2,1)S(1)} %get-tuple-element.32.q_ref.refs_2_, f32[512,512]{1,0:T(8,128)S(1)} %shard_map.95.lo_ref, f32[8,128]{1,0:T(8,128)S(1)} %get-tuple-element.35.gate_ref.refs_4_, bf16[512,2048]{1,0:T(8,128)(2,1)S(1)} %copy-done, ...), custom_call_target="tpu_custom_call" | custom-call | flops 268435456 | bytes 1048576 | tf_op jit(solution)/shard_map/pallas_call | solution.py:451
  23.6 1.6 %collective-permute-start.7 = (bf16[128,2048]{1,0:T(8,128)(2,1)S(1)}, bf16[128,2048]{1,0:T(8,128)(2,1)S(1)}, u32[]{:S(2)}, u32[]{:S(2)}) collective-permute-start(bf16[128,2048]{1,0:T(8,128)(2,1)S(1)} %copy-done.1), channel_id=1, source_target_pairs={{0,2},{1,3},{2,0},{3,1},{4,6},{5,7},{6,4},{7,5},{8,10},{9,11},{10,... | collective-permute-start | bytes 1572872 | tf_op jit(solution)/shard_map/ppermute | solution.py:349
  25.4 12.6 %collective-permute-done.7.refs_0_ = bf16[128,2048]{1,0:T(8,128)(2,1)S(1)} collective-permute-done((bf16[128,2048]{1,0:T(8,128)(2,1)S(1)}, bf16[128,2048]{1,0:T(8,128)(2,1)S(1)}, u32[]{:S(2)}, u32[]{:S(2)}) %collective-permute-start.7) | collective-permute-done | bytes 524320 | tf_op jit(solution)/shard_map/ppermute | solution.py:349
  38.0 1.1 %shard_map.99 = (bf16[128,2048]{1,0:T(8,128)(2,1)S(1)}, f32[128,2048]{1,0:T(8,128)S(1)}) custom-call(bf16[512,512]{1,0:T(8,128)(2,1)S(1)} %get-tuple-element.32.q_ref.refs_2_, f32[528,128]{1,0:T(8,128)S(1)} %get-tuple-element.39.mem_ref, f32[512,512]{1,0:T(8,128)S(1)} %shard_map.95.lo_ref, f32[8,128]{1,0:T(8,128)S(1)} %get-tuple-element.35.gate_ref.refs_4_, ...), custom_call_target="tpu_custom_call" | custom-call | flops 268435456 | bytes 1048576 | tf_op jit(solution)/shard_map/pallas_call | solution.py:464
  39.1 1.6 %collective-permute-start.5 = (bf16[128,2048]{1,0:T(8,128)(2,1)S(1)}, bf16[128,2048]{1,0:T(8,128)(2,1)S(1)}, u32[]{:S(2)}, u32[]{:S(2)}) collective-permute-start(bf16[128,2048]{1,0:T(8,128)(2,1)S(1)} %get-tuple-element.42), channel_id=1, source_target_pairs={{0,2},{1,3},{2,0},{3,1},{4,6},{5,7},{6,4},{7,5},{8,10},{9,11},{10,... | collective-permute-start | bytes 1572872 | tf_op jit(solution)/shard_map/ppermute | solution.py:349
  43.5 1.6 %collective-permute-start.9 = (bf16[528,128]{1,0:T(8,128)(2,1)S(1)}, bf16[528,128]{1,0:T(8,128)(2,1)S(1)}, u32[]{:S(2)}, u32[]{:S(2)}) collective-permute-start(bf16[528,128]{1,0:T(8,128)(2,1)S(1)} %shard_map.105.refs_0_), channel_id=1, source_target_pairs={{0,4},{4,0},{8,12},{12,8},{16,20},{20,16},{24,28},{28,24},{1,5},{5... | collective-permute-start | bytes 405512 | tf_op jit(solution)/shard_map/ppermute | solution.py:349
  45.0 4.2 %collective-permute-done.9.refs_1_.refs_4_ = bf16[528,128]{1,0:T(8,128)(2,1)S(1)} collective-permute-done((bf16[528,128]{1,0:T(8,128)(2,1)S(1)}, bf16[528,128]{1,0:T(8,128)(2,1)S(1)}, u32[]{:S(2)}, u32[]{:S(2)}) %collective-permute-start.9) | collective-permute-done | bytes 135200 | tf_op jit(solution)/shard_map/ppermute | solution.py:349
  49.3 1.7 %collective-permute-start.10 = (bf16[528,128]{1,0:T(8,128)(2,1)S(1)}, bf16[528,128]{1,0:T(8,128)(2,1)S(1)}, u32[]{:S(2)}, u32[]{:S(2)}) collective-permute-start(bf16[528,128]{1,0:T(8,128)(2,1)S(1)} %shard_map.106), channel_id=1, source_target_pairs={{0,8},{4,12},{8,0},{12,4},{16,24},{20,28},{24,16},{28,20},{1,9},{5... | collective-permute-start | bytes 405512 | tf_op jit(solution)/shard_map/ppermute | solution.py:349
  51.0 3.4 %collective-permute-done.10.refs_2_.refs_5_ = bf16[528,128]{1,0:T(8,128)(2,1)S(1)} collective-permute-done((bf16[528,128]{1,0:T(8,128)(2,1)S(1)}, bf16[528,128]{1,0:T(8,128)(2,1)S(1)}, u32[]{:S(2)}, u32[]{:S(2)}) %collective-permute-start.10) | collective-permute-done | bytes 135200 | tf_op jit(solution)/shard_map/ppermute | solution.py:349
  54.4 1.8 %collective-permute-start.11 = (bf16[272,128]{1,0:T(8,128)(2,1)S(1)}, bf16[272,128]{1,0:T(8,128)(2,1)S(1)}, u32[]{:S(2)}, u32[]{:S(2)}) collective-permute-start(bf16[272,128]{1,0:T(8,128)(2,1)S(1)} %get-tuple-element.48), channel_id=1, source_target_pairs={{0,16},{4,20},{8,24},{12,28},{16,0},{20,4},{24,8},{28,12},{1,17},{... | collective-permute-start | bytes 208904 | tf_op jit(solution)/shard_map/ppermute | solution.py:349
  56.3 1.2 %collective-permute-start.12 = (bf16[256,128]{1,0:T(8,128)(2,1)S(1)}, bf16[256,128]{1,0:T(8,128)(2,1)S(1)}, u32[]{:S(2)}, u32[]{:S(2)}) collective-permute-start(bf16[256,128]{1,0:T(8,128)(2,1)S(1)} %get-tuple-element.49), channel_id=1, source_target_pairs={{0,16},{4,20},{8,24},{12,28},{16,0},{20,4},{24,8},{28,12},{1,17},{... | collective-permute-start | bytes 196616 | tf_op jit(solution)/shard_map/ppermute | solution.py:349
  57.4 2.5 %shard_map.108 = (bf16[512,256]{1,0:T(8,128)(2,1)S(1)}, f32[512,256]{1,0:T(8,128)S(1)}, f32[512,256]{1,0:T(8,128)S(1)}) custom-call(bf16[512,512]{1,0:T(8,128)(2,1)S(1)} %get-tuple-element.32.q_ref.refs_2_, bf16[512,512]{1,0:T(8,128)(2,1)S(1)} %get-tuple-element.33.k_ref.refs_0_, bf16[512,512]{1,0:T(8,128)(2,1)S(1)} %get-tuple-element.34.v_ref.refs_1_, ...), custom_call_target="tpu_custom_call" | custom-call | flops 268435456 | bytes 1048576 | tf_op jit(solution)/shard_map/pallas_call | solution.py:485
  59.9 2.5 %shard_map.104 = (bf16[512,256]{1,0:T(8,128)(2,1)S(1)}, f32[512,256]{1,0:T(8,128)S(1)}, f32[512,256]{1,0:T(8,128)S(1)}) custom-call(bf16[512,512]{1,0:T(8,128)(2,1)S(1)} %get-tuple-element.32.q_ref.refs_2_, bf16[512,512]{1,0:T(8,128)(2,1)S(1)} %get-tuple-element.33.k_ref.refs_0_, bf16[512,512]{1,0:T(8,128)(2,1)S(1)} %get-tuple-element.34.v_ref.refs_1_, ...), custom_call_target="tpu_custom_call" | custom-call | flops 268435456 | bytes 1048576 | tf_op jit(solution)/shard_map/pallas_call | solution.py:485
  62.4 1.3 %shard_map.109 = (bf16[512,512]{1,0:T(8,128)(2,1)}, bf16[512,512]{1,0:T(8,128)(2,1)}, bf16[512,512]{1,0:T(8,128)(2,1)}) custom-call(bf16[512,512]{1,0:T(8,128)(2,1)S(1)} %get-tuple-element.33.k_ref.refs_0_, bf16[512,512]{1,0:T(8,128)(2,1)S(1)} %get-tuple-element.34.v_ref.refs_1_, f32[512,256]{1,0:T(8,128)S(1)} %get-tuple-element.50.refs_2_, ...), custom_call_target="tpu_custom_call" | custom-call | flops 268435456 | bytes 1048576 | tf_op jit(solution)/shard_map/pallas_call | solution.py:506
  63.7 1.3 %shard_map.110 = (bf16[512,512]{1,0:T(8,128)(2,1)}, bf16[512,512]{1,0:T(8,128)(2,1)}, bf16[512,512]{1,0:T(8,128)(2,1)}) custom-call(bf16[512,512]{1,0:T(8,128)(2,1)S(1)} %get-tuple-element.33.k_ref.refs_0_, bf16[512,512]{1,0:T(8,128)(2,1)S(1)} %get-tuple-element.34.v_ref.refs_1_, ...), custom_call_target="tpu_custom_call", output_to_operand_aliasing={{0}: (8, {}), {1}: (9, {}), {2}: (10, {})} | custom-call | flops 268435456 | bytes 1048576 | tf_op jit(solution)/shard_map/pallas_call | solution.py:506
  (24 shorter events, 4.2 us)
Async XLA Ops:
  2.5 19.9 %copy-start = (bf16[512,2048]{1,0:T(8,128)(2,1)S(1)}, bf16[512,2048]{1,0:T(8,128)(2,1)}, u32[]{:S(2)}) copy-start(bf16[512,2048]{1,0:T(8,128)(2,1)} %refs_2_.3) | copy-start | bytes 6291460
  2.5 6.6 %collective-permute-start = (bf16[528,128]{1,0:T(8,128)(2,1)S(1)}, bf16[528,128]{1,0:T(8,128)(2,1)S(1)}, u32[]{:S(2)}, u32[]{:S(2)}) collective-permute-start(bf16[528,128]{1,0:T(8,128)(2,1)S(1)} %get-tuple-element.36.refs_0_), channel_id=1, source_target_pairs={{0,4},{4,0},{8,12},{12,8},{16,20},{20,16},{24,28},{28,24},{1,5},{5... | collective-permute-start | bytes 405512 | tf_op jit(solution)/shard_map/ppermute | solution.py:349
  9.2 5.1 %collective-permute-start.1 = (bf16[528,128]{1,0:T(8,128)(2,1)S(1)}, bf16[528,128]{1,0:T(8,128)(2,1)S(1)}, u32[]{:S(2)}, u32[]{:S(2)}) collective-permute-start(bf16[528,128]{1,0:T(8,128)(2,1)S(1)} %shard_map.96), channel_id=1, source_target_pairs={{0,8},{4,12},{8,0},{12,4},{16,24},{20,28},{24,16},{28,20},{1,9},{5... | collective-permute-start | bytes 405512 | tf_op jit(solution)/shard_map/ppermute | solution.py:349
  14.3 8.1 %collective-permute-start.2 = (bf16[272,128]{1,0:T(8,128)(2,1)S(1)}, bf16[272,128]{1,0:T(8,128)(2,1)S(1)}, u32[]{:S(2)}, u32[]{:S(2)}) collective-permute-start(bf16[272,128]{1,0:T(8,128)(2,1)S(1)} %get-tuple-element.37), channel_id=1, source_target_pairs={{0,16},{4,20},{8,24},{12,28},{16,0},{20,4},{24,8},{28,12},{1,17},{... | collective-permute-start | bytes 208904 | tf_op jit(solution)/shard_map/ppermute | solution.py:349
  17.2 5.2 %collective-permute-start.3 = (bf16[256,128]{1,0:T(8,128)(2,1)S(1)}, bf16[256,128]{1,0:T(8,128)(2,1)S(1)}, u32[]{:S(2)}, u32[]{:S(2)}) collective-permute-start(bf16[256,128]{1,0:T(8,128)(2,1)S(1)} %get-tuple-element.38), channel_id=1, source_target_pairs={{0,16},{4,20},{8,24},{12,28},{16,0},{20,4},{24,8},{28,12},{1,17},{... | collective-permute-start | bytes 196616 | tf_op jit(solution)/shard_map/ppermute | solution.py:349
  21.1 2.5 %copy-start.1 = (bf16[128,2048]{1,0:T(8,128)(2,1)S(1)}, bf16[128,2048]{1,0:T(8,128)(2,1)}, u32[]{:S(2)}) copy-start(bf16[128,2048]{1,0:T(8,128)(2,1)} %refs_0_.1) | copy-start | bytes 1572868
  23.6 14.4 %collective-permute-start.4 = (bf16[256,2048]{1,0:T(8,128)(2,1)S(1)}, bf16[256,2048]{1,0:T(8,128)(2,1)S(1)}, u32[]{:S(2)}, u32[]{:S(2)}) collective-permute-start(bf16[256,2048]{1,0:T(8,128)(2,1)S(1)} %get-tuple-element.40), channel_id=1, source_target_pairs={{0,1},{1,0},{2,3},{3,2},{4,5},{5,4},{6,7},{7,6},{8,9},{9,8},{10,11... | collective-permute-start | bytes 3145736 | tf_op jit(solution)/shard_map/ppermute | solution.py:349
  23.6 14.3 %collective-permute-start.7 = (bf16[128,2048]{1,0:T(8,128)(2,1)S(1)}, bf16[128,2048]{1,0:T(8,128)(2,1)S(1)}, u32[]{:S(2)}, u32[]{:S(2)}) collective-permute-start(bf16[128,2048]{1,0:T(8,128)(2,1)S(1)} %copy-done.1), channel_id=1, source_target_pairs={{0,2},{1,3},{2,0},{3,1},{4,6},{5,7},{6,4},{7,5},{8,10},{9,11},{10,... | collective-permute-start | bytes 1572872 | tf_op jit(solution)/shard_map/ppermute | solution.py:349
  25.2 15.4 %collective-permute-start.6 = (bf16[128,2048]{1,0:T(8,128)(2,1)S(1)}, bf16[128,2048]{1,0:T(8,128)(2,1)S(1)}, u32[]{:S(2)}, u32[]{:S(2)}) collective-permute-start(bf16[128,2048]{1,0:T(8,128)(2,1)S(1)} %copy-done.1), channel_id=1, source_target_pairs={{0,1},{1,0},{2,3},{3,2},{4,5},{5,4},{6,7},{7,6},{8,9},{9,8},{10,11... | collective-permute-start | bytes 1572872 | tf_op jit(solution)/shard_map/ppermute | solution.py:349
  38.0 3.4 %collective-permute-start.8 = (bf16[128,2048]{1,0:T(8,128)(2,1)S(1)}, bf16[128,2048]{1,0:T(8,128)(2,1)S(1)}, u32[]{:S(2)}, u32[]{:S(2)}) collective-permute-start(bf16[128,2048]{1,0:T(8,128)(2,1)S(1)} %collective-permute-done.7.refs_0_), channel_id=1, source_target_pairs={{0,1},{1,0},{2,3},{3,2},{4,5},{5,4},{6,7},{7,6},{8,9},{9,8},{10,11... | collective-permute-start | bytes 1572872 | tf_op jit(solution)/shard_map/ppermute | solution.py:349
  39.1 25.9 %collective-permute-start.5 = (bf16[128,2048]{1,0:T(8,128)(2,1)S(1)}, bf16[128,2048]{1,0:T(8,128)(2,1)S(1)}, u32[]{:S(2)}, u32[]{:S(2)}) collective-permute-start(bf16[128,2048]{1,0:T(8,128)(2,1)S(1)} %get-tuple-element.42), channel_id=1, source_target_pairs={{0,2},{1,3},{2,0},{3,1},{4,6},{5,7},{6,4},{7,5},{8,10},{9,11},{10,... | collective-permute-start | bytes 1572872 | tf_op jit(solution)/shard_map/ppermute | solution.py:349
  43.5 5.8 %collective-permute-start.9 = (bf16[528,128]{1,0:T(8,128)(2,1)S(1)}, bf16[528,128]{1,0:T(8,128)(2,1)S(1)}, u32[]{:S(2)}, u32[]{:S(2)}) collective-permute-start(bf16[528,128]{1,0:T(8,128)(2,1)S(1)} %shard_map.105.refs_0_), channel_id=1, source_target_pairs={{0,4},{4,0},{8,12},{12,8},{16,20},{20,16},{24,28},{28,24},{1,5},{5... | collective-permute-start | bytes 405512 | tf_op jit(solution)/shard_map/ppermute | solution.py:349
  49.3 5.1 %collective-permute-start.10 = (bf16[528,128]{1,0:T(8,128)(2,1)S(1)}, bf16[528,128]{1,0:T(8,128)(2,1)S(1)}, u32[]{:S(2)}, u32[]{:S(2)}) collective-permute-start(bf16[528,128]{1,0:T(8,128)(2,1)S(1)} %shard_map.106), channel_id=1, source_target_pairs={{0,8},{4,12},{8,0},{12,4},{16,24},{20,28},{24,16},{28,20},{1,9},{5... | collective-permute-start | bytes 405512 | tf_op jit(solution)/shard_map/ppermute | solution.py:349
  54.4 8.0 %collective-permute-start.11 = (bf16[272,128]{1,0:T(8,128)(2,1)S(1)}, bf16[272,128]{1,0:T(8,128)(2,1)S(1)}, u32[]{:S(2)}, u32[]{:S(2)}) collective-permute-start(bf16[272,128]{1,0:T(8,128)(2,1)S(1)} %get-tuple-element.48), channel_id=1, source_target_pairs={{0,16},{4,20},{8,24},{12,28},{16,0},{20,4},{24,8},{28,12},{1,17},{... | collective-permute-start | bytes 208904 | tf_op jit(solution)/shard_map/ppermute | solution.py:349
  56.3 7.4 %collective-permute-start.12 = (bf16[256,128]{1,0:T(8,128)(2,1)S(1)}, bf16[256,128]{1,0:T(8,128)(2,1)S(1)}, u32[]{:S(2)}, u32[]{:S(2)}) collective-permute-start(bf16[256,128]{1,0:T(8,128)(2,1)S(1)} %get-tuple-element.49), channel_id=1, source_target_pairs={{0,16},{4,20},{8,24},{12,28},{16,0},{20,4},{24,8},{28,12},{1,17},{... | collective-permute-start | bytes 196616 | tf_op jit(solution)/shard_map/ppermute | solution.py:349

commit v4 on v3

--- a/solution.py
+++ b/solution.py
@@ -275,8 +275,17 @@
     keep_ref[...] = total[half:]
 
 
-def output_done_body(keep_ref, recv_ref, o_ref):
-    o_ref[...] = (keep_ref[...] + recv_ref[...].astype(f32)).astype(bf16)
+def output_done_body(moves, keep_ref, recv_ref, *refs):
+    gqs, (out_hbm, gq_hbm, out_ref, sems) = refs[: len(moves)], refs[len(moves) :]
+    copies = [
+        pltpu.make_async_copy(ref, gq_hbm.at[:, spots], sems.at[n]) for n, (ref, spots) in enumerate(zip(gqs, moves))
+    ]
+    out_ref[...] = (keep_ref[...] + recv_ref[...].astype(f32)).astype(bf16)
+    copies = [pltpu.make_async_copy(out_ref, out_hbm, sems.at[len(moves)])] + copies
+    for copy in copies:
+        copy.start()
+    for copy in copies:
+        copy.wait()
 
 
 def local_backward_body(group, block, q_ref, k_ref, v_ref, g_ref, mem_ref, gate_ref, *refs):
@@ -318,28 +327,42 @@
         gq_ref[:, cols(n)] = (jnp.concatenate(gq, 0) + gqf * slope(qx)).astype(bf16)
 
 
-def final_body(group, moves, steps, *refs):
-    k_ref, v_ref, kl_ref, vl_ref = refs[:4]
-    recvs = refs[4 : 4 + steps]
-    if group[0] == 0:
-        recvs = recvs + (None,)
-    gqs = refs[4 + steps : 4 + steps + len(moves)]
-    gq_hbm, gk_hbm, gv_hbm, gk_ref, gv_ref, sems, gq_sems = refs[-7:]
-    copies = []
-    for n, (ref, spots) in enumerate(zip(gqs, moves)):
-        copies.append(pltpu.make_async_copy(ref, gq_hbm.at[:, spots], gq_sems.at[n]))
-        copies[-1].start()
+def final_part(group, k_ref, v_ref, kl_ref, vl_ref, recvs, store):
     for i, h in enumerate(group):
         kx = k_ref[:, cols(h)].astype(f32)
         matrix = scan_state(True, recvs, rows_of(h))
         msum = scan_state(True, recvs, slice(0, PAD))[h : h + 1, :]
         gkf = halves(dot(v_ref[:, cols(h)], jnp.concatenate(split(matrix), 0), 1, 1)) + msum
-        gk_ref[:, cols(i)] = (kl_ref[:, cols(i)] + gkf * slope(kx)).astype(bf16)
-        copies.append(pltpu.make_async_copy(gk_ref.at[:, cols(i)], gk_hbm.at[:, cols(h)], sems.at[0, i]))
+        store(0, i, (kl_ref[:, cols(i)] + gkf * slope(kx)).astype(bf16))
+        store(1, i, (vl_ref[:, cols(i)] + twofold(feat(kx), matrix)).astype(bf16))
+
+
+def final_first_body(group, steps, *refs):
+    outs = refs[-2:]
+
+    def store(n, i, x):
+        outs[n][:, cols(i)] = x
+
+    final_part(group, *refs[:4], refs[4 : 4 + steps] + (None,), store)
+
+
+def final_second_body(before, group, steps, *refs):
+    firsts = refs[4 + steps : 6 + steps]
+    outs, parts, sems = refs[-5:-3], refs[-3:-1], refs[-1]
+    copies = []
+
+    def send(ref, out, spots, sem):
+        copies.append(pltpu.make_async_copy(ref, out.at[:, spots], sem))
         copies[-1].start()
-        gv_ref[:, cols(i)] = (vl_ref[:, cols(i)] + twofold(feat(kx), matrix)).astype(bf16)
-        copies.append(pltpu.make_async_copy(gv_ref.at[:, cols(i)], gv_hbm.at[:, cols(h)], sems.at[1, i]))
-        copies[-1].start()
+
+    for n in range(2):
+        send(firsts[n], outs[n], slice(0, before * HD), sems.at[n, len(group)])
+
+    def store(n, i, x):
+        parts[n][:, cols(i)] = x
+        send(parts[n].at[:, cols(i)], outs[n], cols(group[i]), sems.at[n, i])
+
+    final_part(group, *refs[:4], refs[4 : 4 + steps], store)
     for copy in copies:
         copy.wait()
 
@@ -411,10 +434,10 @@
     fwd = scan(own, "seq", cut)
 
     held = {0: cotangent}
-    near, later = [0], []
+    order, later = [[0]], []
     if tp > 1:
         held[1] = swap(cotangent, "tp", 1)
-        near = [0, 1]
+        order = [[0, 1]]
     bit = 2
     far = [0]
     while bit < tp:
@@ -425,7 +448,7 @@
     for m in far[1:]:
         held[m | 1] = swap(held[m], "tp", 1)
         later += [m, m | 1]
-    order = [near] + ([later] if later else [])
+    order += [later] if later else []
 
     local_out = call(
         functools.partial(local_forward_body, heads, block), [(full, f32)], [VM, VM, VM]
@@ -474,10 +497,6 @@
         send, keep = total[:part].astype(bf16), total[part:]
         bit *= 2
     recv = swap(send, "tp", bit)
-    output = call(
-        output_done_body, [((length // tp, model), bf16)], [VM, VM], flops=1 << 20
-    )(keep, recv)[0]
-
     pieces = []
     for group in groups:
         part = (length, len(group) * HD)
@@ -488,35 +507,33 @@
                 [VM] * 6,
             )(query, keys, values, grad, memory, gates)
         )
-    grads_out = None
-    for n, group in enumerate(groups):
-        recvs = bwd[:-1] if n == 0 else bwd
-        args = [keys, values, *pieces[n][1:], *recvs]
-        specs = [VM] * len(args)
-        moves, alias = [], None
-        if n == 0:
-            args += [piece[0] for piece in pieces]
-            specs += [VM] * len(pieces)
-            moves = [slice(g[0] * HD, (g[-1] + 1) * HD) for g in groups]
-        else:
-            alias = {len(args) + i: i for i in range(3)}
-            args += grads_out
-            specs += [hbm] * 3
-        part = (length, len(group) * HD)
-        grads_out = call(
-            functools.partial(final_body, group, moves, len(recvs)),
-            [(full, bf16)] * 3,
-            specs,
-            out_specs=[hbm] * 3,
-            scratch=[
-                pltpu.VMEM(part, bf16),
-                pltpu.VMEM(part, bf16),
-                pltpu.SemaphoreType.DMA((2, len(group))),
-                pltpu.SemaphoreType.DMA((len(groups),)),
-            ],
-            alias=alias,
-        )(*args)
-    grad_query, grad_keys, grad_values = grads_out
+    own_rows = (length // tp, model)
+    output, grad_query = call(
+        functools.partial(output_done_body, [slice(g[0] * HD, (g[-1] + 1) * HD) for g in groups]),
+        [(own_rows, bf16), (full, bf16)],
+        [VM] * (2 + len(groups)),
+        out_specs=[hbm] * 2,
+        scratch=[pltpu.VMEM(own_rows, bf16), pltpu.SemaphoreType.DMA((len(groups) + 1,))],
+        flops=1 << 20,
+    )(keep, recv, *[piece[0] for piece in pieces])
+    part = (length, first * HD)
+    early = call(
+        functools.partial(final_first_body, groups[0], len(bwd) - 1),
+        [(part, bf16)] * 2,
+        [VM] * (3 + len(bwd)),
+    )(keys, values, *pieces[0][1:], *bwd[:-1])
+    part = (length, len(groups[1]) * HD)
+    grad_keys, grad_values = call(
+        functools.partial(final_second_body, first, groups[1], len(bwd)),
+        [(full, bf16)] * 2,
+        [VM] * (6 + len(bwd)),
+        out_specs=[hbm] * 2,
+        scratch=[
+            pltpu.VMEM(part, bf16),
+            pltpu.VMEM(part, bf16),
+            pltpu.SemaphoreType.DMA((2, len(groups[1]) + 1)),
+        ],
+    )(keys, values, *pieces[1][1:], *bwd, *early)
     return (output, grad_query, grad_keys, grad_values)
 
 

time: 66 us -> 65.5 us (level)
  transfers between devices with their start and end apart: 13 -> 13, of which waited for: 6 -> 6; matrix products, arithmetic and copies ran while one was open for 0% -> 0% of each run, Pallas kernels for 23% -> 22%
where the time goes in v4:
time: 65.5 us; the launch traced here: 65.3 us
  waiting for transfers between devices  28.3 us (43%)
  Pallas kernels  18.7 us (29%)
  starting transfers between devices  17.5 us (27%)
  between operations  0.81 us (1%)
    ppermute x13, waiting for transfers between devices, swap(): return lax.ppermute(x, axis, [(i, i ^ bit) for i in range(count)])  28.3 us
    ppermute x13, starting transfers between devices, swap(): return lax.ppermute(x, axis, [(i, i ^ bit) for i in range(count)])  17.5 us
    pallas_call x2, Pallas kernels, local(): call(functools.partial(local_backward_body, group, block), [(part, bf16),...  4.96 us
    pallas_call x1, Pallas kernels, local(): call(functools.partial(local_forward_body, heads, block), [(full, f32)],...  2.22 us
    pallas_call x1, Pallas kernels, local(): call(functools.partial(own_memory_body, heads), [(packed, bf16), (full, b...  1.88 us
    pallas_call x1, Pallas kernels, local(): call(functools.partial(load_query_body, heads), [(full, bf16), ((2 * widt...  1.56 us
    pallas_call x2, Pallas kernels, local(): call(grad_mixed_body, [((rows, width), bf16)], [VM] * (len(masks) + 1))  1.47 us
  transfers between devices with their start and end apart: 13, of which 6 were waited for; matrix products, arithmetic and copies ran while one was open for 0% of the time, Pallas kernels for 22%

profile of v4, /device:TPU:0, one launch (start us, length us, event | category | flops | bytes accessed | tf_op | source)
XLA Modules:
  0.0 65.3 jit_solution(14457137626941709971)
XLA Ops:
  0.6 1.9 %shard_map.94 = (bf16[528,128]{1,0:T(8,128)(2,1)S(1)}, bf16[512,512]{1,0:T(8,128)(2,1)S(1)}, bf16[512,512]{1,0:T(8,128)(2,1)S(1)}) custom-call(bf16[512,512]{1,0:T(8,128)(2,1)} %k_hbm.1, bf16[512,512]{1,0:T(8,128)(2,1)} %v_hbm.1), custom_call_target="tpu_custom_call" | custom-call | flops 268435456 | bytes 1048576 | tf_op jit(solution)/shard_map/pallas_call | solution.py:421
  2.5 3.0 %collective-permute-start = (bf16[528,128]{1,0:T(8,128)(2,1)S(1)}, bf16[528,128]{1,0:T(8,128)(2,1)S(1)}, u32[]{:S(2)}, u32[]{:S(2)}) collective-permute-start(bf16[528,128]{1,0:T(8,128)(2,1)S(1)} %get-tuple-element.36.refs_0_), channel_id=1, source_target_pairs={{0,4},{4,0},{8,12},{12,8},{16,20},{20,16},{24,28},{28,24},{1,5},{5... | collective-permute-start | bytes 405512 | tf_op jit(solution)/shard_map/ppermute | solution.py:372
  5.6 3.6 %collective-permute-done.refs_1_.refs_0_.refs_5_ = bf16[528,128]{1,0:T(8,128)(2,1)S(1)} collective-permute-done((bf16[528,128]{1,0:T(8,128)(2,1)S(1)}, bf16[528,128]{1,0:T(8,128)(2,1)S(1)}, u32[]{:S(2)}, u32[]{:S(2)}) %collective-permute-start) | collective-permute-done | bytes 135200 | tf_op jit(solution)/shard_map/ppermute | solution.py:372
  9.2 1.9 %collective-permute-start.1 = (bf16[528,128]{1,0:T(8,128)(2,1)S(1)}, bf16[528,128]{1,0:T(8,128)(2,1)S(1)}, u32[]{:S(2)}, u32[]{:S(2)}) collective-permute-start(bf16[528,128]{1,0:T(8,128)(2,1)S(1)} %shard_map.96), channel_id=1, source_target_pairs={{0,8},{4,12},{8,0},{12,4},{16,24},{20,28},{24,16},{28,20},{1,9},{5... | collective-permute-start | bytes 405512 | tf_op jit(solution)/shard_map/ppermute | solution.py:372
  11.1 3.2 %collective-permute-done.1.refs_2_.refs_1_.refs_6_ = bf16[528,128]{1,0:T(8,128)(2,1)S(1)} collective-permute-done((bf16[528,128]{1,0:T(8,128)(2,1)S(1)}, bf16[528,128]{1,0:T(8,128)(2,1)S(1)}, u32[]{:S(2)}, u32[]{:S(2)}) %collective-permute-start.1) | collective-permute-done | bytes 135200 | tf_op jit(solution)/shard_map/ppermute | solution.py:372
  14.3 2.9 %collective-permute-start.2 = (bf16[272,128]{1,0:T(8,128)(2,1)S(1)}, bf16[272,128]{1,0:T(8,128)(2,1)S(1)}, u32[]{:S(2)}, u32[]{:S(2)}) collective-permute-start(bf16[272,128]{1,0:T(8,128)(2,1)S(1)} %get-tuple-element.37), channel_id=1, source_target_pairs={{0,16},{4,20},{8,24},{12,28},{16,0},{20,4},{24,8},{28,12},{1,17},{... | collective-permute-start | bytes 208904 | tf_op jit(solution)/shard_map/ppermute | solution.py:372
  17.3 1.6 %shard_map.93 = (bf16[512,512]{1,0:T(8,128)(2,1)S(1)}, bf16[1024,512]{1,0:T(8,128)(2,1)S(1)}, f32[8,128]{1,0:T(8,128)S(1)}) custom-call(bf16[512,512]{1,0:T(8,128)(2,1)} %q_hbm.1, f32[4]{0:T(128)} %beta_hbm.1), custom_call_target="tpu_custom_call" | custom-call | flops 65536 | bytes 1048576 | tf_op jit(solution)/shard_map/pallas_call | solution.py:427
  18.9 2.2 %shard_map.95.lo_ref = f32[512,512]{1,0:T(8,128)S(1)} custom-call(bf16[512,512]{1,0:T(8,128)(2,1)S(1)} %get-tuple-element.32.q_ref.refs_2_, bf16[512,512]{1,0:T(8,128)(2,1)S(1)} %get-tuple-element.33.k_ref.refs_0_, bf16[512,512]{1,0:T(8,128)(2,1)S(1)} %get-tuple-element.34.v_ref.refs_1_), custom_call_target="tpu_custom_call" | custom-call | flops 268435456 | bytes 1048576 | tf_op jit(solution)/shard_map/pallas_call | solution.py:453
  21.1 1.3 %collective-permute-done.3.refs_3_ = bf16[256,128]{1,0:T(8,128)(2,1)S(1)} collective-permute-done((bf16[256,128]{1,0:T(8,128)(2,1)S(1)}, bf16[256,128]{1,0:T(8,128)(2,1)S(1)}, u32[]{:S(2)}, u32[]{:S(2)}) %collective-permute-start.3) | collective-permute-done | bytes 65568 | tf_op jit(solution)/shard_map/ppermute | solution.py:372
  22.4 1.2 %shard_map.98 = (f32[528,128]{1,0:T(8,128)S(1)}, bf16[256,2048]{1,0:T(8,128)(2,1)S(1)}) custom-call(bf16[512,512]{1,0:T(8,128)(2,1)S(1)} %get-tuple-element.32.q_ref.refs_2_, f32[512,512]{1,0:T(8,128)S(1)} %shard_map.95.lo_ref, f32[8,128]{1,0:T(8,128)S(1)} %get-tuple-element.35.gate_ref.refs_4_, bf16[512,2048]{1,0:T(8,128)(2,1)S(1)} %copy-done, ...), custom_call_target="tpu_custom_call" | custom-call | flops 268435456 | bytes 1048576 | tf_op jit(solution)/shard_map/pallas_call | solution.py:474
  23.6 1.6 %collective-permute-start.7 = (bf16[128,2048]{1,0:T(8,128)(2,1)S(1)}, bf16[128,2048]{1,0:T(8,128)(2,1)S(1)}, u32[]{:S(2)}, u32[]{:S(2)}) collective-permute-start(bf16[128,2048]{1,0:T(8,128)(2,1)S(1)} %copy-done.1), channel_id=1, source_target_pairs={{0,2},{1,3},{2,0},{3,1},{4,6},{5,7},{6,4},{7,5},{8,10},{9,11},{10,... | collective-permute-start | bytes 1572872 | tf_op jit(solution)/shard_map/ppermute | solution.py:372
  25.4 12.6 %collective-permute-done.7.refs_0_ = bf16[128,2048]{1,0:T(8,128)(2,1)S(1)} collective-permute-done((bf16[128,2048]{1,0:T(8,128)(2,1)S(1)}, bf16[128,2048]{1,0:T(8,128)(2,1)S(1)}, u32[]{:S(2)}, u32[]{:S(2)}) %collective-permute-start.7) | collective-permute-done | bytes 524320 | tf_op jit(solution)/shard_map/ppermute | solution.py:372
  38.0 1.1 %shard_map.99 = (bf16[128,2048]{1,0:T(8,128)(2,1)S(1)}, f32[128,2048]{1,0:T(8,128)S(1)}) custom-call(bf16[512,512]{1,0:T(8,128)(2,1)S(1)} %get-tuple-element.32.q_ref.refs_2_, f32[528,128]{1,0:T(8,128)S(1)} %get-tuple-element.39.mem_ref, f32[512,512]{1,0:T(8,128)S(1)} %shard_map.95.lo_ref, f32[8,128]{1,0:T(8,128)S(1)} %get-tuple-element.35.gate_ref.refs_4_, ...), custom_call_target="tpu_custom_call" | custom-call | flops 268435456 | bytes 1048576 | tf_op jit(solution)/shard_map/pallas_call | solution.py:487
  39.1 1.6 %collective-permute-start.5 = (bf16[128,2048]{1,0:T(8,128)(2,1)S(1)}, bf16[128,2048]{1,0:T(8,128)(2,1)S(1)}, u32[]{:S(2)}, u32[]{:S(2)}) collective-permute-start(bf16[128,2048]{1,0:T(8,128)(2,1)S(1)} %get-tuple-element.42), channel_id=1, source_target_pairs={{0,2},{1,3},{2,0},{3,1},{4,6},{5,7},{6,4},{7,5},{8,10},{9,11},{10,... | collective-permute-start | bytes 1572872 | tf_op jit(solution)/shard_map/ppermute | solution.py:372
  43.5 1.6 %collective-permute-start.9 = (bf16[528,128]{1,0:T(8,128)(2,1)S(1)}, bf16[528,128]{1,0:T(8,128)(2,1)S(1)}, u32[]{:S(2)}, u32[]{:S(2)}) collective-permute-start(bf16[528,128]{1,0:T(8,128)(2,1)S(1)} %shard_map.106.refs_0_), channel_id=1, source_target_pairs={{0,4},{4,0},{8,12},{12,8},{16,20},{20,16},{24,28},{28,24},{1,5},{5... | collective-permute-start | bytes 405512 | tf_op jit(solution)/shard_map/ppermute | solution.py:372
  45.0 4.2 %collective-permute-done.9.refs_1_.refs_4_ = bf16[528,128]{1,0:T(8,128)(2,1)S(1)} collective-permute-done((bf16[528,128]{1,0:T(8,128)(2,1)S(1)}, bf16[528,128]{1,0:T(8,128)(2,1)S(1)}, u32[]{:S(2)}, u32[]{:S(2)}) %collective-permute-start.9) | collective-permute-done | bytes 135200 | tf_op jit(solution)/shard_map/ppermute | solution.py:372
  49.3 1.6 %collective-permute-start.10 = (bf16[528,128]{1,0:T(8,128)(2,1)S(1)}, bf16[528,128]{1,0:T(8,128)(2,1)S(1)}, u32[]{:S(2)}, u32[]{:S(2)}) collective-permute-start(bf16[528,128]{1,0:T(8,128)(2,1)S(1)} %shard_map.107), channel_id=1, source_target_pairs={{0,8},{4,12},{8,0},{12,4},{16,24},{20,28},{24,16},{28,20},{1,9},{5... | collective-permute-start | bytes 405512 | tf_op jit(solution)/shard_map/ppermute | solution.py:372
  51.0 3.4 %collective-permute-done.10.refs_2_.refs_5_ = bf16[528,128]{1,0:T(8,128)(2,1)S(1)} collective-permute-done((bf16[528,128]{1,0:T(8,128)(2,1)S(1)}, bf16[528,128]{1,0:T(8,128)(2,1)S(1)}, u32[]{:S(2)}, u32[]{:S(2)}) %collective-permute-start.10) | collective-permute-done | bytes 135200 | tf_op jit(solution)/shard_map/ppermute | solution.py:372
  54.4 1.8 %collective-permute-start.11 = (bf16[272,128]{1,0:T(8,128)(2,1)S(1)}, bf16[272,128]{1,0:T(8,128)(2,1)S(1)}, u32[]{:S(2)}, u32[]{:S(2)}) collective-permute-start(bf16[272,128]{1,0:T(8,128)(2,1)S(1)} %get-tuple-element.52), channel_id=1, source_target_pairs={{0,16},{4,20},{8,24},{12,28},{16,0},{20,4},{24,8},{28,12},{1,17},{... | collective-permute-start | bytes 208904 | tf_op jit(solution)/shard_map/ppermute | solution.py:372
  56.3 1.2 %collective-permute-start.12 = (bf16[256,128]{1,0:T(8,128)(2,1)S(1)}, bf16[256,128]{1,0:T(8,128)(2,1)S(1)}, u32[]{:S(2)}, u32[]{:S(2)}) collective-permute-start(bf16[256,128]{1,0:T(8,128)(2,1)S(1)} %get-tuple-element.53), channel_id=1, source_target_pairs={{0,16},{4,20},{8,24},{12,28},{16,0},{20,4},{24,8},{28,12},{1,17},{... | collective-permute-start | bytes 196616 | tf_op jit(solution)/shard_map/ppermute | solution.py:372
  57.4 2.5 %shard_map.104 = (bf16[512,256]{1,0:T(8,128)(2,1)S(1)}, f32[512,256]{1,0:T(8,128)S(1)}, f32[512,256]{1,0:T(8,128)S(1)}) custom-call(bf16[512,512]{1,0:T(8,128)(2,1)S(1)} %get-tuple-element.32.q_ref.refs_2_, bf16[512,512]{1,0:T(8,128)(2,1)S(1)} %get-tuple-element.33.k_ref.refs_0_, bf16[512,512]{1,0:T(8,128)(2,1)S(1)} %get-tuple-element.34.v_ref.refs_1_, ...), custom_call_target="tpu_custom_call" | custom-call | flops 268435456 | bytes 1048576 | tf_op jit(solution)/shard_map/pallas_call | solution.py:504
  59.9 2.5 %shard_map.103 = (bf16[512,256]{1,0:T(8,128)(2,1)S(1)}, f32[512,256]{1,0:T(8,128)S(1)}, f32[512,256]{1,0:T(8,128)S(1)}) custom-call(bf16[512,512]{1,0:T(8,128)(2,1)S(1)} %get-tuple-element.32.q_ref.refs_2_, bf16[512,512]{1,0:T(8,128)(2,1)S(1)} %get-tuple-element.33.k_ref.refs_0_, bf16[512,512]{1,0:T(8,128)(2,1)S(1)} %get-tuple-element.34.v_ref.refs_1_, ...), custom_call_target="tpu_custom_call" | custom-call | flops 268435456 | bytes 1048576 | tf_op jit(solution)/shard_map/pallas_call | solution.py:504
  63.0 1.3 %shard_map.110 = (bf16[512,512]{1,0:T(8,128)(2,1)}, bf16[512,512]{1,0:T(8,128)(2,1)}) custom-call(bf16[512,512]{1,0:T(8,128)(2,1)S(1)} %get-tuple-element.33.k_ref.refs_0_, bf16[512,512]{1,0:T(8,128)(2,1)S(1)} %get-tuple-element.34.v_ref.refs_1_, f32[512,256]{1,0:T(8,128)S(1)} %get-tuple-element.49.refs_2_, f32[512,256]{1,0:T(8,128)S(1)} %get-tuple-element.50.refs_3_, ...), custom_call_target="tpu_custom_call" | custom-call | flops 268435456 | bytes 1048576 | tf_op jit(solution)/shard_map/pallas_call | solution.py:526
  64.3 1.1 %shard_map.105 = (bf16[128,2048]{1,0:T(8,128)(2,1)}, bf16[512,512]{1,0:T(8,128)(2,1)}) custom-call(f32[128,2048]{1,0:T(8,128)S(1)} %get-tuple-element.41.keep_ref, bf16[128,2048]{1,0:T(8,128)(2,1)S(1)} %collective-permute-done.5.recv_ref, bf16[512,256]{1,0:T(8,128)(2,1)S(1)} %get-tuple-element.45.refs_0_, bf16[512,256]{1,0:T(8,128)(2,1)S(1)} %get-tuple-element.46.refs_1_), custom_call_target="tpu_custom_call" | custom-call | flops 1048576 | bytes 1048576 | tf_op jit(solution)/shard_map/pallas_call | solution.py:511
  (24 shorter events, 3.8 us)
Async XLA Ops:
  2.5 19.9 %copy-start = (bf16[512,2048]{1,0:T(8,128)(2,1)S(1)}, bf16[512,2048]{1,0:T(8,128)(2,1)}, u32[]{:S(2)}) copy-start(bf16[512,2048]{1,0:T(8,128)(2,1)} %refs_2_.3) | copy-start | bytes 6291460
  2.5 6.6 %collective-permute-start = (bf16[528,128]{1,0:T(8,128)(2,1)S(1)}, bf16[528,128]{1,0:T(8,128)(2,1)S(1)}, u32[]{:S(2)}, u32[]{:S(2)}) collective-permute-start(bf16[528,128]{1,0:T(8,128)(2,1)S(1)} %get-tuple-element.36.refs_0_), channel_id=1, source_target_pairs={{0,4},{4,0},{8,12},{12,8},{16,20},{20,16},{24,28},{28,24},{1,5},{5... | collective-permute-start | bytes 405512 | tf_op jit(solution)/shard_map/ppermute | solution.py:372
  9.2 5.1 %collective-permute-start.1 = (bf16[528,128]{1,0:T(8,128)(2,1)S(1)}, bf16[528,128]{1,0:T(8,128)(2,1)S(1)}, u32[]{:S(2)}, u32[]{:S(2)}) collective-permute-start(bf16[528,128]{1,0:T(8,128)(2,1)S(1)} %shard_map.96), channel_id=1, source_target_pairs={{0,8},{4,12},{8,0},{12,4},{16,24},{20,28},{24,16},{28,20},{1,9},{5... | collective-permute-start | bytes 405512 | tf_op jit(solution)/shard_map/ppermute | solution.py:372
  14.3 8.1 %collective-permute-start.2 = (bf16[272,128]{1,0:T(8,128)(2,1)S(1)}, bf16[272,128]{1,0:T(8,128)(2,1)S(1)}, u32[]{:S(2)}, u32[]{:S(2)}) collective-permute-start(bf16[272,128]{1,0:T(8,128)(2,1)S(1)} %get-tuple-element.37), channel_id=1, source_target_pairs={{0,16},{4,20},{8,24},{12,28},{16,0},{20,4},{24,8},{28,12},{1,17},{... | collective-permute-start | bytes 208904 | tf_op jit(solution)/shard_map/ppermute | solution.py:372
  17.2 5.2 %collective-permute-start.3 = (bf16[256,128]{1,0:T(8,128)(2,1)S(1)}, bf16[256,128]{1,0:T(8,128)(2,1)S(1)}, u32[]{:S(2)}, u32[]{:S(2)}) collective-permute-start(bf16[256,128]{1,0:T(8,128)(2,1)S(1)} %get-tuple-element.38), channel_id=1, source_target_pairs={{0,16},{4,20},{8,24},{12,28},{16,0},{20,4},{24,8},{28,12},{1,17},{... | collective-permute-start | bytes 196616 | tf_op jit(solution)/shard_map/ppermute | solution.py:372
  21.1 2.5 %copy-start.1 = (bf16[128,2048]{1,0:T(8,128)(2,1)S(1)}, bf16[128,2048]{1,0:T(8,128)(2,1)}, u32[]{:S(2)}) copy-start(bf16[128,2048]{1,0:T(8,128)(2,1)} %refs_0_.1) | copy-start | bytes 1572868
  23.6 14.4 %collective-permute-start.4 = (bf16[256,2048]{1,0:T(8,128)(2,1)S(1)}, bf16[256,2048]{1,0:T(8,128)(2,1)S(1)}, u32[]{:S(2)}, u32[]{:S(2)}) collective-permute-start(bf16[256,2048]{1,0:T(8,128)(2,1)S(1)} %get-tuple-element.40), channel_id=1, source_target_pairs={{0,1},{1,0},{2,3},{3,2},{4,5},{5,4},{6,7},{7,6},{8,9},{9,8},{10,11... | collective-permute-start | bytes 3145736 | tf_op jit(solution)/shard_map/ppermute | solution.py:372
  23.6 14.3 %collective-permute-start.7 = (bf16[128,2048]{1,0:T(8,128)(2,1)S(1)}, bf16[128,2048]{1,0:T(8,128)(2,1)S(1)}, u32[]{:S(2)}, u32[]{:S(2)}) collective-permute-start(bf16[128,2048]{1,0:T(8,128)(2,1)S(1)} %copy-done.1), channel_id=1, source_target_pairs={{0,2},{1,3},{2,0},{3,1},{4,6},{5,7},{6,4},{7,5},{8,10},{9,11},{10,... | collective-permute-start | bytes 1572872 | tf_op jit(solution)/shard_map/ppermute | solution.py:372
  25.2 15.4 %collective-permute-start.6 = (bf16[128,2048]{1,0:T(8,128)(2,1)S(1)}, bf16[128,2048]{1,0:T(8,128)(2,1)S(1)}, u32[]{:S(2)}, u32[]{:S(2)}) collective-permute-start(bf16[128,2048]{1,0:T(8,128)(2,1)S(1)} %copy-done.1), channel_id=1, source_target_pairs={{0,1},{1,0},{2,3},{3,2},{4,5},{5,4},{6,7},{7,6},{8,9},{9,8},{10,11... | collective-permute-start | bytes 1572872 | tf_op jit(solution)/shard_map/ppermute | solution.py:372
  38.0 3.4 %collective-permute-start.8 = (bf16[128,2048]{1,0:T(8,128)(2,1)S(1)}, bf16[128,2048]{1,0:T(8,128)(2,1)S(1)}, u32[]{:S(2)}, u32[]{:S(2)}) collective-permute-start(bf16[128,2048]{1,0:T(8,128)(2,1)S(1)} %collective-permute-done.7.refs_0_), channel_id=1, source_target_pairs={{0,1},{1,0},{2,3},{3,2},{4,5},{5,4},{6,7},{7,6},{8,9},{9,8},{10,11... | collective-permute-start | bytes 1572872 | tf_op jit(solution)/shard_map/ppermute | solution.py:372
  39.1 25.2 %collective-permute-start.5 = (bf16[128,2048]{1,0:T(8,128)(2,1)S(1)}, bf16[128,2048]{1,0:T(8,128)(2,1)S(1)}, u32[]{:S(2)}, u32[]{:S(2)}) collective-permute-start(bf16[128,2048]{1,0:T(8,128)(2,1)S(1)} %get-tuple-element.42), channel_id=1, source_target_pairs={{0,2},{1,3},{2,0},{3,1},{4,6},{5,7},{6,4},{7,5},{8,10},{9,11},{10,... | collective-permute-start | bytes 1572872 | tf_op jit(solution)/shard_map/ppermute | solution.py:372
  43.5 5.8 %collective-permute-start.9 = (bf16[528,128]{1,0:T(8,128)(2,1)S(1)}, bf16[528,128]{1,0:T(8,128)(2,1)S(1)}, u32[]{:S(2)}, u32[]{:S(2)}) collective-permute-start(bf16[528,128]{1,0:T(8,128)(2,1)S(1)} %shard_map.106.refs_0_), channel_id=1, source_target_pairs={{0,4},{4,0},{8,12},{12,8},{16,20},{20,16},{24,28},{28,24},{1,5},{5... | collective-permute-start | bytes 405512 | tf_op jit(solution)/shard_map/ppermute | solution.py:372
  49.3 5.1 %collective-permute-start.10 = (bf16[528,128]{1,0:T(8,128)(2,1)S(1)}, bf16[528,128]{1,0:T(8,128)(2,1)S(1)}, u32[]{:S(2)}, u32[]{:S(2)}) collective-permute-start(bf16[528,128]{1,0:T(8,128)(2,1)S(1)} %shard_map.107), channel_id=1, source_target_pairs={{0,8},{4,12},{8,0},{12,4},{16,24},{20,28},{24,16},{28,20},{1,9},{5... | collective-permute-start | bytes 405512 | tf_op jit(solution)/shard_map/ppermute | solution.py:372
  54.4 8.0 %collective-permute-start.11 = (bf16[272,128]{1,0:T(8,128)(2,1)S(1)}, bf16[272,128]{1,0:T(8,128)(2,1)S(1)}, u32[]{:S(2)}, u32[]{:S(2)}) collective-permute-start(bf16[272,128]{1,0:T(8,128)(2,1)S(1)} %get-tuple-element.52), channel_id=1, source_target_pairs={{0,16},{4,20},{8,24},{12,28},{16,0},{20,4},{24,8},{28,12},{1,17},{... | collective-permute-start | bytes 208904 | tf_op jit(solution)/shard_map/ppermute | solution.py:372
  56.3 6.7 %collective-permute-start.12 = (bf16[256,128]{1,0:T(8,128)(2,1)S(1)}, bf16[256,128]{1,0:T(8,128)(2,1)S(1)}, u32[]{:S(2)}, u32[]{:S(2)}) collective-permute-start(bf16[256,128]{1,0:T(8,128)(2,1)S(1)} %get-tuple-element.53), channel_id=1, source_target_pairs={{0,16},{4,20},{8,24},{12,28},{16,0},{20,4},{24,8},{28,12},{1,17},{... | collective-permute-start | bytes 196616 | tf_op jit(solution)/shard_map/ppermute | solution.py:372

commit v5 on v4

--- a/solution.py
+++ b/solution.py
@@ -53,6 +53,10 @@
 
 def cols(h):
     return slice(h * HD, (h + 1) * HD)
+
+
+def pair(h):
+    return slice(2 * h * HD, 2 * (h + 1) * HD)
 
 
 def call(body, outs, specs, out_specs=None, scratch=(), flops=1 << 28, vmem=24, alias=None):
@@ -108,7 +112,7 @@
     o_ref[:PAD, :] = pad_rows(sums)
 
 
-def load_query_body(heads, q_hbm, beta_hbm, q_ref, qt_ref, gate_ref, beta_ref, sems):
+def load_query_body(heads, q_hbm, beta_hbm, q_ref, qf_ref, qs_ref, qt_ref, gate_ref, beta_ref, sems):
     rows = q_ref.shape[0] // heads
     beta_copy = pltpu.make_async_copy(beta_hbm, beta_ref, sems.at[heads])
     beta_copy.start()
@@ -122,8 +126,11 @@
     for copy in copies:
         copy.wait()
     for h in range(heads):
-        both = side(*split(feat(q_ref[:, cols(h)].astype(f32))))
-        qt_ref[2 * h * HD : 2 * (h + 1) * HD, :] = both.T
+        qf = feat(q_ref[:, cols(h)].astype(f32))
+        both = side(*split(qf))
+        qf_ref[:, cols(h)] = qf
+        qs_ref[:, pair(h)] = both
+        qt_ref[pair(h), :] = both.T
 
 
 def add_body(count, *refs):
@@ -151,8 +158,9 @@
     return state
 
 
-def read_memory(qf, matrix, msum):
-    numer = twofold(qf, matrix)
+def read_memory(qf, qs, matrix, msum):
+    both = side(*split(matrix))
+    numer = halves(dot(qs, jnp.concatenate([both, both], 0), 1, 0))
     r = 1.0 / (jnp.sum(qf * msum, 1, keepdims=True) + 1.0)
     return numer * r, r
 
@@ -200,35 +208,39 @@
             g_ref[pl.ds(spot, rows), :] = grad[i * rows : (i + 1) * rows, :]
 
 
-def segment_memory_grad(h, q_ref, qt_ref, g_ref, gate_ref, matrix, msum):
-    qf = feat(q_ref[:, cols(h)].astype(f32))
-    mem_out, r = read_memory(qf, matrix, msum)
+def segment_memory_grad(h, qf_ref, qs_ref, qt_ref, g_ref, gate_ref, matrix, msum):
+    qf = qf_ref[:, cols(h)]
+    mem_out, r = read_memory(qf, qs_ref[:, pair(h)], matrix, msum)
     gmem = gate_ref[h : h + 1, :] * g_ref[:, cols(h)].astype(f32)
     gden = -jnp.sum(gmem * mem_out, 1, keepdims=True) * r
-    both = halves(dot(qt_ref[2 * h * HD : 2 * (h + 1) * HD, :], side(*split(gmem * r)), 1, 0))
+    both = halves(dot(qt_ref[pair(h), :], side(*split(gmem * r)), 1, 0))
     return (both[:HD] + both[HD:]).astype(bf16), jnp.sum(gden * qf, 0, keepdims=True)
 
 
 def memory_grad_first_body(group, count, order, steps, *refs):
-    grads, (q_ref, qt_ref, gate_ref) = refs[: len(order)], refs[len(order) : len(order) + 3]
-    recvs = refs[len(order) + 3 : len(order) + 3 + steps] + (None,)
+    grads, (qf_ref, qs_ref, qt_ref, gate_ref) = refs[: len(order)], refs[len(order) : len(order) + 4]
+    recvs = refs[len(order) + 4 : len(order) + 4 + steps] + (None,)
     o_ref, g_ref = refs[-2:]
     gather_grad(count, order, grads, g_ref)
     sums = scan_state(False, recvs, slice(0, PAD))
     rows = []
     for h in group:
         matrix = scan_state(False, recvs, rows_of(h))
-        o_ref[rows_of(h), :], row = segment_memory_grad(h, q_ref, qt_ref, g_ref, gate_ref, matrix, sums[h : h + 1, :])
+        o_ref[rows_of(h), :], row = segment_memory_grad(
+            h, qf_ref, qs_ref, qt_ref, g_ref, gate_ref, matrix, sums[h : h + 1, :]
+        )
         rows.append(row)
     o_ref[:PAD, :] = jnp.concatenate(rows + [jnp.zeros((PAD - len(rows), HD), f32)], 0).astype(bf16)
 
 
-def memory_grad_second_body(first, group, first_ref, q_ref, qt_ref, gate_ref, g_ref, mem_ref, o_ref):
+def memory_grad_second_body(first, group, first_ref, qf_ref, qs_ref, qt_ref, gate_ref, g_ref, mem_ref, o_ref):
     cut = first_ref.shape[0]
     o_ref[:cut, :] = first_ref[...]
     rows = []
     for h in group:
-        o_ref[rows_of(h), :], row = segment_memory_grad(h, q_ref, qt_ref, g_ref, gate_ref, *memory_of(mem_ref, h))
+        o_ref[rows_of(h), :], row = segment_memory_grad(
+            h, qf_ref, qs_ref, qt_ref, g_ref, gate_ref, *memory_of(mem_ref, h)
+        )
         rows.append(row)
     head = first_ref[:PAD, :].astype(f32)
     tail = [jnp.zeros((PAD - first - len(rows), HD), f32)]
@@ -245,30 +257,32 @@
     return out
 
 
-def mixed_rows(heads, count, masks, q_ref, mem_ref, lo_ref, gate_ref, mix_ref):
+def mixed_rows(heads, count, masks, qf_ref, qs_ref, mem_ref, lo_ref, gate_ref, mix_ref):
     place = lax.axis_index("tp")
-    rows = q_ref.shape[0] // count
+    rows = qf_ref.shape[0] // count
     for i, m in enumerate(masks):
         spot = pl.multiple_of(flipped(place, m, count) * rows, rows)
         for h in range(heads):
-            qf = feat(q_ref[pl.ds(spot, rows), cols(h)].astype(f32))
-            mem_out = read_memory(qf, *memory_of(mem_ref, h))[0]
+            qf, qs = qf_ref[pl.ds(spot, rows), cols(h)], qs_ref[pl.ds(spot, rows), pair(h)]
+            mem_out = read_memory(qf, qs, *memory_of(mem_ref, h))[0]
             g = gate_ref[h : h + 1, :]
             x = g * mem_out + (1.0 - g) * lo_ref[pl.ds(spot, rows), cols(h)]
             mix_ref[i * rows : (i + 1) * rows, cols(h)] = x.astype(bf16)
 
 
-def output_send_body(heads, count, masks, steps, q_ref, lo_ref, gate_ref, w_ref, *refs):
+def output_send_body(heads, count, masks, steps, qf_ref, qs_ref, lo_ref, gate_ref, w_ref, *refs):
     recvs, (mem_ref, send_ref, mix_ref) = refs[:steps], refs[steps:]
     cut = recvs[-2].shape[0]
     for rows in (slice(0, cut), slice(cut, mem_ref.shape[0])):
         mem_ref[rows, :] = scan_state(False, recvs, rows)
-    mixed_rows(heads, count, masks, q_ref, mem_ref, lo_ref, gate_ref, mix_ref)
+    mixed_rows(heads, count, masks, qf_ref, qs_ref, mem_ref, lo_ref, gate_ref, mix_ref)
     send_ref[...] = dot(mix_ref[...], w_ref[...], 1, 0).astype(bf16)
 
 
-def output_keep_body(heads, count, masks, q_ref, mem_ref, lo_ref, gate_ref, w_ref, recv_ref, send_ref, keep_ref, mix_ref):
-    mixed_rows(heads, count, masks, q_ref, mem_ref, lo_ref, gate_ref, mix_ref)
+def output_keep_body(
+    heads, count, masks, qf_ref, qs_ref, mem_ref, lo_ref, gate_ref, w_ref, recv_ref, send_ref, keep_ref, mix_ref
+):
+    mixed_rows(heads, count, masks, qf_ref, qs_ref, mem_ref, lo_ref, gate_ref, mix_ref)
     total = dot(mix_ref[...], w_ref[...], 1, 0) + recv_ref[...].astype(f32)
     half = send_ref.shape[0]
     send_ref[...] = total[:half].astype(bf16)
@@ -288,7 +302,9 @@
         copy.wait()
 
 
-def local_backward_body(group, block, q_ref, k_ref, v_ref, g_ref, mem_ref, gate_ref, *refs):
+def local_backward_body(
+    group, block, q_ref, qf_ref, qs_ref, k_ref, v_ref, g_ref, mem_ref, gate_ref, *refs
+):
     gq_ref, gk_ref, gv_ref = refs
     blocks = q_ref.shape[0] // block
     for n, h in enumerate(group):
@@ -318,9 +334,8 @@
             gk_ref[i * block : (i + 1) * block, cols(n)] = gk[i]
             gv_ref[i * block : (i + 1) * block, cols(n)] = gv[i]
         qx = q_ref[:, cols(h)].astype(f32)
-        qf = feat(qx)
         matrix, msum = memory_of(mem_ref, h)
-        mem_out, r = read_memory(qf, matrix, msum)
+        mem_out, r = read_memory(qf_ref[:, cols(h)], qs_ref[:, pair(h)], matrix, msum)
         gmem = g * g_ref[:, cols(h)].astype(f32)
         gden = -jnp.sum(gmem * mem_out, 1, keepdims=True) * r
         gqf = twofold(gmem * r, matrix, True) + gden * msum
@@ -424,9 +439,9 @@
         [hbm] * 2,
         scratch=[pltpu.SemaphoreType.DMA((2, heads))],
     )(*in_hbm(keys, values))
-    query, query_t, gates = call(
+    query, feats, feats_s, feats_t, gates = call(
         functools.partial(load_query_body, heads),
-        [(full, bf16), ((2 * width, length), bf16), ((-(-heads // 8) * 8, HD), f32)],
+        [(full, bf16), (full, f32), ((length, 2 * width), bf16), ((2 * width, length), bf16), ((-(-heads // 8) * 8, HD), f32)],
         [hbm] * 2,
         scratch=[pltpu.SMEM((heads,), f32), pltpu.SemaphoreType.DMA((heads + 1,))],
         flops=1 << 16,
@@ -469,27 +484,27 @@
     part, grad = call(
         functools.partial(memory_grad_first_body, groups[0], tp, order, steps - 1),
         [((cut, HD), bf16), (full, bf16)],
-        [VM] * (len(order) + 2 + steps),
-    )(*grads, query, query_t, gates, *fwd[:-1])
+        [VM] * (len(order) + 3 + steps),
+    )(*grads, feats, feats_s, feats_t, gates, *fwd[:-1])
     memory, send = call(
         functools.partial(output_send_body, heads, tp, places[:half], steps),
         [(packed, f32), ((length // 2, model), bf16)],
-        [VM] * (4 + steps),
+        [VM] * (5 + steps),
         scratch=[pltpu.VMEM((length // 2, width), bf16)],
-    )(query, local_out, gates, out_weight, *fwd)
+    )(feats, feats_s, local_out, gates, out_weight, *fwd)
     recv = swap(send, "tp", 1)
     memory_grad = call(
-        functools.partial(memory_grad_second_body, first, groups[1]), [(packed, bf16)], [VM] * 6
-    )(part, query, query_t, gates, grad, memory)[0]
+        functools.partial(memory_grad_second_body, first, groups[1]), [(packed, bf16)], [VM] * 7
+    )(part, feats, feats_s, feats_t, gates, grad, memory)[0]
     bwd = scan(memory_grad, "seq", cut)
 
     quarter = length // 4
     send, keep = call(
         functools.partial(output_keep_body, heads, tp, places[half:]),
         [((quarter, model), bf16), ((quarter, model), f32)],
-        [VM] * 6,
+        [VM] * 7,
         scratch=[pltpu.VMEM((length // 2, width), bf16)],
-    )(query, memory, local_out, gates, out_weight, recv)
+    )(feats, feats_s, memory, local_out, gates, out_weight, recv)
     bit = 2
     while 2 * bit < tp:
         total = keep + swap(send, "tp", bit).astype(f32)
@@ -504,8 +519,8 @@
             call(
                 functools.partial(local_backward_body, group, block),
                 [(part, bf16), (part, f32), (part, f32)],
-                [VM] * 6,
-            )(query, keys, values, grad, memory, gates)
+                [VM] * 8,
+            )(query, feats, feats_s, keys, values, grad, memory, gates)
         )
     own_rows = (length // tp, model)
     output, grad_query = call(

time: 65.5 us -> 65 us (level)
  no operation moved by 1% of the time
where the time goes in v5:
time: 65 us; the launch traced here: 64.9 us
  waiting for transfers between devices  28.3 us (44%)
  Pallas kernels  18.3 us (28%)
  starting transfers between devices  17.5 us (27%)
  between operations  0.8 us (1%)
    ppermute x13, waiting for transfers between devices, swap(): return lax.ppermute(x, axis, [(i, i ^ bit) for i in range(count)])  28.3 us
    ppermute x13, starting transfers between devices, swap(): return lax.ppermute(x, axis, [(i, i ^ bit) for i in range(count)])  17.5 us
    pallas_call x2, Pallas kernels, local(): call(functools.partial(local_backward_body, group, block), [(part, bf16),...  4.83 us
    pallas_call x1, Pallas kernels, local(): call(functools.partial(local_forward_body, heads, block), [(full, f32)],...  2.21 us
    pallas_call x1, Pallas kernels, local(): call(functools.partial(own_memory_body, heads), [(packed, bf16), (full, b...  1.88 us
    pallas_call x1, Pallas kernels, local(): call(functools.partial(load_query_body, heads), [(full, bf16), (full, f32...  1.61 us
    pallas_call x2, Pallas kernels, local(): call(grad_mixed_body, [((rows, width), bf16)], [VM] * (len(masks) + 1))  1.48 us
  transfers between devices with their start and end apart: 13, of which 6 were waited for; matrix products, arithmetic and copies ran while one was open for 0% of the time, Pallas kernels for 22%

profile of v5, /device:TPU:0, one launch (start us, length us, event | category | flops | bytes accessed | tf_op | source)
XLA Modules:
  0.0 64.9 jit_solution(10886598739658932000)
XLA Ops:
  0.6 1.9 %shard_map.94 = (bf16[528,128]{1,0:T(8,128)(2,1)S(1)}, bf16[512,512]{1,0:T(8,128)(2,1)S(1)}, bf16[512,512]{1,0:T(8,128)(2,1)S(1)}) custom-call(bf16[512,512]{1,0:T(8,128)(2,1)} %k_hbm.1, bf16[512,512]{1,0:T(8,128)(2,1)} %v_hbm.1), custom_call_target="tpu_custom_call" | custom-call | flops 268435456 | bytes 1048576 | tf_op jit(solution)/shard_map/pallas_call | solution.py:436
  2.5 3.0 %collective-permute-start = (bf16[528,128]{1,0:T(8,128)(2,1)S(1)}, bf16[528,128]{1,0:T(8,128)(2,1)S(1)}, u32[]{:S(2)}, u32[]{:S(2)}) collective-permute-start(bf16[528,128]{1,0:T(8,128)(2,1)S(1)} %get-tuple-element.40.refs_0_), channel_id=1, source_target_pairs={{0,4},{4,0},{8,12},{12,8},{16,20},{20,16},{24,28},{28,24},{1,5},{5... | collective-permute-start | bytes 405512 | tf_op jit(solution)/shard_map/ppermute | solution.py:387
  5.6 3.6 %collective-permute-done.refs_1_.refs_0_.refs_6_ = bf16[528,128]{1,0:T(8,128)(2,1)S(1)} collective-permute-done((bf16[528,128]{1,0:T(8,128)(2,1)S(1)}, bf16[528,128]{1,0:T(8,128)(2,1)S(1)}, u32[]{:S(2)}, u32[]{:S(2)}) %collective-permute-start) | collective-permute-done | bytes 135200 | tf_op jit(solution)/shard_map/ppermute | solution.py:387
  9.2 1.9 %collective-permute-start.1 = (bf16[528,128]{1,0:T(8,128)(2,1)S(1)}, bf16[528,128]{1,0:T(8,128)(2,1)S(1)}, u32[]{:S(2)}, u32[]{:S(2)}) collective-permute-start(bf16[528,128]{1,0:T(8,128)(2,1)S(1)} %shard_map.96), channel_id=1, source_target_pairs={{0,8},{4,12},{8,0},{12,4},{16,24},{20,28},{24,16},{28,20},{1,9},{5... | collective-permute-start | bytes 405512 | tf_op jit(solution)/shard_map/ppermute | solution.py:387
  11.1 3.2 %collective-permute-done.1.refs_2_.refs_1_.refs_7_ = bf16[528,128]{1,0:T(8,128)(2,1)S(1)} collective-permute-done((bf16[528,128]{1,0:T(8,128)(2,1)S(1)}, bf16[528,128]{1,0:T(8,128)(2,1)S(1)}, u32[]{:S(2)}, u32[]{:S(2)}) %collective-permute-start.1) | collective-permute-done | bytes 135200 | tf_op jit(solution)/shard_map/ppermute | solution.py:387
  14.3 2.9 %collective-permute-start.2 = (bf16[272,128]{1,0:T(8,128)(2,1)S(1)}, bf16[272,128]{1,0:T(8,128)(2,1)S(1)}, u32[]{:S(2)}, u32[]{:S(2)}) collective-permute-start(bf16[272,128]{1,0:T(8,128)(2,1)S(1)} %get-tuple-element.41), channel_id=1, source_target_pairs={{0,16},{4,20},{8,24},{12,28},{16,0},{20,4},{24,8},{28,12},{1,17},{... | collective-permute-start | bytes 208904 | tf_op jit(solution)/shard_map/ppermute | solution.py:387
  17.3 1.6 %shard_map.93 = (bf16[512,512]{1,0:T(8,128)(2,1)S(1)}, f32[512,512]{1,0:T(8,128)S(1)}, bf16[512,1024]{1,0:T(8,128)(2,1)S(1)}, bf16[1024,512]{1,0:T(8,128)(2,1)S(1)}, f32[8,128]{1,0:T(8,128)S(1)}) custom-call(bf16[512,512]{1,0:T(8,128)(2,1)} %q_hbm.1, f32[4]{0:T(128)} %beta_hbm.1), custom_call_target="tpu_custom_call" | custom-call | flops 65536 | bytes 1048576 | tf_op jit(solution)/shard_map/pallas_call | solution.py:442
  18.9 2.2 %shard_map.95.lo_ref = f32[512,512]{1,0:T(8,128)S(1)} custom-call(bf16[512,512]{1,0:T(8,128)(2,1)S(1)} %get-tuple-element.36.q_ref, bf16[512,512]{1,0:T(8,128)(2,1)S(1)} %get-tuple-element.37.k_ref.refs_0_, bf16[512,512]{1,0:T(8,128)(2,1)S(1)} %get-tuple-element.38.v_ref.refs_1_), custom_call_target="tpu_custom_call" | custom-call | flops 268435456 | bytes 1048576 | tf_op jit(solution)/shard_map/pallas_call | solution.py:468
  21.1 1.3 %collective-permute-done.3.refs_3_ = bf16[256,128]{1,0:T(8,128)(2,1)S(1)} collective-permute-done((bf16[256,128]{1,0:T(8,128)(2,1)S(1)}, bf16[256,128]{1,0:T(8,128)(2,1)S(1)}, u32[]{:S(2)}, u32[]{:S(2)}) %collective-permute-start.3) | collective-permute-done | bytes 65568 | tf_op jit(solution)/shard_map/ppermute | solution.py:387
  22.4 1.1 %shard_map.98 = (f32[528,128]{1,0:T(8,128)S(1)}, bf16[256,2048]{1,0:T(8,128)(2,1)S(1)}) custom-call(f32[512,512]{1,0:T(8,128)S(1)} %get-tuple-element.34.qf_ref.refs_2_, bf16[512,1024]{1,0:T(8,128)(2,1)S(1)} %get-tuple-element.35.qs_ref.refs_3_, f32[512,512]{1,0:T(8,128)S(1)} %shard_map.95.lo_ref, f32[8,128]{1,0:T(8,128)S(1)} %get-tuple-element.39.gate_ref.refs_5_, ...), custom_call_target="tpu_custom_call" | custom-call | flops 268435456 | bytes 1048576 | tf_op jit(solution)/shard_map/pallas_call | solution.py:489
  23.6 1.6 %collective-permute-start.7 = (bf16[128,2048]{1,0:T(8,128)(2,1)S(1)}, bf16[128,2048]{1,0:T(8,128)(2,1)S(1)}, u32[]{:S(2)}, u32[]{:S(2)}) collective-permute-start(bf16[128,2048]{1,0:T(8,128)(2,1)S(1)} %copy-done.1), channel_id=1, source_target_pairs={{0,2},{1,3},{2,0},{3,1},{4,6},{5,7},{6,4},{7,5},{8,10},{9,11},{10,... | collective-permute-start | bytes 1572872 | tf_op jit(solution)/shard_map/ppermute | solution.py:387
  25.3 12.6 %collective-permute-done.7.refs_0_ = bf16[128,2048]{1,0:T(8,128)(2,1)S(1)} collective-permute-done((bf16[128,2048]{1,0:T(8,128)(2,1)S(1)}, bf16[128,2048]{1,0:T(8,128)(2,1)S(1)}, u32[]{:S(2)}, u32[]{:S(2)}) %collective-permute-start.7) | collective-permute-done | bytes 524320 | tf_op jit(solution)/shard_map/ppermute | solution.py:387
  37.9 1.0 %shard_map.99 = (bf16[128,2048]{1,0:T(8,128)(2,1)S(1)}, f32[128,2048]{1,0:T(8,128)S(1)}) custom-call(f32[512,512]{1,0:T(8,128)S(1)} %get-tuple-element.34.qf_ref.refs_2_, bf16[512,1024]{1,0:T(8,128)(2,1)S(1)} %get-tuple-element.35.qs_ref.refs_3_, f32[528,128]{1,0:T(8,128)S(1)} %get-tuple-element.43.mem_ref, f32[512,512]{1,0:T(8,128)S(1)} %shard_map.95.lo_ref, ...), custom_call_target="tpu_custom_call" | custom-call | flops 268435456 | bytes 1048576 | tf_op jit(solution)/shard_map/pallas_call | solution.py:502
  38.9 1.6 %collective-permute-start.5 = (bf16[128,2048]{1,0:T(8,128)(2,1)S(1)}, bf16[128,2048]{1,0:T(8,128)(2,1)S(1)}, u32[]{:S(2)}, u32[]{:S(2)}) collective-permute-start(bf16[128,2048]{1,0:T(8,128)(2,1)S(1)} %get-tuple-element.46), channel_id=1, source_target_pairs={{0,2},{1,3},{2,0},{3,1},{4,6},{5,7},{6,4},{7,5},{8,10},{9,11},{10,... | collective-permute-start | bytes 1572872 | tf_op jit(solution)/shard_map/ppermute | solution.py:387
  43.2 1.6 %collective-permute-start.9 = (bf16[528,128]{1,0:T(8,128)(2,1)S(1)}, bf16[528,128]{1,0:T(8,128)(2,1)S(1)}, u32[]{:S(2)}, u32[]{:S(2)}) collective-permute-start(bf16[528,128]{1,0:T(8,128)(2,1)S(1)} %shard_map.106.refs_0_), channel_id=1, source_target_pairs={{0,4},{4,0},{8,12},{12,8},{16,20},{20,16},{24,28},{28,24},{1,5},{5... | collective-permute-start | bytes 405512 | tf_op jit(solution)/shard_map/ppermute | solution.py:387
  44.8 4.2 %collective-permute-done.9.refs_1_.refs_4_ = bf16[528,128]{1,0:T(8,128)(2,1)S(1)} collective-permute-done((bf16[528,128]{1,0:T(8,128)(2,1)S(1)}, bf16[528,128]{1,0:T(8,128)(2,1)S(1)}, u32[]{:S(2)}, u32[]{:S(2)}) %collective-permute-start.9) | collective-permute-done | bytes 135200 | tf_op jit(solution)/shard_map/ppermute | solution.py:387
  49.0 1.7 %collective-permute-start.10 = (bf16[528,128]{1,0:T(8,128)(2,1)S(1)}, bf16[528,128]{1,0:T(8,128)(2,1)S(1)}, u32[]{:S(2)}, u32[]{:S(2)}) collective-permute-start(bf16[528,128]{1,0:T(8,128)(2,1)S(1)} %shard_map.107), channel_id=1, source_target_pairs={{0,8},{4,12},{8,0},{12,4},{16,24},{20,28},{24,16},{28,20},{1,9},{5... | collective-permute-start | bytes 405512 | tf_op jit(solution)/shard_map/ppermute | solution.py:387
  50.7 3.4 %collective-permute-done.10.refs_2_.refs_5_ = bf16[528,128]{1,0:T(8,128)(2,1)S(1)} collective-permute-done((bf16[528,128]{1,0:T(8,128)(2,1)S(1)}, bf16[528,128]{1,0:T(8,128)(2,1)S(1)}, u32[]{:S(2)}, u32[]{:S(2)}) %collective-permute-start.10) | collective-permute-done | bytes 135200 | tf_op jit(solution)/shard_map/ppermute | solution.py:387
  54.2 1.8 %collective-permute-start.11 = (bf16[272,128]{1,0:T(8,128)(2,1)S(1)}, bf16[272,128]{1,0:T(8,128)(2,1)S(1)}, u32[]{:S(2)}, u32[]{:S(2)}) collective-permute-start(bf16[272,128]{1,0:T(8,128)(2,1)S(1)} %get-tuple-element.56), channel_id=1, source_target_pairs={{0,16},{4,20},{8,24},{12,28},{16,0},{20,4},{24,8},{28,12},{1,17},{... | collective-permute-start | bytes 208904 | tf_op jit(solution)/shard_map/ppermute | solution.py:387
  56.0 1.1 %collective-permute-start.12 = (bf16[256,128]{1,0:T(8,128)(2,1)S(1)}, bf16[256,128]{1,0:T(8,128)(2,1)S(1)}, u32[]{:S(2)}, u32[]{:S(2)}) collective-permute-start(bf16[256,128]{1,0:T(8,128)(2,1)S(1)} %get-tuple-element.57), channel_id=1, source_target_pairs={{0,16},{4,20},{8,24},{12,28},{16,0},{20,4},{24,8},{28,12},{1,17},{... | collective-permute-start | bytes 196616 | tf_op jit(solution)/shard_map/ppermute | solution.py:387
  57.1 2.4 %shard_map.104 = (bf16[512,256]{1,0:T(8,128)(2,1)S(1)}, f32[512,256]{1,0:T(8,128)S(1)}, f32[512,256]{1,0:T(8,128)S(1)}) custom-call(bf16[512,512]{1,0:T(8,128)(2,1)S(1)} %get-tuple-element.36.q_ref, f32[512,512]{1,0:T(8,128)S(1)} %get-tuple-element.34.qf_ref.refs_2_, bf16[512,1024]{1,0:T(8,128)(2,1)S(1)} %get-tuple-element.35.qs_ref.refs_3_, ...), custom_call_target="tpu_custom_call" | custom-call | flops 268435456 | bytes 1048576 | tf_op jit(solution)/shard_map/pallas_call | solution.py:519
  59.6 2.4 %shard_map.103 = (bf16[512,256]{1,0:T(8,128)(2,1)S(1)}, f32[512,256]{1,0:T(8,128)S(1)}, f32[512,256]{1,0:T(8,128)S(1)}) custom-call(bf16[512,512]{1,0:T(8,128)(2,1)S(1)} %get-tuple-element.36.q_ref, f32[512,512]{1,0:T(8,128)S(1)} %get-tuple-element.34.qf_ref.refs_2_, bf16[512,1024]{1,0:T(8,128)(2,1)S(1)} %get-tuple-element.35.qs_ref.refs_3_, ...), custom_call_target="tpu_custom_call" | custom-call | flops 268435456 | bytes 1048576 | tf_op jit(solution)/shard_map/pallas_call | solution.py:519
  62.5 1.3 %shard_map.110 = (bf16[512,512]{1,0:T(8,128)(2,1)}, bf16[512,512]{1,0:T(8,128)(2,1)}) custom-call(bf16[512,512]{1,0:T(8,128)(2,1)S(1)} %get-tuple-element.37.k_ref.refs_0_, bf16[512,512]{1,0:T(8,128)(2,1)S(1)} %get-tuple-element.38.v_ref.refs_1_, f32[512,256]{1,0:T(8,128)S(1)} %get-tuple-element.53.refs_2_, f32[512,256]{1,0:T(8,128)S(1)} %get-tuple-element.54.refs_3_, ...), custom_call_target="tpu_custom_call" | custom-call | flops 268435456 | bytes 1048576 | tf_op jit(solution)/shard_map/pallas_call | solution.py:541
  63.8 1.1 %shard_map.105 = (bf16[128,2048]{1,0:T(8,128)(2,1)}, bf16[512,512]{1,0:T(8,128)(2,1)}) custom-call(f32[128,2048]{1,0:T(8,128)S(1)} %get-tuple-element.45.keep_ref, bf16[128,2048]{1,0:T(8,128)(2,1)S(1)} %collective-permute-done.5.recv_ref, bf16[512,256]{1,0:T(8,128)(2,1)S(1)} %get-tuple-element.49.refs_0_, bf16[512,256]{1,0:T(8,128)(2,1)S(1)} %get-tuple-element.50.refs_1_), custom_call_target="tpu_custom_call" | custom-call | flops 1048576 | bytes 1048576 | tf_op jit(solution)/shard_map/pallas_call | solution.py:526
  (24 shorter events, 3.7 us)
Async XLA Ops:
  2.5 19.9 %copy-start = (bf16[512,2048]{1,0:T(8,128)(2,1)S(1)}, bf16[512,2048]{1,0:T(8,128)(2,1)}, u32[]{:S(2)}) copy-start(bf16[512,2048]{1,0:T(8,128)(2,1)} %refs_2_.3) | copy-start | bytes 6291460
  2.5 6.6 %collective-permute-start = (bf16[528,128]{1,0:T(8,128)(2,1)S(1)}, bf16[528,128]{1,0:T(8,128)(2,1)S(1)}, u32[]{:S(2)}, u32[]{:S(2)}) collective-permute-start(bf16[528,128]{1,0:T(8,128)(2,1)S(1)} %get-tuple-element.40.refs_0_), channel_id=1, source_target_pairs={{0,4},{4,0},{8,12},{12,8},{16,20},{20,16},{24,28},{28,24},{1,5},{5... | collective-permute-start | bytes 405512 | tf_op jit(solution)/shard_map/ppermute | solution.py:387
  9.2 5.1 %collective-permute-start.1 = (bf16[528,128]{1,0:T(8,128)(2,1)S(1)}, bf16[528,128]{1,0:T(8,128)(2,1)S(1)}, u32[]{:S(2)}, u32[]{:S(2)}) collective-permute-start(bf16[528,128]{1,0:T(8,128)(2,1)S(1)} %shard_map.96), channel_id=1, source_target_pairs={{0,8},{4,12},{8,0},{12,4},{16,24},{20,28},{24,16},{28,20},{1,9},{5... | collective-permute-start | bytes 405512 | tf_op jit(solution)/shard_map/ppermute | solution.py:387
  14.3 8.1 %collective-permute-start.2 = (bf16[272,128]{1,0:T(8,128)(2,1)S(1)}, bf16[272,128]{1,0:T(8,128)(2,1)S(1)}, u32[]{:S(2)}, u32[]{:S(2)}) collective-permute-start(bf16[272,128]{1,0:T(8,128)(2,1)S(1)} %get-tuple-element.41), channel_id=1, source_target_pairs={{0,16},{4,20},{8,24},{12,28},{16,0},{20,4},{24,8},{28,12},{1,17},{... | collective-permute-start | bytes 208904 | tf_op jit(solution)/shard_map/ppermute | solution.py:387
  17.2 5.2 %collective-permute-start.3 = (bf16[256,128]{1,0:T(8,128)(2,1)S(1)}, bf16[256,128]{1,0:T(8,128)(2,1)S(1)}, u32[]{:S(2)}, u32[]{:S(2)}) collective-permute-start(bf16[256,128]{1,0:T(8,128)(2,1)S(1)} %get-tuple-element.42), channel_id=1, source_target_pairs={{0,16},{4,20},{8,24},{12,28},{16,0},{20,4},{24,8},{28,12},{1,17},{... | collective-permute-start | bytes 196616 | tf_op jit(solution)/shard_map/ppermute | solution.py:387
  22.4 1.2 %copy-start.1 = (bf16[128,2048]{1,0:T(8,128)(2,1)S(1)}, bf16[128,2048]{1,0:T(8,128)(2,1)}, u32[]{:S(2)}) copy-start(bf16[128,2048]{1,0:T(8,128)(2,1)} %refs_0_.1) | copy-start | bytes 1572868
  23.5 14.4 %collective-permute-start.4 = (bf16[256,2048]{1,0:T(8,128)(2,1)S(1)}, bf16[256,2048]{1,0:T(8,128)(2,1)S(1)}, u32[]{:S(2)}, u32[]{:S(2)}) collective-permute-start(bf16[256,2048]{1,0:T(8,128)(2,1)S(1)} %get-tuple-element.44), channel_id=1, source_target_pairs={{0,1},{1,0},{2,3},{3,2},{4,5},{5,4},{6,7},{7,6},{8,9},{9,8},{10,11... | collective-permute-start | bytes 3145736 | tf_op jit(solution)/shard_map/ppermute | solution.py:387
  23.6 14.3 %collective-permute-start.7 = (bf16[128,2048]{1,0:T(8,128)(2,1)S(1)}, bf16[128,2048]{1,0:T(8,128)(2,1)S(1)}, u32[]{:S(2)}, u32[]{:S(2)}) collective-permute-start(bf16[128,2048]{1,0:T(8,128)(2,1)S(1)} %copy-done.1), channel_id=1, source_target_pairs={{0,2},{1,3},{2,0},{3,1},{4,6},{5,7},{6,4},{7,5},{8,10},{9,11},{10,... | collective-permute-start | bytes 1572872 | tf_op jit(solution)/shard_map/ppermute | solution.py:387
  25.2 15.4 %collective-permute-start.6 = (bf16[128,2048]{1,0:T(8,128)(2,1)S(1)}, bf16[128,2048]{1,0:T(8,128)(2,1)S(1)}, u32[]{:S(2)}, u32[]{:S(2)}) collective-permute-start(bf16[128,2048]{1,0:T(8,128)(2,1)S(1)} %copy-done.1), channel_id=1, source_target_pairs={{0,1},{1,0},{2,3},{3,2},{4,5},{5,4},{6,7},{7,6},{8,9},{9,8},{10,11... | collective-permute-start | bytes 1572872 | tf_op jit(solution)/shard_map/ppermute | solution.py:387
  37.9 3.4 %collective-permute-start.8 = (bf16[128,2048]{1,0:T(8,128)(2,1)S(1)}, bf16[128,2048]{1,0:T(8,128)(2,1)S(1)}, u32[]{:S(2)}, u32[]{:S(2)}) collective-permute-start(bf16[128,2048]{1,0:T(8,128)(2,1)S(1)} %collective-permute-done.7.refs_0_), channel_id=1, source_target_pairs={{0,1},{1,0},{2,3},{3,2},{4,5},{5,4},{6,7},{7,6},{8,9},{9,8},{10,11... | collective-permute-start | bytes 1572872 | tf_op jit(solution)/shard_map/ppermute | solution.py:387
  38.9 24.9 %collective-permute-start.5 = (bf16[128,2048]{1,0:T(8,128)(2,1)S(1)}, bf16[128,2048]{1,0:T(8,128)(2,1)S(1)}, u32[]{:S(2)}, u32[]{:S(2)}) collective-permute-start(bf16[128,2048]{1,0:T(8,128)(2,1)S(1)} %get-tuple-element.46), channel_id=1, source_target_pairs={{0,2},{1,3},{2,0},{3,1},{4,6},{5,7},{6,4},{7,5},{8,10},{9,11},{10,... | collective-permute-start | bytes 1572872 | tf_op jit(solution)/shard_map/ppermute | solution.py:387
  43.2 5.8 %collective-permute-start.9 = (bf16[528,128]{1,0:T(8,128)(2,1)S(1)}, bf16[528,128]{1,0:T(8,128)(2,1)S(1)}, u32[]{:S(2)}, u32[]{:S(2)}) collective-permute-start(bf16[528,128]{1,0:T(8,128)(2,1)S(1)} %shard_map.106.refs_0_), channel_id=1, source_target_pairs={{0,4},{4,0},{8,12},{12,8},{16,20},{20,16},{24,28},{28,24},{1,5},{5... | collective-permute-start | bytes 405512 | tf_op jit(solution)/shard_map/ppermute | solution.py:387
  49.0 5.1 %collective-permute-start.10 = (bf16[528,128]{1,0:T(8,128)(2,1)S(1)}, bf16[528,128]{1,0:T(8,128)(2,1)S(1)}, u32[]{:S(2)}, u32[]{:S(2)}) collective-permute-start(bf16[528,128]{1,0:T(8,128)(2,1)S(1)} %shard_map.107), channel_id=1, source_target_pairs={{0,8},{4,12},{8,0},{12,4},{16,24},{20,28},{24,16},{28,20},{1,9},{5... | collective-permute-start | bytes 405512 | tf_op jit(solution)/shard_map/ppermute | solution.py:387
  54.2 7.8 %collective-permute-start.11 = (bf16[272,128]{1,0:T(8,128)(2,1)S(1)}, bf16[272,128]{1,0:T(8,128)(2,1)S(1)}, u32[]{:S(2)}, u32[]{:S(2)}) collective-permute-start(bf16[272,128]{1,0:T(8,128)(2,1)S(1)} %get-tuple-element.56), channel_id=1, source_target_pairs={{0,16},{4,20},{8,24},{12,28},{16,0},{20,4},{24,8},{28,12},{1,17},{... | collective-permute-start | bytes 208904 | tf_op jit(solution)/shard_map/ppermute | solution.py:387
  56.0 6.5 %collective-permute-start.12 = (bf16[256,128]{1,0:T(8,128)(2,1)S(1)}, bf16[256,128]{1,0:T(8,128)(2,1)S(1)}, u32[]{:S(2)}, u32[]{:S(2)}) collective-permute-start(bf16[256,128]{1,0:T(8,128)(2,1)S(1)} %get-tuple-element.57), channel_id=1, source_target_pairs={{0,16},{4,20},{8,24},{12,28},{16,0},{20,4},{24,8},{28,12},{1,17},{... | collective-permute-start | bytes 196616 | tf_op jit(solution)/shard_map/ppermute | solution.py:387

commit v6 on v5

--- a/solution.py
+++ b/solution.py
@@ -214,31 +214,31 @@
     gmem = gate_ref[h : h + 1, :] * g_ref[:, cols(h)].astype(f32)
     gden = -jnp.sum(gmem * mem_out, 1, keepdims=True) * r
     both = halves(dot(qt_ref[pair(h), :], side(*split(gmem * r)), 1, 0))
-    return (both[:HD] + both[HD:]).astype(bf16), jnp.sum(gden * qf, 0, keepdims=True)
+    return (both[:HD] + both[HD:]).astype(bf16), jnp.sum(gden * qf, 0, keepdims=True), mem_out
 
 
 def memory_grad_first_body(group, count, order, steps, *refs):
     grads, (qf_ref, qs_ref, qt_ref, gate_ref) = refs[: len(order)], refs[len(order) : len(order) + 4]
     recvs = refs[len(order) + 4 : len(order) + 4 + steps] + (None,)
-    o_ref, g_ref = refs[-2:]
+    o_ref, g_ref, out_ref = refs[-3:]
     gather_grad(count, order, grads, g_ref)
     sums = scan_state(False, recvs, slice(0, PAD))
     rows = []
     for h in group:
         matrix = scan_state(False, recvs, rows_of(h))
-        o_ref[rows_of(h), :], row = segment_memory_grad(
+        o_ref[rows_of(h), :], row, out_ref[:, cols(h - group[0])] = segment_memory_grad(
             h, qf_ref, qs_ref, qt_ref, g_ref, gate_ref, matrix, sums[h : h + 1, :]
         )
         rows.append(row)
     o_ref[:PAD, :] = jnp.concatenate(rows + [jnp.zeros((PAD - len(rows), HD), f32)], 0).astype(bf16)
 
 
-def memory_grad_second_body(first, group, first_ref, qf_ref, qs_ref, qt_ref, gate_ref, g_ref, mem_ref, o_ref):
+def memory_grad_second_body(first, group, first_ref, qf_ref, qs_ref, qt_ref, gate_ref, g_ref, mem_ref, o_ref, out_ref):
     cut = first_ref.shape[0]
     o_ref[:cut, :] = first_ref[...]
     rows = []
     for h in group:
-        o_ref[rows_of(h), :], row = segment_memory_grad(
+        o_ref[rows_of(h), :], row, out_ref[:, cols(h - group[0])] = segment_memory_grad(
             h, qf_ref, qs_ref, qt_ref, g_ref, gate_ref, *memory_of(mem_ref, h)
         )
         rows.append(row)
@@ -257,32 +257,38 @@
     return out
 
 
-def mixed_rows(heads, count, masks, qf_ref, qs_ref, mem_ref, lo_ref, gate_ref, mix_ref):
+def mixed_rows(heads, count, masks, qf_ref, qs_ref, mem_ref, lo_ref, gate_ref, mix_ref, known):
     place = lax.axis_index("tp")
     rows = qf_ref.shape[0] // count
     for i, m in enumerate(masks):
         spot = pl.multiple_of(flipped(place, m, count) * rows, rows)
         for h in range(heads):
             qf, qs = qf_ref[pl.ds(spot, rows), cols(h)], qs_ref[pl.ds(spot, rows), pair(h)]
-            mem_out = read_memory(qf, qs, *memory_of(mem_ref, h))[0]
+            if h in known:
+                mem_out = known[h][0][pl.ds(spot, rows), cols(known[h][1])]
+            else:
+                mem_out = read_memory(qf, qs, *memory_of(mem_ref, h))[0]
             g = gate_ref[h : h + 1, :]
             x = g * mem_out + (1.0 - g) * lo_ref[pl.ds(spot, rows), cols(h)]
             mix_ref[i * rows : (i + 1) * rows, cols(h)] = x.astype(bf16)
 
 
-def output_send_body(heads, count, masks, steps, qf_ref, qs_ref, lo_ref, gate_ref, w_ref, *refs):
+def output_send_body(heads, count, masks, steps, qf_ref, qs_ref, lo_ref, gate_ref, w_ref, known_ref, *refs):
+    known = {h: (known_ref, h) for h in range(known_ref.shape[1] // HD)}
     recvs, (mem_ref, send_ref, mix_ref) = refs[:steps], refs[steps:]
     cut = recvs[-2].shape[0]
     for rows in (slice(0, cut), slice(cut, mem_ref.shape[0])):
         mem_ref[rows, :] = scan_state(False, recvs, rows)
-    mixed_rows(heads, count, masks, qf_ref, qs_ref, mem_ref, lo_ref, gate_ref, mix_ref)
+    mixed_rows(heads, count, masks, qf_ref, qs_ref, mem_ref, lo_ref, gate_ref, mix_ref, known)
     send_ref[...] = dot(mix_ref[...], w_ref[...], 1, 0).astype(bf16)
 
 
 def output_keep_body(
-    heads, count, masks, qf_ref, qs_ref, mem_ref, lo_ref, gate_ref, w_ref, recv_ref, send_ref, keep_ref, mix_ref
+    heads, count, masks, qf_ref, qs_ref, mem_ref, lo_ref, gate_ref, w_ref, recv_ref, low_ref, high_ref, send_ref, keep_ref, mix_ref
 ):
-    mixed_rows(heads, count, masks, qf_ref, qs_ref, mem_ref, lo_ref, gate_ref, mix_ref)
+    first = low_ref.shape[1] // HD
+    known = {h: (low_ref, h) if h < first else (high_ref, h - first) for h in range(heads)}
+    mixed_rows(heads, count, masks, qf_ref, qs_ref, mem_ref, lo_ref, gate_ref, mix_ref, known)
     total = dot(mix_ref[...], w_ref[...], 1, 0) + recv_ref[...].astype(f32)
     half = send_ref.shape[0]
     send_ref[...] = total[:half].astype(bf16)
@@ -302,9 +308,7 @@
         copy.wait()
 
 
-def local_backward_body(
-    group, block, q_ref, qf_ref, qs_ref, k_ref, v_ref, g_ref, mem_ref, gate_ref, *refs
-):
+def local_backward_body(group, block, q_ref, qf_ref, qs_ref, k_ref, v_ref, g_ref, mem_ref, gate_ref, *refs):
     gq_ref, gk_ref, gv_ref = refs
     blocks = q_ref.shape[0] // block
     for n, h in enumerate(group):
@@ -481,30 +485,32 @@
     places = [reverse_bits(tp - 1 - i, tp) for i in range(tp)]
     half = tp // 2
     steps = len(fwd)
-    part, grad = call(
+    part, grad, low = call(
         functools.partial(memory_grad_first_body, groups[0], tp, order, steps - 1),
-        [((cut, HD), bf16), (full, bf16)],
+        [((cut, HD), bf16), (full, bf16), ((length, first * HD), f32)],
         [VM] * (len(order) + 3 + steps),
     )(*grads, feats, feats_s, feats_t, gates, *fwd[:-1])
     memory, send = call(
         functools.partial(output_send_body, heads, tp, places[:half], steps),
         [(packed, f32), ((length // 2, model), bf16)],
-        [VM] * (5 + steps),
+        [VM] * (6 + steps),
         scratch=[pltpu.VMEM((length // 2, width), bf16)],
-    )(feats, feats_s, local_out, gates, out_weight, *fwd)
+    )(feats, feats_s, local_out, gates, out_weight, low, *fwd)
     recv = swap(send, "tp", 1)
-    memory_grad = call(
-        functools.partial(memory_grad_second_body, first, groups[1]), [(packed, bf16)], [VM] * 7
-    )(part, feats, feats_s, feats_t, gates, grad, memory)[0]
+    memory_grad, high = call(
+        functools.partial(memory_grad_second_body, first, groups[1]),
+        [(packed, bf16), ((length, len(groups[1]) * HD), f32)],
+        [VM] * 7,
+    )(part, feats, feats_s, feats_t, gates, grad, memory)
     bwd = scan(memory_grad, "seq", cut)
 
     quarter = length // 4
     send, keep = call(
         functools.partial(output_keep_body, heads, tp, places[half:]),
         [((quarter, model), bf16), ((quarter, model), f32)],
-        [VM] * 7,
+        [VM] * 9,
         scratch=[pltpu.VMEM((length // 2, width), bf16)],
-    )(feats, feats_s, memory, local_out, gates, out_weight, recv)
+    )(feats, feats_s, memory, local_out, gates, out_weight, recv, low, high)
     bit = 2
     while 2 * bit < tp:
         total = keep + swap(send, "tp", bit).astype(f32)
@@ -517,9 +523,7 @@
         part = (length, len(group) * HD)
         pieces.append(
             call(
-                functools.partial(local_backward_body, group, block),
-                [(part, bf16), (part, f32), (part, f32)],
-                [VM] * 8,
+                functools.partial(local_backward_body, group, block), [(part, bf16), (part, f32), (part, f32)], [VM] * 8
             )(query, feats, feats_s, keys, values, grad, memory, gates)
         )
     own_rows = (length // tp, model)
@@ -533,9 +537,7 @@
     )(keep, recv, *[piece[0] for piece in pieces])
     part = (length, first * HD)
     early = call(
-        functools.partial(final_first_body, groups[0], len(bwd) - 1),
-        [(part, bf16)] * 2,
-        [VM] * (3 + len(bwd)),
+        functools.partial(final_first_body, groups[0], len(bwd) - 1), [(part, bf16)] * 2, [VM] * (3 + len(bwd))
     )(keys, values, *pieces[0][1:], *bwd[:-1])
     part = (length, len(groups[1]) * HD)
     grad_keys, grad_values = call(

time: 65 us -> 66.9 us (1.029)
  waiting for transfers between devices: 28.3 us -> 30.4 us
    ppermute x13, waiting for transfers between devices: 28.3 us -> 30.4 us  [swap(): return lax.ppermute(x, axis, [(i, i ^ bit) for i in range(count)])]
  transfers between devices with their start and end apart: 13 -> 13, of which waited for: 6 -> 7; matrix products, arithmetic and copies ran while one was open for 0% -> 0% of each run, Pallas kernels for 22% -> 23%
where the time goes in v6:
time: 66.9 us; the launch traced here: 66.7 us
  waiting for transfers between devices  30.4 us (45%)
  Pallas kernels  17.9 us (27%)
  starting transfers between devices  17.5 us (26%)
  between operations  0.81 us (1%)
    ppermute x13, waiting for transfers between devices, swap(): return lax.ppermute(x, axis, [(i, i ^ bit) for i in range(count)])  30.4 us
    ppermute x13, starting transfers between devices, swap(): return lax.ppermute(x, axis, [(i, i ^ bit) for i in range(count)])  17.5 us
    pallas_call x2, Pallas kernels, local(): call(functools.partial(local_backward_body, group, block), [(part, bf16),...  4.88 us
    pallas_call x1, Pallas kernels, local(): call(functools.partial(local_forward_body, heads, block), [(full, f32)],...  2.22 us
    pallas_call x1, Pallas kernels, local(): call(functools.partial(own_memory_body, heads), [(packed, bf16), (full, b...  1.88 us
    pallas_call x1, Pallas kernels, local(): call(functools.partial(load_query_body, heads), [(full, bf16), (full, f32...  1.61 us
    pallas_call x2, Pallas kernels, local(): call(grad_mixed_body, [((rows, width), bf16)], [VM] * (len(masks) + 1))  1.48 us
  transfers between devices with their start and end apart: 13, of which 7 were waited for; matrix products, arithmetic and copies ran while one was open for 0% of the time, Pallas kernels for 23%

profile of v6, /device:TPU:0, one launch (start us, length us, event | category | flops | bytes accessed | tf_op | source)
XLA Modules:
  0.0 66.7 jit_solution(16024980464500657396)
XLA Ops:
  0.6 3.1 %collective-permute-start.1 = (bf16[128,2048]{1,0:T(8,128)(2,1)}, bf16[128,2048]{1,0:T(8,128)(2,1)S(1)}, u32[]{:S(2)}, u32[]{:S(2)}) collective-permute-start(bf16[128,2048]{1,0:T(8,128)(2,1)} %refs_0_.1), channel_id=1, source_target_pairs={{0,2},{1,3},{2,0},{3,1},{4,6},{5,7},{6,4},{7,5},{8,10},{9,11},{10,... | collective-permute-start | bytes 1572872 | tf_op jit(solution)/shard_map/ppermute | solution.py:391
  3.7 12.1 %collective-permute-done.1.refs_0_ = bf16[128,2048]{1,0:T(8,128)(2,1)S(1)} collective-permute-done((bf16[128,2048]{1,0:T(8,128)(2,1)}, bf16[128,2048]{1,0:T(8,128)(2,1)S(1)}, u32[]{:S(2)}, u32[]{:S(2)}) %collective-permute-start.1) | collective-permute-done | bytes 524320 | tf_op jit(solution)/shard_map/ppermute | solution.py:391
  15.8 1.9 %shard_map.94 = (bf16[528,128]{1,0:T(8,128)(2,1)S(1)}, bf16[512,512]{1,0:T(8,128)(2,1)S(1)}, bf16[512,512]{1,0:T(8,128)(2,1)S(1)}) custom-call(bf16[512,512]{1,0:T(8,128)(2,1)} %k_hbm.1, bf16[512,512]{1,0:T(8,128)(2,1)} %v_hbm.1), custom_call_target="tpu_custom_call" | custom-call | flops 268435456 | bytes 1048576 | tf_op jit(solution)/shard_map/pallas_call | solution.py:440
  17.7 1.8 %collective-permute-start.3 = (bf16[528,128]{1,0:T(8,128)(2,1)S(1)}, bf16[528,128]{1,0:T(8,128)(2,1)S(1)}, u32[]{:S(2)}, u32[]{:S(2)}) collective-permute-start(bf16[528,128]{1,0:T(8,128)(2,1)S(1)} %get-tuple-element.44.refs_0_), channel_id=1, source_target_pairs={{0,4},{4,0},{8,12},{12,8},{16,20},{20,16},{24,28},{28,24},{1,5},{5... | collective-permute-start | bytes 405512 | tf_op jit(solution)/shard_map/ppermute | solution.py:391
  19.5 4.3 %collective-permute-done.3.refs_1_.refs_6_.refs_0_ = bf16[528,128]{1,0:T(8,128)(2,1)S(1)} collective-permute-done((bf16[528,128]{1,0:T(8,128)(2,1)S(1)}, bf16[528,128]{1,0:T(8,128)(2,1)S(1)}, u32[]{:S(2)}, u32[]{:S(2)}) %collective-permute-start.3) | collective-permute-done | bytes 135200 | tf_op jit(solution)/shard_map/ppermute | solution.py:391
  23.8 1.9 %collective-permute-start.4 = (bf16[528,128]{1,0:T(8,128)(2,1)S(1)}, bf16[528,128]{1,0:T(8,128)(2,1)S(1)}, u32[]{:S(2)}, u32[]{:S(2)}) collective-permute-start(bf16[528,128]{1,0:T(8,128)(2,1)S(1)} %shard_map.98), channel_id=1, source_target_pairs={{0,8},{4,12},{8,0},{12,4},{16,24},{20,28},{24,16},{28,20},{1,9},{5... | collective-permute-start | bytes 405512 | tf_op jit(solution)/shard_map/ppermute | solution.py:391
  25.7 1.6 %shard_map.93 = (bf16[512,512]{1,0:T(8,128)(2,1)S(1)}, f32[512,512]{1,0:T(8,128)S(1)}, bf16[512,1024]{1,0:T(8,128)(2,1)S(1)}, bf16[1024,512]{1,0:T(8,128)(2,1)S(1)}, f32[8,128]{1,0:T(8,128)S(1)}) custom-call(bf16[512,512]{1,0:T(8,128)(2,1)} %q_hbm.1, f32[4]{0:T(128)} %beta_hbm.1), custom_call_target="tpu_custom_call" | custom-call | flops 65536 | bytes 1048576 | tf_op jit(solution)/shard_map/pallas_call | solution.py:446
  27.3 1.8 %collective-permute-done.4.refs_2_.refs_7_.refs_1_ = bf16[528,128]{1,0:T(8,128)(2,1)S(1)} collective-permute-done((bf16[528,128]{1,0:T(8,128)(2,1)S(1)}, bf16[528,128]{1,0:T(8,128)(2,1)S(1)}, u32[]{:S(2)}, u32[]{:S(2)}) %collective-permute-start.4) | collective-permute-done | bytes 135200 | tf_op jit(solution)/shard_map/ppermute | solution.py:391
  29.1 2.8 %collective-permute-start.5 = (bf16[272,128]{1,0:T(8,128)(2,1)S(1)}, bf16[272,128]{1,0:T(8,128)(2,1)S(1)}, u32[]{:S(2)}, u32[]{:S(2)}) collective-permute-start(bf16[272,128]{1,0:T(8,128)(2,1)S(1)} %get-tuple-element.45), channel_id=1, source_target_pairs={{0,16},{4,20},{8,24},{12,28},{16,0},{20,4},{24,8},{28,12},{1,17},{... | collective-permute-start | bytes 208904 | tf_op jit(solution)/shard_map/ppermute | solution.py:391
  32.0 2.2 %shard_map.95.lo_ref = f32[512,512]{1,0:T(8,128)S(1)} custom-call(bf16[512,512]{1,0:T(8,128)(2,1)S(1)} %get-tuple-element.39.q_ref, bf16[512,512]{1,0:T(8,128)(2,1)S(1)} %get-tuple-element.40.k_ref.refs_0_, bf16[512,512]{1,0:T(8,128)(2,1)S(1)} %get-tuple-element.41.v_ref.refs_1_), custom_call_target="tpu_custom_call" | custom-call | flops 268435456 | bytes 1048576 | tf_op jit(solution)/shard_map/pallas_call | solution.py:472
  36.5 2.9 %collective-permute-done.6.refs_3_ = bf16[256,128]{1,0:T(8,128)(2,1)S(1)} collective-permute-done((bf16[256,128]{1,0:T(8,128)(2,1)S(1)}, bf16[256,128]{1,0:T(8,128)(2,1)S(1)}, u32[]{:S(2)}, u32[]{:S(2)}) %collective-permute-start.6) | collective-permute-done | bytes 65568 | tf_op jit(solution)/shard_map/ppermute | solution.py:391
  39.4 0.9 %shard_map.101 = (f32[528,128]{1,0:T(8,128)S(1)}, bf16[256,2048]{1,0:T(8,128)(2,1)S(1)}) custom-call(f32[512,512]{1,0:T(8,128)S(1)} %get-tuple-element.37.refs_2_.qf_ref, bf16[512,1024]{1,0:T(8,128)(2,1)S(1)} %get-tuple-element.38.refs_3_.qs_ref, f32[512,512]{1,0:T(8,128)S(1)} %shard_map.95.lo_ref, f32[8,128]{1,0:T(8,128)S(1)} %get-tuple-element.42.refs_5_.gate_ref, ...), custom_call_target="tpu_custom_call" | custom-call | flops 268435456 | bytes 1048576 | tf_op jit(solution)/shard_map/pallas_call | solution.py:493
  41.0 2.1 %collective-permute-done.7.recv_ref = bf16[256,2048]{1,0:T(8,128)(2,1)S(1)} collective-permute-done((bf16[256,2048]{1,0:T(8,128)(2,1)S(1)}, bf16[256,2048]{1,0:T(8,128)(2,1)S(1)}, u32[]{:S(2)}, u32[]{:S(2)}) %collective-permute-start.7) | collective-permute-done | bytes 1048608 | tf_op jit(solution)/shard_map/ppermute | solution.py:391
  43.8 1.6 %collective-permute-start.8 = (bf16[128,2048]{1,0:T(8,128)(2,1)S(1)}, bf16[128,2048]{1,0:T(8,128)(2,1)S(1)}, u32[]{:S(2)}, u32[]{:S(2)}) collective-permute-start(bf16[128,2048]{1,0:T(8,128)(2,1)S(1)} %get-tuple-element.54), channel_id=1, source_target_pairs={{0,2},{1,3},{2,0},{3,1},{4,6},{5,7},{6,4},{7,5},{8,10},{9,11},{10,... | collective-permute-start | bytes 1572872 | tf_op jit(solution)/shard_map/ppermute | solution.py:391
  45.4 1.5 %collective-permute-start.9 = (bf16[528,128]{1,0:T(8,128)(2,1)S(1)}, bf16[528,128]{1,0:T(8,128)(2,1)S(1)}, u32[]{:S(2)}, u32[]{:S(2)}) collective-permute-start(bf16[528,128]{1,0:T(8,128)(2,1)S(1)} %get-tuple-element.61.refs_0_), channel_id=1, source_target_pairs={{0,4},{4,0},{8,12},{12,8},{16,20},{20,16},{24,28},{28,24},{1,5},{5... | collective-permute-start | bytes 405512 | tf_op jit(solution)/shard_map/ppermute | solution.py:391
  46.9 3.8 %collective-permute-done.9.refs_1_.refs_4_ = bf16[528,128]{1,0:T(8,128)(2,1)S(1)} collective-permute-done((bf16[528,128]{1,0:T(8,128)(2,1)S(1)}, bf16[528,128]{1,0:T(8,128)(2,1)S(1)}, u32[]{:S(2)}, u32[]{:S(2)}) %collective-permute-start.9) | collective-permute-done | bytes 135200 | tf_op jit(solution)/shard_map/ppermute | solution.py:391
  50.8 1.6 %collective-permute-start.10 = (bf16[528,128]{1,0:T(8,128)(2,1)S(1)}, bf16[528,128]{1,0:T(8,128)(2,1)S(1)}, u32[]{:S(2)}, u32[]{:S(2)}) collective-permute-start(bf16[528,128]{1,0:T(8,128)(2,1)S(1)} %shard_map.107), channel_id=1, source_target_pairs={{0,8},{4,12},{8,0},{12,4},{16,24},{20,28},{24,16},{28,20},{1,9},{5... | collective-permute-start | bytes 405512 | tf_op jit(solution)/shard_map/ppermute | solution.py:391
  52.5 3.4 %collective-permute-done.10.refs_2_.refs_5_ = bf16[528,128]{1,0:T(8,128)(2,1)S(1)} collective-permute-done((bf16[528,128]{1,0:T(8,128)(2,1)S(1)}, bf16[528,128]{1,0:T(8,128)(2,1)S(1)}, u32[]{:S(2)}, u32[]{:S(2)}) %collective-permute-start.10) | collective-permute-done | bytes 135200 | tf_op jit(solution)/shard_map/ppermute | solution.py:391
  56.0 0.8 %collective-permute-start.11 = (bf16[272,128]{1,0:T(8,128)(2,1)S(1)}, bf16[272,128]{1,0:T(8,128)(2,1)S(1)}, u32[]{:S(2)}, u32[]{:S(2)}) collective-permute-start(bf16[272,128]{1,0:T(8,128)(2,1)S(1)} %get-tuple-element.62), channel_id=1, source_target_pairs={{0,16},{4,20},{8,24},{12,28},{16,0},{20,4},{24,8},{28,12},{1,17},{... | collective-permute-start | bytes 208904 | tf_op jit(solution)/shard_map/ppermute | solution.py:391
  56.8 2.2 %collective-permute-start.12 = (bf16[256,128]{1,0:T(8,128)(2,1)S(1)}, bf16[256,128]{1,0:T(8,128)(2,1)S(1)}, u32[]{:S(2)}, u32[]{:S(2)}) collective-permute-start(bf16[256,128]{1,0:T(8,128)(2,1)S(1)} %get-tuple-element.63), channel_id=1, source_target_pairs={{0,16},{4,20},{8,24},{12,28},{16,0},{20,4},{24,8},{28,12},{1,17},{... | collective-permute-start | bytes 196616 | tf_op jit(solution)/shard_map/ppermute | solution.py:391
  58.9 2.4 %shard_map.104 = (bf16[512,256]{1,0:T(8,128)(2,1)S(1)}, f32[512,256]{1,0:T(8,128)S(1)}, f32[512,256]{1,0:T(8,128)S(1)}) custom-call(bf16[512,512]{1,0:T(8,128)(2,1)S(1)} %get-tuple-element.39.q_ref, f32[512,512]{1,0:T(8,128)S(1)} %get-tuple-element.37.refs_2_.qf_ref, bf16[512,1024]{1,0:T(8,128)(2,1)S(1)} %get-tuple-element.38.refs_3_.qs_ref, ...), custom_call_target="tpu_custom_call" | custom-call | flops 268435456 | bytes 1048576 | tf_op jit(solution)/shard_map/pallas_call | solution.py:525
  61.4 2.4 %shard_map.105 = (bf16[512,256]{1,0:T(8,128)(2,1)S(1)}, f32[512,256]{1,0:T(8,128)S(1)}, f32[512,256]{1,0:T(8,128)S(1)}) custom-call(bf16[512,512]{1,0:T(8,128)(2,1)S(1)} %get-tuple-element.39.q_ref, f32[512,512]{1,0:T(8,128)S(1)} %get-tuple-element.37.refs_2_.qf_ref, bf16[512,1024]{1,0:T(8,128)(2,1)S(1)} %get-tuple-element.38.refs_3_.qs_ref, ...), custom_call_target="tpu_custom_call" | custom-call | flops 268435456 | bytes 1048576 | tf_op jit(solution)/shard_map/pallas_call | solution.py:525
  64.4 1.3 %shard_map.110 = (bf16[512,512]{1,0:T(8,128)(2,1)}, bf16[512,512]{1,0:T(8,128)(2,1)}) custom-call(bf16[512,512]{1,0:T(8,128)(2,1)S(1)} %get-tuple-element.40.k_ref.refs_0_, bf16[512,512]{1,0:T(8,128)(2,1)S(1)} %get-tuple-element.41.v_ref.refs_1_, f32[512,256]{1,0:T(8,128)S(1)} %get-tuple-element.59.refs_2_, f32[512,256]{1,0:T(8,128)S(1)} %get-tuple-element.60.refs_3_, ...), custom_call_target="tpu_custom_call" | custom-call | flops 268435456 | bytes 1048576 | tf_op jit(solution)/shard_map/pallas_call | solution.py:543
  65.7 1.1 %shard_map.106 = (bf16[128,2048]{1,0:T(8,128)(2,1)}, bf16[512,512]{1,0:T(8,128)(2,1)}) custom-call(f32[128,2048]{1,0:T(8,128)S(1)} %get-tuple-element.53.keep_ref, bf16[128,2048]{1,0:T(8,128)(2,1)S(1)} %collective-permute-done.8.recv_ref, bf16[512,256]{1,0:T(8,128)(2,1)S(1)} %get-tuple-element.55.refs_0_, bf16[512,256]{1,0:T(8,128)(2,1)S(1)} %get-tuple-element.56.refs_1_), custom_call_target="tpu_custom_call" | custom-call | flops 1048576 | bytes 1048576 | tf_op jit(solution)/shard_map/pallas_call | solution.py:530
  (24 shorter events, 4.4 us)
Async XLA Ops:
  0.6 15.2 %collective-permute-start.1 = (bf16[128,2048]{1,0:T(8,128)(2,1)}, bf16[128,2048]{1,0:T(8,128)(2,1)S(1)}, u32[]{:S(2)}, u32[]{:S(2)}) collective-permute-start(bf16[128,2048]{1,0:T(8,128)(2,1)} %refs_0_.1), channel_id=1, source_target_pairs={{0,2},{1,3},{2,0},{3,1},{4,6},{5,7},{6,4},{7,5},{8,10},{9,11},{10,... | collective-permute-start | bytes 1572872 | tf_op jit(solution)/shard_map/ppermute | solution.py:391
  3.7 30.7 %collective-permute-start = (bf16[128,2048]{1,0:T(8,128)(2,1)}, bf16[128,2048]{1,0:T(8,128)(2,1)S(1)}, u32[]{:S(2)}, u32[]{:S(2)}) collective-permute-start(bf16[128,2048]{1,0:T(8,128)(2,1)} %refs_0_.1), channel_id=1, source_target_pairs={{0,1},{1,0},{2,3},{3,2},{4,5},{5,4},{6,7},{7,6},{8,9},{9,8},{10,11... | collective-permute-start | bytes 1572872 | tf_op jit(solution)/shard_map/ppermute | solution.py:391
  15.8 19.3 %collective-permute-start.2 = (bf16[128,2048]{1,0:T(8,128)(2,1)S(1)}, bf16[128,2048]{1,0:T(8,128)(2,1)S(1)}, u32[]{:S(2)}, u32[]{:S(2)}) collective-permute-start(bf16[128,2048]{1,0:T(8,128)(2,1)S(1)} %collective-permute-done.1.refs_0_), channel_id=1, source_target_pairs={{0,1},{1,0},{2,3},{3,2},{4,5},{5,4},{6,7},{7,6},{8,9},{9,8},{10,11... | collective-permute-start | bytes 1572872 | tf_op jit(solution)/shard_map/ppermute | solution.py:391
  17.7 16.7 %copy-start = (bf16[512,2048]{1,0:T(8,128)(2,1)S(1)}, bf16[512,2048]{1,0:T(8,128)(2,1)}, u32[]{:S(2)}) copy-start(bf16[512,2048]{1,0:T(8,128)(2,1)} %w_ref.3) | copy-start | bytes 6291460
  17.7 16.7 %copy-start.1 = (bf16[128,2048]{1,0:T(8,128)(2,1)S(1)}, bf16[128,2048]{1,0:T(8,128)(2,1)}, u32[]{:S(2)}) copy-start(bf16[128,2048]{1,0:T(8,128)(2,1)} %refs_0_.1) | copy-start | bytes 1572868
  17.7 6.1 %collective-permute-start.3 = (bf16[528,128]{1,0:T(8,128)(2,1)S(1)}, bf16[528,128]{1,0:T(8,128)(2,1)S(1)}, u32[]{:S(2)}, u32[]{:S(2)}) collective-permute-start(bf16[528,128]{1,0:T(8,128)(2,1)S(1)} %get-tuple-element.44.refs_0_), channel_id=1, source_target_pairs={{0,4},{4,0},{8,12},{12,8},{16,20},{20,16},{24,28},{28,24},{1,5},{5... | collective-permute-start | bytes 405512 | tf_op jit(solution)/shard_map/ppermute | solution.py:391
  23.8 5.3 %collective-permute-start.4 = (bf16[528,128]{1,0:T(8,128)(2,1)S(1)}, bf16[528,128]{1,0:T(8,128)(2,1)S(1)}, u32[]{:S(2)}, u32[]{:S(2)}) collective-permute-start(bf16[528,128]{1,0:T(8,128)(2,1)S(1)} %shard_map.98), channel_id=1, source_target_pairs={{0,8},{4,12},{8,0},{12,4},{16,24},{20,28},{24,16},{28,20},{1,9},{5... | collective-permute-start | bytes 405512 | tf_op jit(solution)/shard_map/ppermute | solution.py:391
  29.1 6.8 %collective-permute-start.5 = (bf16[272,128]{1,0:T(8,128)(2,1)S(1)}, bf16[272,128]{1,0:T(8,128)(2,1)S(1)}, u32[]{:S(2)}, u32[]{:S(2)}) collective-permute-start(bf16[272,128]{1,0:T(8,128)(2,1)S(1)} %get-tuple-element.45), channel_id=1, source_target_pairs={{0,16},{4,20},{8,24},{12,28},{16,0},{20,4},{24,8},{28,12},{1,17},{... | collective-permute-start | bytes 208904 | tf_op jit(solution)/shard_map/ppermute | solution.py:391
  34.2 5.2 %collective-permute-start.6 = (bf16[256,128]{1,0:T(8,128)(2,1)S(1)}, bf16[256,128]{1,0:T(8,128)(2,1)S(1)}, u32[]{:S(2)}, u32[]{:S(2)}) collective-permute-start(bf16[256,128]{1,0:T(8,128)(2,1)S(1)} %get-tuple-element.47), channel_id=1, source_target_pairs={{0,16},{4,20},{8,24},{12,28},{16,0},{20,4},{24,8},{28,12},{1,17},{... | collective-permute-start | bytes 196616 | tf_op jit(solution)/shard_map/ppermute | solution.py:391
  40.3 2.7 %collective-permute-start.7 = (bf16[256,2048]{1,0:T(8,128)(2,1)S(1)}, bf16[256,2048]{1,0:T(8,128)(2,1)S(1)}, u32[]{:S(2)}, u32[]{:S(2)}) collective-permute-start(bf16[256,2048]{1,0:T(8,128)(2,1)S(1)} %get-tuple-element.49), channel_id=1, source_target_pairs={{0,1},{1,0},{2,3},{3,2},{4,5},{5,4},{6,7},{7,6},{8,9},{9,8},{10,11... | collective-permute-start | bytes 3145736 | tf_op jit(solution)/shard_map/ppermute | solution.py:391
  43.8 21.8 %collective-permute-start.8 = (bf16[128,2048]{1,0:T(8,128)(2,1)S(1)}, bf16[128,2048]{1,0:T(8,128)(2,1)S(1)}, u32[]{:S(2)}, u32[]{:S(2)}) collective-permute-start(bf16[128,2048]{1,0:T(8,128)(2,1)S(1)} %get-tuple-element.54), channel_id=1, source_target_pairs={{0,2},{1,3},{2,0},{3,1},{4,6},{5,7},{6,4},{7,5},{8,10},{9,11},{10,... | collective-permute-start | bytes 1572872 | tf_op jit(solution)/shard_map/ppermute | solution.py:391
  45.4 5.3 %collective-permute-start.9 = (bf16[528,128]{1,0:T(8,128)(2,1)S(1)}, bf16[528,128]{1,0:T(8,128)(2,1)S(1)}, u32[]{:S(2)}, u32[]{:S(2)}) collective-permute-start(bf16[528,128]{1,0:T(8,128)(2,1)S(1)} %get-tuple-element.61.refs_0_), channel_id=1, source_target_pairs={{0,4},{4,0},{8,12},{12,8},{16,20},{20,16},{24,28},{28,24},{1,5},{5... | collective-permute-start | bytes 405512 | tf_op jit(solution)/shard_map/ppermute | solution.py:391
  50.8 5.1 %collective-permute-start.10 = (bf16[528,128]{1,0:T(8,128)(2,1)S(1)}, bf16[528,128]{1,0:T(8,128)(2,1)S(1)}, u32[]{:S(2)}, u32[]{:S(2)}) collective-permute-start(bf16[528,128]{1,0:T(8,128)(2,1)S(1)} %shard_map.107), channel_id=1, source_target_pairs={{0,8},{4,12},{8,0},{12,4},{16,24},{20,28},{24,16},{28,20},{1,9},{5... | collective-permute-start | bytes 405512 | tf_op jit(solution)/shard_map/ppermute | solution.py:391
  56.0 7.9 %collective-permute-start.11 = (bf16[272,128]{1,0:T(8,128)(2,1)S(1)}, bf16[272,128]{1,0:T(8,128)(2,1)S(1)}, u32[]{:S(2)}, u32[]{:S(2)}) collective-permute-start(bf16[272,128]{1,0:T(8,128)(2,1)S(1)} %get-tuple-element.62), channel_id=1, source_target_pairs={{0,16},{4,20},{8,24},{12,28},{16,0},{20,4},{24,8},{28,12},{1,17},{... | collective-permute-start | bytes 208904 | tf_op jit(solution)/shard_map/ppermute | solution.py:391
  56.8 7.6 %collective-permute-start.12 = (bf16[256,128]{1,0:T(8,128)(2,1)S(1)}, bf16[256,128]{1,0:T(8,128)(2,1)S(1)}, u32[]{:S(2)}, u32[]{:S(2)}) collective-permute-start(bf16[256,128]{1,0:T(8,128)(2,1)S(1)} %get-tuple-element.63), channel_id=1, source_target_pairs={{0,16},{4,20},{8,24},{12,28},{16,0},{20,4},{24,8},{28,12},{1,17},{... | collective-permute-start | bytes 196616 | tf_op jit(solution)/shard_map/ppermute | solution.py:391
